TPU v7x, 512 devices: a whole 4x4x16 slice. The times are simulated.
512 devices in a mesh: seq: 128 (over x, z, core), head: 4 (over y).
Axes of the slice: x: 4, y: 4, z: 16, core: 2. Of those that a mesh axis runs over, the one named last changes fastest.
Arguments:
- queries: bfloat16 [16384, 1024], P('seq', 'head'), may hold values from -6 to 6
- keys: bfloat16 [16384, 1024], P('seq', 'head'), may hold values from -6 to 6
- values: bfloat16 [16384, 1024], P('seq', 'head'), may hold values from -3 to 3
- out_grad: bfloat16 [16384, 1024], P('seq', 'head'), may hold values from -3 to 3
- w_query: bfloat16 [1024, 2048], P('head'), may hold values from -0.1875 to 0.1875
- w_key: bfloat16 [1024, 2048], P('head'), may hold values from -0.1875 to 0.1875
- w_value: bfloat16 [1024, 2048], P('head'), may hold values from -0.1875 to 0.1875
Outputs:
- input_grad: bfloat16 [16384, 2048], P('seq', 'head')
All inputs are finite; a program needn't handle non-finite values.
Results may differ from a plain program's by a relative error of at most 0.0064.
Values sent between devices are 32-bit elements; how exact they have to be, the bound alone decides.
No kernel may reach another device: no remote copies, remote signals or barrier semaphores. Data moves between devices by JAX's collectives and lax.ppermute only.
A program may use at most 128 MiB of HBM per device.

v0:
```python
import jax
import jax.numpy as jnp
import numpy as np
from jax import lax
from jax.sharding import PartitionSpec as P

HD = 64


def shifted(value, axis, steps):
    count = lax.axis_size(axis)
    leading, last = (max(0, -steps), min(count, count - steps))
    return lax.ppermute(value, axis, [(source, source + steps) for source in range(leading, last)])


def cut_along(value, dim, devices):
    dims = value.shape
    blocks = value.reshape(*dims[:dim], devices, dims[dim] // devices, *dims[dim + 1 :])
    return jnp.moveaxis(blocks, dim, 0)


def summed_on_arrival(value, axis, dim):
    devices = lax.axis_size(axis)
    blocks = lax.all_to_all(cut_along(value, dim, devices), axis, 0, 0, tiled=True)
    return jnp.sum(blocks, axis=0)


def pair_tables(width):
    first, second = np.triu_indices(width)
    count = first.shape[0]
    select_first = np.zeros((width, count), np.float32)
    select_second = np.zeros((width, count), np.float32)
    select_first[first, np.arange(count)] = 1.0
    select_second[second, np.arange(count)] = 1.0
    scaling = np.where(first == second, 1.0, np.sqrt(2.0)) / width
    return (select_first, select_second, scaling.astype(np.float32))


def expand_features(inputs, pick_first, pick_second, scaling):
    first = jnp.dot(inputs, pick_first, preferred_element_type=jnp.bfloat16)
    second = jnp.dot(inputs, pick_second, preferred_element_type=jnp.bfloat16)
    feats = (first.astype(jnp.float32) * second.astype(jnp.float32) * scaling).astype(jnp.bfloat16)
    return (first, second, feats)


def chain_back(first, second, dphi, back_first, back_second, scaling):
    scaled = dphi * scaling
    left = scaled * second.astype(jnp.float32)
    right = scaled * first.astype(jnp.float32)
    return jnp.dot(left, back_first, preferred_element_type=jnp.float32) + jnp.dot(
        right, back_second, preferred_element_type=jnp.float32
    )


def on_device(queries, keys, values, out_grad, w_query, w_key, w_value):
    count_rows = queries.shape[0]
    head_count = queries.shape[1] // HD
    select_first, select_second, scale_np = pair_tables(HD)
    pick_first = jnp.asarray(select_first, jnp.bfloat16)
    pick_second = jnp.asarray(select_second, jnp.bfloat16)
    back_first = jnp.asarray(select_first.T, jnp.float32)
    back_second = jnp.asarray(select_second.T, jnp.float32)
    scaling = jnp.asarray(scale_np, jnp.float32)
    feat_count = scale_np.shape[0]
    query_heads = queries.reshape(count_rows, head_count, HD)
    key_heads = keys.reshape(count_rows, head_count, HD)
    value_heads = values.reshape(count_rows, head_count, HD)
    grad_heads = out_grad.reshape(count_rows, head_count, HD)
    query_expanded = []
    key_expanded = []
    kv_parts = []
    grad_parts = []
    for number in range(head_count):
        query_set = expand_features(query_heads[:, number], pick_first, pick_second, scaling)
        key_set = expand_features(key_heads[:, number], pick_first, pick_second, scaling)
        query_expanded.append(query_set)
        key_expanded.append(key_set)
        kv_parts.append(
            jnp.einsum(
                "tf,td->fd", key_set[2], value_heads[:, number], preferred_element_type=jnp.float32
            )
        )
        grad_parts.append(
            jnp.einsum(
                "tf,td->fd", query_set[2], grad_heads[:, number], preferred_element_type=jnp.float32
            )
        )
    kv_local = jnp.stack(kv_parts, 1).reshape(feat_count, head_count * HD)
    grad_local = jnp.stack(grad_parts, 1).reshape(feat_count, head_count * HD)
    rounds = (lax.axis_size("seq") - 1).bit_length()
    kv_running = kv_local
    grad_running = grad_local
    for level in range(rounds):
        kv_running = kv_running + shifted(kv_running, "seq", 1 << level)
        grad_running = grad_running + shifted(grad_running, "seq", -(1 << level))
    kv_before = kv_running - kv_local
    grad_after = grad_running - grad_local
    kv_before = kv_before.astype(jnp.bfloat16).reshape(feat_count, head_count, HD)
    grad_after = grad_after.astype(jnp.bfloat16).reshape(feat_count, head_count, HD)
    causal = lax.broadcasted_iota(jnp.int32, (count_rows, count_rows), 0) >= lax.broadcasted_iota(
        jnp.int32, (count_rows, count_rows), 1
    )
    scores = jnp.einsum("thd,shd->hts", query_heads, key_heads, preferred_element_type=jnp.float32)
    products = jnp.einsum(
        "thd,shd->hts", grad_heads, value_heads, preferred_element_type=jnp.float32
    )
    attn = jnp.where(causal, (scores / HD) ** 2, 0.0).astype(jnp.bfloat16)
    pgrad = jnp.where(causal, 2.0 * scores * products / (HD * HD), 0.0).astype(jnp.bfloat16)
    query_local = jnp.einsum("hts,shd->thd", pgrad, key_heads, preferred_element_type=jnp.float32)
    key_local = jnp.einsum("hts,thd->shd", pgrad, query_heads, preferred_element_type=jnp.float32)
    value_local = jnp.einsum("hts,thd->shd", attn, grad_heads, preferred_element_type=jnp.float32)
    query_out = []
    key_out = []
    value_out = []
    for number in range(head_count):
        qfirst, qsecond, query_feat = query_expanded[number]
        kfirst, ksecond, key_feat = key_expanded[number]
        dfq = jnp.einsum(
            "td,fd->tf",
            grad_heads[:, number],
            kv_before[:, number],
            preferred_element_type=jnp.float32,
        )
        dfk = jnp.einsum(
            "td,fd->tf",
            value_heads[:, number],
            grad_after[:, number],
            preferred_element_type=jnp.float32,
        )
        query_out.append(
            query_local[:, number]
            + chain_back(qfirst, qsecond, dfq, back_first, back_second, scaling)
        )
        key_out.append(
            key_local[:, number]
            + chain_back(kfirst, ksecond, dfk, back_first, back_second, scaling)
        )
        value_out.append(
            value_local[:, number]
            + jnp.einsum(
                "tf,fd->td", key_feat, grad_after[:, number], preferred_element_type=jnp.float32
            )
        )
    query_grad = jnp.stack(query_out, 1).astype(jnp.bfloat16).reshape(count_rows, head_count * HD)
    key_grad = jnp.stack(key_out, 1).astype(jnp.bfloat16).reshape(count_rows, head_count * HD)
    value_grad = jnp.stack(value_out, 1).astype(jnp.bfloat16).reshape(count_rows, head_count * HD)
    partial_sum = jnp.dot(query_grad, w_query, preferred_element_type=jnp.float32)
    partial_sum = partial_sum + jnp.dot(key_grad, w_key, preferred_element_type=jnp.float32)
    partial_sum = partial_sum + jnp.dot(value_grad, w_value, preferred_element_type=jnp.float32)
    return summed_on_arrival(partial_sum, "head", 1).astype(jnp.bfloat16)


def solution(mesh):
    placed = (
        P("seq", "head"),
        P("seq", "head"),
        P("seq", "head"),
        P("seq", "head"),
        P("head", None),
        P("head", None),
        P("head", None),
    )
    return jax.shard_map(
        on_device, mesh=mesh, in_specs=placed, out_specs=P("seq", "head"), check_vma=False
    )
```

profile of v0, /device:TPU:1, one launch (start us, length us, event | category | flops | bytes accessed | tf_op | source)
XLA Modules:
  0.0 1016.4 jit_solution(368824423691675058)
XLA Ops:
  10.7 4.4 multiply_convert_fusion.7
  16.9 1.6 pad_maximum_fusion
  18.5 1.9 copy.82
  20.4 4.9 collective-permute-start
  25.4 1.6 copy.77
  26.9 2.4 convolution_convert_fusion.1
  33.3 1.6 copy.79
  34.9 2.2 convolution_bitcast_fusion
  43.2 1.6 pad_maximum_fusion.1
  44.8 3.0 copy.86
  47.7 6.5 collective-permute-start.7
  54.2 2.0 add.108
  57.7 17.9 %collective-permute-done.7 = f32[2080,256]{1,0:T(8,128)S(1)} collective-permute-done((f32[2080,256]{1,0:T(8,128)}, f32[2080,256]{1,0:T(8,128)S(1)}, u32[]{:S(2)}, u32[]{:S(2)}) %collective-permute-start.7) | collective-permute-done | bytes 2129952 | tf_op jit(solution)/shard_map/ppermute | solution.py:13
  77.2 26.0 %collective-permute-done.1 = f32[2080,256]{1,0:T(8,128)S(1)} collective-permute-done((f32[2080,256]{1,0:T(8,128)S(1)}, f32[2080,256]{1,0:T(8,128)S(1)}, u32[]{:S(2)}, u32[]{:S(2)}) %collective-permute-start.1) | collective-permute-done | bytes 2129952 | tf_op jit(solution)/shard_map/ppermute | solution.py:13
  103.5 3.8 collective-permute-start.2
  107.4 17.3 %collective-permute-done.8 = f32[2080,256]{1,0:T(8,128)S(1)} collective-permute-done((f32[2080,256]{1,0:T(8,128)S(1)}, f32[2080,256]{1,0:T(8,128)S(1)}, u32[]{:S(2)}, u32[]{:S(2)}) %collective-permute-start.8) | collective-permute-done | bytes 2129952 | tf_op jit(solution)/shard_map/ppermute | solution.py:13
  126.2 69.1 %collective-permute-done.2 = f32[2080,256]{1,0:T(8,128)S(1)} collective-permute-done((f32[2080,256]{1,0:T(8,128)S(1)}, f32[2080,256]{1,0:T(8,128)S(1)}, u32[]{:S(2)}, u32[]{:S(2)}) %collective-permute-start.2) | collective-permute-done | bytes 2129952 | tf_op jit(solution)/shard_map/ppermute | solution.py:13
  195.6 12.2 %collective-permute-start.3 = (f32[2080,256]{1,0:T(8,128)S(1)}, f32[2080,256]{1,0:T(8,128)S(1)}, u32[]{:S(2)}, u32[]{:S(2)}) collective-permute-start(f32[2080,256]{1,0:T(8,128)S(1)} %add.110), channel_id=1, source_target_pairs={{0,32},{4,36},{8,40},{12,44},{16,48},{20,52},{24,56},{28,60},{32,6... | collective-permute-start | bytes 6389768 | tf_op jit(solution)/shard_map/ppermute | solution.py:13
  207.7 13.3 %collective-permute-done.9 = f32[2080,256]{1,0:T(8,128)S(1)} collective-permute-done((f32[2080,256]{1,0:T(8,128)S(1)}, f32[2080,256]{1,0:T(8,128)S(1)}, u32[]{:S(2)}, u32[]{:S(2)}) %collective-permute-start.9) | collective-permute-done | bytes 2129952 | tf_op jit(solution)/shard_map/ppermute | solution.py:13
  222.7 167.3 %collective-permute-done.3 = f32[2080,256]{1,0:T(8,128)S(1)} collective-permute-done((f32[2080,256]{1,0:T(8,128)S(1)}, f32[2080,256]{1,0:T(8,128)S(1)}, u32[]{:S(2)}, u32[]{:S(2)}) %collective-permute-start.3) | collective-permute-done | bytes 2129952 | tf_op jit(solution)/shard_map/ppermute | solution.py:13
  391.8 180.6 %collective-permute-done.10 = f32[2080,256]{1,0:T(8,128)S(1)} collective-permute-done((f32[2080,256]{1,0:T(8,128)S(1)}, f32[2080,256]{1,0:T(8,128)S(1)}, u32[]{:S(2)}, u32[]{:S(2)}) %collective-permute-start.10) | collective-permute-done | bytes 2129952 | tf_op jit(solution)/shard_map/ppermute | solution.py:13
  574.2 170.7 %collective-permute-start.5 = (f32[2080,256]{1,0:T(8,128)S(1)}, f32[2080,256]{1,0:T(8,128)S(1)}, u32[]{:S(2)}, u32[]{:S(2)}) collective-permute-start(f32[2080,256]{1,0:T(8,128)S(1)} %add.112), channel_id=1, source_target_pairs={{0,128},{4,132},{8,136},{12,140},{16,144},{20,148},{24,152},{28,15... | collective-permute-start | bytes 6389768 | tf_op jit(solution)/shard_map/ppermute | solution.py:13
  744.9 42.6 %collective-permute-done.11 = f32[2080,256]{1,0:T(8,128)S(1)} collective-permute-done((f32[2080,256]{1,0:T(8,128)S(1)}, f32[2080,256]{1,0:T(8,128)S(1)}, u32[]{:S(2)}, u32[]{:S(2)}) %collective-permute-start.11) | collective-permute-done | bytes 2129952 | tf_op jit(solution)/shard_map/ppermute | solution.py:13
  789.8 40.6 %collective-permute-start.6 = (f32[2080,256]{1,0:T(8,128)S(1)}, f32[2080,256]{1,0:T(8,128)S(1)}, u32[]{:S(2)}, u32[]{:S(2)}) collective-permute-start(f32[2080,256]{1,0:T(8,128)S(1)} %add.113), channel_id=1, source_target_pairs={{0,256},{4,260},{8,264},{12,268},{16,272},{20,276},{24,280},{28,28... | collective-permute-start | bytes 6389768 | tf_op jit(solution)/shard_map/ppermute | solution.py:13
  832.6 39.9 %collective-permute-done.12 = f32[2080,256]{1,0:T(8,128)S(1)} collective-permute-done((f32[2080,256]{1,0:T(8,128)S(1)}, f32[2080,256]{1,0:T(8,128)S(1)}, u32[]{:S(2)}, u32[]{:S(2)}) %collective-permute-start.12) | collective-permute-done | bytes 2129952 | tf_op jit(solution)/shard_map/ppermute | solution.py:13
  872.5 1.6 add.128
  877.6 1.6 copy.84
  879.3 1.6 convolution_multiply_fusion.4
  884.4 39.5 %collective-permute-done.13 = f32[2080,256]{1,0:T(8,128)} collective-permute-done((f32[2080,256]{1,0:T(8,128)}, f32[2080,256]{1,0:T(8,128)}, u32[]{:S(2)}, u32[]{:S(2)}) %collective-permute-start.13) | collective-permute-done | bytes 2129952 | tf_op jit(solution)/shard_map/ppermute | solution.py:13
  924.0 3.6 subtract_convert_fusion
  927.6 1.6 copy.88
  956.2 59.4 %all_to_all.5 = f32[4,128,512]{2,1,0:T(8,128)S(1)} all-to-all(f32[4,128,512]{2,1,0:T(8,128)S(1)} %bitcast.276), channel_id=1, replica_groups=mesh['seq'=128,'head'=4] {'head'}, dimensions={0} | all-to-all | bytes 2097152 | tf_op jit(solution)/shard_map/all_to_all | solution.py:24
  (201 shorter events, 71.8 us)
Async XLA Ops:
  0.0 952.1 %copy-start = (bf16[256,2048]{1,0:T(8,128)(2,1)S(1)}, bf16[256,2048]{1,0:T(8,128)(2,1)}, u32[]{:S(2)}) copy-start(bf16[256,2048]{1,0:T(8,128)(2,1)} %param.16) | copy-start | bytes 3145732
  0.0 2.4 copy-start.6
  1.1 2.7 copy-start.5
  2.4 8.2 copy-start.9
  7.8 2.8 copy-start.56
  10.7 5.9 copy-start.49
  20.4 33.8 %collective-permute-start = (f32[2080,256]{1,0:T(8,128)S(1)}, f32[2080,256]{1,0:T(8,128)}, u32[]{:S(2)}, u32[]{:S(2)}) collective-permute-start(f32[2080,256]{1,0:T(8,128)S(1)} %copy.82), channel_id=1, source_target_pairs={{0,4},{4,8},{8,12},{12,16},{16,20},{20,24},{24,28},{28,32},{32,36}... | collective-permute-start | bytes 6389768 | tf_op jit(solution)/shard_map/ppermute | solution.py:13
  26.9 2.4 copy-start.46
  26.9 3.7 copy-start.7
  34.9 2.2 copy-start.23
  34.9 2.2 copy-start.29
  34.9 2.2 copy-start.44
  38.4 1.9 copy-start.25
  47.7 27.9 %collective-permute-start.7 = (f32[2080,256]{1,0:T(8,128)}, f32[2080,256]{1,0:T(8,128)S(1)}, u32[]{:S(2)}, u32[]{:S(2)}) collective-permute-start(f32[2080,256]{1,0:T(8,128)} %copy.86), channel_id=1, source_target_pairs={{4,0},{8,4},{12,8},{16,12},{20,16},{24,20},{28,24},{32,28},{36,32}... | collective-permute-start | bytes 6389768 | tf_op jit(solution)/shard_map/ppermute | solution.py:13
  54.2 21.4 %copy-start.3 = (f32[2080,256]{1,0:T(8,128)S(1)}, f32[2080,256]{1,0:T(8,128)}, u32[]{:S(2)}) copy-start(f32[2080,256]{1,0:T(8,128)} %copy.86) | copy-start | bytes 6389764
  56.3 47.0 %collective-permute-start.1 = (f32[2080,256]{1,0:T(8,128)S(1)}, f32[2080,256]{1,0:T(8,128)S(1)}, u32[]{:S(2)}, u32[]{:S(2)}) collective-permute-start(f32[2080,256]{1,0:T(8,128)S(1)} %add.108), channel_id=1, source_target_pairs={{0,8},{4,12},{8,16},{12,20},{16,24},{20,28},{24,32},{28,36},{32,40... | collective-permute-start | bytes 6389768 | tf_op jit(solution)/shard_map/ppermute | solution.py:13
  75.9 48.7 %collective-permute-start.8 = (f32[2080,256]{1,0:T(8,128)S(1)}, f32[2080,256]{1,0:T(8,128)S(1)}, u32[]{:S(2)}, u32[]{:S(2)}) collective-permute-start(f32[2080,256]{1,0:T(8,128)S(1)} %add.123), channel_id=1, source_target_pairs={{8,0},{12,4},{16,8},{20,12},{24,16},{28,20},{32,24},{36,28},{40,32... | collective-permute-start | bytes 6389768 | tf_op jit(solution)/shard_map/ppermute | solution.py:13
  103.5 91.8 %collective-permute-start.2 = (f32[2080,256]{1,0:T(8,128)S(1)}, f32[2080,256]{1,0:T(8,128)S(1)}, u32[]{:S(2)}, u32[]{:S(2)}) collective-permute-start(f32[2080,256]{1,0:T(8,128)S(1)} %add.109), channel_id=1, source_target_pairs={{0,16},{4,20},{8,24},{12,28},{16,32},{20,36},{24,40},{28,44},{32,4... | collective-permute-start | bytes 6389768 | tf_op jit(solution)/shard_map/ppermute | solution.py:13
  124.9 96.0 %collective-permute-start.9 = (f32[2080,256]{1,0:T(8,128)S(1)}, f32[2080,256]{1,0:T(8,128)S(1)}, u32[]{:S(2)}, u32[]{:S(2)}) collective-permute-start(f32[2080,256]{1,0:T(8,128)S(1)} %add.124), channel_id=1, source_target_pairs={{16,0},{20,4},{24,8},{28,12},{32,16},{36,20},{40,24},{44,28},{48,3... | collective-permute-start | bytes 6389768 | tf_op jit(solution)/shard_map/ppermute | solution.py:13
  195.6 194.5 %collective-permute-start.3 = (f32[2080,256]{1,0:T(8,128)S(1)}, f32[2080,256]{1,0:T(8,128)S(1)}, u32[]{:S(2)}, u32[]{:S(2)}) collective-permute-start(f32[2080,256]{1,0:T(8,128)S(1)} %add.110), channel_id=1, source_target_pairs={{0,32},{4,36},{8,40},{12,44},{16,48},{20,52},{24,56},{28,60},{32,6... | collective-permute-start | bytes 6389768 | tf_op jit(solution)/shard_map/ppermute | solution.py:13
  221.3 351.1 %collective-permute-start.10 = (f32[2080,256]{1,0:T(8,128)S(1)}, f32[2080,256]{1,0:T(8,128)S(1)}, u32[]{:S(2)}, u32[]{:S(2)}) collective-permute-start(f32[2080,256]{1,0:T(8,128)S(1)} %add.125), channel_id=1, source_target_pairs={{32,0},{36,4},{40,8},{44,12},{48,16},{52,20},{56,24},{60,28},{64,3... | collective-permute-start | bytes 6389768 | tf_op jit(solution)/shard_map/ppermute | solution.py:13
  390.4 183.6 %collective-permute-start.4 = (f32[2080,256]{1,0:T(8,128)S(1)}, f32[2080,256]{1,0:T(8,128)S(1)}, u32[]{:S(2)}, u32[]{:S(2)}) collective-permute-start(f32[2080,256]{1,0:T(8,128)S(1)} %add.111), channel_id=1, source_target_pairs={{0,64},{4,68},{8,72},{12,76},{16,80},{20,84},{24,88},{28,92},{32,9... | collective-permute-start | bytes 6389768 | tf_op jit(solution)/shard_map/ppermute | solution.py:13
  572.6 214.8 %collective-permute-start.11 = (f32[2080,256]{1,0:T(8,128)S(1)}, f32[2080,256]{1,0:T(8,128)S(1)}, u32[]{:S(2)}, u32[]{:S(2)}) collective-permute-start(f32[2080,256]{1,0:T(8,128)S(1)} %add.126), channel_id=1, source_target_pairs={{64,0},{68,4},{72,8},{76,12},{80,16},{84,20},{88,24},{92,28},{96,3... | collective-permute-start | bytes 6389768 | tf_op jit(solution)/shard_map/ppermute | solution.py:13
  574.2 215.3 %collective-permute-start.5 = (f32[2080,256]{1,0:T(8,128)S(1)}, f32[2080,256]{1,0:T(8,128)S(1)}, u32[]{:S(2)}, u32[]{:S(2)}) collective-permute-start(f32[2080,256]{1,0:T(8,128)S(1)} %add.112), channel_id=1, source_target_pairs={{0,128},{4,132},{8,136},{12,140},{16,144},{20,148},{24,152},{28,15... | collective-permute-start | bytes 6389768 | tf_op jit(solution)/shard_map/ppermute | solution.py:13
  787.8 42.7 %copy-start.48 = (bf16[128,256]{0,1:T(8,128)(2,1)S(1)}, bf16[128,256]{0,1:T(8,128)(2,1)}, u32[]{:S(2)}) copy-start(bf16[128,256]{0,1:T(8,128)(2,1)} %copy.77) | copy-start | bytes 196612
  787.8 42.9 %copy-start.45 = (bf16[128,256]{0,1:T(8,128)(2,1)S(1)}, bf16[128,256]{0,1:T(8,128)(2,1)}, u32[]{:S(2)}) copy-start(bf16[128,256]{0,1:T(8,128)(2,1)} %copy.79) | copy-start | bytes 196612
  787.8 42.9 %copy-start.50 = (bf16[128,256]{0,1:T(8,128)(2,1)S(1)}, bf16[128,256]{0,1:T(8,128)(2,1)}, u32[]{:S(2)}) copy-start(bf16[128,256]{0,1:T(8,128)(2,1)} %copy-done.49) | copy-start | bytes 196612
  787.8 84.7 %collective-permute-start.12 = (f32[2080,256]{1,0:T(8,128)S(1)}, f32[2080,256]{1,0:T(8,128)S(1)}, u32[]{:S(2)}, u32[]{:S(2)}) collective-permute-start(f32[2080,256]{1,0:T(8,128)S(1)} %add.127), channel_id=1, source_target_pairs={{128,0},{132,4},{136,8},{140,12},{144,16},{148,20},{152,24},{156,2... | collective-permute-start | bytes 6389768 | tf_op jit(solution)/shard_map/ppermute | solution.py:13
  789.8 86.3 %collective-permute-start.6 = (f32[2080,256]{1,0:T(8,128)S(1)}, f32[2080,256]{1,0:T(8,128)S(1)}, u32[]{:S(2)}, u32[]{:S(2)}) collective-permute-start(f32[2080,256]{1,0:T(8,128)S(1)} %add.113), channel_id=1, source_target_pairs={{0,256},{4,260},{8,264},{12,268},{16,272},{20,276},{24,280},{28,28... | collective-permute-start | bytes 6389768 | tf_op jit(solution)/shard_map/ppermute | solution.py:13
  874.1 49.9 %collective-permute-start.13 = (f32[2080,256]{1,0:T(8,128)}, f32[2080,256]{1,0:T(8,128)}, u32[]{:S(2)}, u32[]{:S(2)}) collective-permute-start(f32[2080,256]{1,0:T(8,128)} %add.128), channel_id=1, source_target_pairs={{256,0},{260,4},{264,8},{268,12},{272,16},{276,20},{280,24},{284,2... | collective-permute-start | bytes 6389768 | tf_op jit(solution)/shard_map/ppermute | solution.py:13
  882.4 41.6 %copy-start.4 = (f32[2080,256]{1,0:T(8,128)S(1)}, f32[2080,256]{1,0:T(8,128)}, u32[]{:S(2)}) copy-start(f32[2080,256]{1,0:T(8,128)} %copy.86) | copy-start | bytes 6389764
  931.3 1.8 copy-start.33
  (39 other events, 46.9 us)
where the time goes:
time: 1030 us; the launch traced here: 1020 us
  waiting for transfers between devices  614 us (60%)
  starting transfers between devices  250 us (24%)
  blocking collectives  59.4 us (6%)
  matrix products  44.2 us (4%)
  local copies, waits for them, and re-layouts  33.1 us (3%)
  other arithmetic  15.5 us (2%)
    ppermute x14, waiting for transfers between devices, shifted(): lax.ppermute(value, axis, [(source, source + steps) for source in range(l...  614 us
    ppermute x14, starting transfers between devices, shifted(): lax.ppermute(value, axis, [(source, source + steps) for source in range(l...  250 us
    all_to_all x1, blocking collectives, summed_on_arrival(): lax.all_to_all(cut_along(value, dim, devices), axis, 0, 0, tiled=True)  59.4 us
    unnamed x118, local copies, waits for them, and re-layouts  24.9 us
  transfers between devices with their start and end apart: 14, of which 11 were waited for; matrix products, arithmetic and copies ran while one was open for 4% of the time, Pallas kernels for 0%

commit v1 on v0

v1 whole, which is shorter than its diff:
```python
import functools

import jax
import jax.numpy as jnp
from jax import lax
from jax.experimental import pallas as pl
from jax.experimental.pallas import tpu as pltpu
from jax.sharding import Mesh
from jax.sharding import PartitionSpec as P

HD = 64
TB = 128
CHIPS = 4
BLOCKS = 8
GRAIN = 8
SIZES = [HD - GRAIN * (j // GRAIN) for j in range(HD)]
STARTS = [sum(SIZES[:j]) for j in range(HD)]
PAIRS = sum(SIZES)
HALF = PAIRS // 2
SPLIT_J = STARTS.index(HALF)
VMEM = pl.BlockSpec(memory_space=pltpu.VMEM)
F32 = jnp.float32
BF16 = jnp.bfloat16


def call(body, out_shape, args, name, scratch=(), flops=0, nbytes=0):
    return pl.pallas_call(
        body,
        out_shape=out_shape,
        in_specs=[VMEM] * len(args),
        out_specs=jax.tree.map(lambda unused: VMEM, out_shape),
        scratch_shapes=list(scratch),
        name=name,
        compiler_params=pltpu.CompilerParams(vmem_limit_bytes=24 << 20),
        cost_estimate=pl.CostEstimate(flops=flops, bytes_accessed=nbytes, transcendentals=0),
    )(*args)


def dot(a, b):
    return jnp.dot(a, b, preferred_element_type=F32)


def pack_body(q_ref, k_ref, v_ref, g_ref, out_ref):
    for head in range(CHIPS):
        cols = slice(head * HD, (head + 1) * HD)
        out_ref[head, 0] = jnp.concatenate([q_ref[:, cols], g_ref[:, cols]], axis=1).astype(F32)
        out_ref[head, 1] = jnp.concatenate([k_ref[:, cols], v_ref[:, cols]], axis=1).astype(F32)


def write_features(xt, factor, feats_ref):
    for block in range(HD // GRAIN):
        low = GRAIN * block
        base = xt[low:]
        if factor != 1.0 and low + GRAIN < HD:
            base = jnp.concatenate([xt[low : low + GRAIN], xt[low + GRAIN :] * factor], axis=0)
        for j in range(low, low + GRAIN, 2):
            pair = [base * xt[j : j + 1], base * xt[j + 1 : j + 2]]
            start = STARTS[j]
            feats_ref[start : start + 2 * SIZES[j], :] = jnp.concatenate(pair, axis=0).astype(BF16)


def state_body(own_ref, other_ref, state_ref, tok_ref, src_ref, out_ref, feats_ref):
    core = lax.axis_index("core")
    for chip in range(CHIPS):
        for ref, parity in ((own_ref, core), (other_ref, 1 - core)):
            source = ref[chip, 1 - core]
            tok_ref[2 * chip + parity] = source.astype(BF16)
            src_ref[2 * chip + parity] = source.T.astype(BF16)
            out_ref[2 * chip + parity] = ref[chip, core].T.astype(BF16)
    state_ref[...] = jnp.zeros_like(state_ref)

    def step(tile, carry):
        xt = jnp.concatenate([src_ref[2 * tile, :HD], src_ref[2 * tile + 1, :HD]], axis=1)
        write_features(xt.astype(F32), 1.0, feats_ref)
        tok = jnp.concatenate([tok_ref[2 * tile], tok_ref[2 * tile + 1]], axis=0)
        values = tok[:, HD:]
        zeros = jnp.zeros_like(values)
        state_ref[...] += dot(
            feats_ref[:HALF, :], jnp.concatenate([values, zeros], axis=1)
        ) + dot(feats_ref[HALF:, :], jnp.concatenate([zeros, values], axis=1))
        return carry

    lax.fori_loop(0, BLOCKS // 2, step, 0)


def local_body(tok_ref, src_ref, out_ref, local_ref):
    core = lax.axis_index("core")
    tiles = BLOCKS // 2
    width = 2 * TB
    sign = 1 - 2 * core
    local_ref[...] = jnp.zeros_like(local_ref)
    ahead = lax.broadcasted_iota(jnp.int32, (width, width), 0) - lax.broadcasted_iota(
        jnp.int32, (width, width), 1
    )

    def outer(tile, carry):
        target = jnp.concatenate([out_ref[2 * tile], out_ref[2 * tile + 1]], axis=1)
        zeros = jnp.zeros((HD, width), BF16)
        score_rhs = jnp.concatenate([target[:HD], zeros], axis=0)
        value_rhs = jnp.concatenate([zeros, target[HD:]], axis=0)

        def inner(source, carry):
            tok = jnp.concatenate([tok_ref[2 * source], tok_ref[2 * source + 1]], axis=0)
            scores = dot(tok, score_rhs)
            products = dot(tok, value_rhs)
            keep = (ahead + (source - tile) * width) * sign <= 0
            scaled = jnp.where(keep, scores, 0.0) * (1.0 / HD)
            attn = (scaled * scaled).astype(BF16)
            pgrad = (scaled * products * (2.0 / HD)).astype(BF16)
            left = jnp.concatenate([src_ref[2 * source], src_ref[2 * source + 1]], axis=1)
            local_ref[tile, :HD] += dot(left[:HD], pgrad)
            local_ref[tile, HD:] += dot(left[HD:], attn)
            return carry

        first = jnp.where(core == 0, 0, tile)
        last = jnp.where(core == 0, tile + 1, tiles)
        lax.fori_loop(first, last, inner, 0)
        return carry

    lax.fori_loop(0, tiles, outer, 0)


def scan_body(parts_ref, sums_ref):
    core = lax.axis_index("core")
    count = parts_ref.shape[0]

    def step(number, total):
        place = number + core * (count - 1 - 2 * number)
        sums_ref[place] = total
        return total + parts_ref[place]

    lax.fori_loop(0, count, step, jnp.zeros(parts_ref.shape[1:], F32))


def grads_body(state_ref, out_ref, local_ref, grads_ref, rows_ref, cols_ref, wide_ref, feats_ref):
    rows_ref[...] = state_ref[...].astype(BF16)
    for tile in range(HALF // TB):
        part = slice(tile * TB, (tile + 1) * TB)
        cols_ref[:, part] = state_ref[part, :].T.astype(BF16)

    def step(tile, carry):
        target = jnp.concatenate([out_ref[2 * tile], out_ref[2 * tile + 1]], axis=1)
        xt = target[:HD].astype(F32)
        zeros = jnp.zeros((HD, 2 * TB), BF16)
        wide_ref[:HALF] = dot(rows_ref[...], jnp.concatenate([target[HD:], zeros], axis=0))
        wide_ref[HALF:] = dot(rows_ref[...], jnp.concatenate([zeros, target[HD:]], axis=0))
        write_features(xt, 2.0, feats_ref)
        values = dot(cols_ref[:HD, :], feats_ref[:HALF]) + dot(cols_ref[HD:, :], feats_ref[HALF:])
        count = HD // GRAIN
        grains = [xt[GRAIN * block : GRAIN * (block + 1)] for block in range(count)]
        sums = [jnp.zeros((GRAIN, 2 * TB), F32) for unused in range(count)]
        for block in range(count):
            rows = []
            for j in range(GRAIN * block, GRAIN * (block + 1)):
                row = xt[j : j + 1]
                across = None
                for other in range(block, count):
                    start = STARTS[j] + GRAIN * (other - block)
                    wide = wide_ref[start : start + GRAIN]
                    sums[other] = sums[other] + row * wide
                    if other > block:
                        term = grains[other] * wide
                        across = term if across is None else across + term
                if across is not None:
                    rows.append(jnp.sum(across, axis=0, keepdims=True))
            if rows:
                sums[block] = sums[block] + jnp.concatenate(rows, axis=0)
        result = local_ref[tile] + jnp.concatenate(
            [
                jnp.concatenate(sums, axis=0) * (2.0 / (HD * HD)),
                values * (1.0 / (HD * HD)),
            ],
            axis=0,
        )
        grads_ref[2 * tile] = result[:, :TB].T
        grads_ref[2 * tile + 1] = result[:, TB:].T
        return carry

    lax.fori_loop(0, BLOCKS // 2, step, 0)


def project_body(grads_ref, wq_ref, wk_ref, wv_ref, out_ref):
    query = jnp.concatenate([grads_ref[2 * h][:, :HD] for h in range(CHIPS)], axis=1)
    key = jnp.concatenate([grads_ref[2 * h + 1][:, :HD] for h in range(CHIPS)], axis=1)
    value = jnp.concatenate([grads_ref[2 * h + 1][:, HD:] for h in range(CHIPS)], axis=1)
    query, key, value = query.astype(BF16), key.astype(BF16), value.astype(BF16)
    width = out_ref.shape[2]
    for place in range(out_ref.shape[0]):
        cols = slice(place * width, (place + 1) * width)
        out_ref[place] = (
            dot(query, wq_ref[:, cols]) + dot(key, wk_ref[:, cols]) + dot(value, wv_ref[:, cols])
        )


def on_device(queries, keys, values, out_grad, w_query, w_key, w_value):
    shape = jax.ShapeDtypeStruct
    groups = lax.axis_size("x") * lax.axis_size("zg")
    packed = call(
        pack_body,
        shape((CHIPS, 2, TB, TB), F32),
        (queries, keys, values, out_grad),
        "pack",
        flops=1 << 20,
        nbytes=1 << 20,
    )
    own = lax.all_to_all(packed, "zc", 0, 0, tiled=True)
    other = lax.ppermute(own, "core", [(0, 1), (1, 0)])
    blocks = shape((BLOCKS, TB, TB), BF16)
    state, tok, src, out = call(
        state_body,
        (shape((HALF, TB), F32), blocks, blocks, blocks),
        (own, other),
        "state",
        scratch=[pltpu.VMEM((PAIRS, 2 * TB), BF16)],
        flops=4 << 30,
        nbytes=3 << 20,
    )
    shards = lax.all_to_all(
        state.reshape(groups, HALF // groups, TB), ("x", "zg"), 0, 0, tiled=True
    )
    local = call(
        local_body,
        shape((BLOCKS // 2, TB, 2 * TB), F32),
        (tok, src, out),
        "local",
        flops=4 << 30,
        nbytes=1 << 20,
    )
    sums = call(
        scan_body, shape(shards.shape, F32), (shards,), "scan", flops=1 << 20, nbytes=1 << 20
    )
    before = lax.all_to_all(sums, ("x", "zg"), 0, 0, tiled=True).reshape(HALF, TB)
    grads = call(
        grads_body,
        shape((BLOCKS, TB, TB), F32),
        (before, out, local),
        "grads",
        scratch=[
            pltpu.VMEM((HALF, TB), BF16),
            pltpu.VMEM((TB, HALF), BF16),
            pltpu.VMEM((PAIRS, 2 * TB), F32),
            pltpu.VMEM((PAIRS, 2 * TB), BF16),
        ],
        flops=4 << 30,
        nbytes=3 << 20,
    )
    mine = lax.all_to_all(grads, ("zc", "core"), 0, 0, tiled=True)
    heads = lax.axis_size("y")
    partial_sum = call(
        project_body,
        shape((heads, TB, w_query.shape[1] // heads), F32),
        (mine, w_query, w_key, w_value),
        "project",
        flops=1 << 29,
        nbytes=4 << 20,
    )
    pieces = lax.all_to_all(partial_sum, "y", 0, 0, tiled=True)
    return jnp.sum(pieces, axis=0).astype(BF16)


def solution(mesh):
    seq, head = mesh.devices.shape
    cols = 4 if seq >= 128 else 2
    grid = Mesh(
        mesh.devices.reshape(seq // (cols * 8), cols, CHIPS, 2, head),
        ("x", "zg", "zc", "core", "y"),
    )
    tokens = ("x", "zg", "zc", "core")
    placed = (P(tokens, "y"),) * 4 + (P("y", None),) * 3
    return jax.shard_map(
        on_device, mesh=grid, in_specs=placed, out_specs=P(tokens, "y"), check_vma=False
    )
```

time: 1030 us -> 164 us (0.16); the launches traced: 1020 us -> 163 us
  waiting for transfers between devices: 614 us -> 25 us
  starting transfers between devices: 250 us -> 10.9 us
  blocking collectives: 59.4 us -> 112 us
  matrix products: 44.2 us -> 0 us
  local copies, waits for them, and re-layouts: 33.1 us -> 3.37 us
  other arithmetic: 15.5 us -> 0.76 us
  Pallas kernels: 0 us -> 11 us
    ppermute x14 -> x1, waiting for transfers between devices: 614 us -> 1.51 us  [on_device(): other = lax.ppermute(own, 'core', [(0, 1), (1, 0)])]
    ppermute x14 -> x1, starting transfers between devices: 250 us -> 4 us  [on_device(): other = lax.ppermute(own, 'core', [(0, 1), (1, 0)])]
    all_to_all x1 -> x4, blocking collectives: 59.4 us -> 112 us  [the longest x1 47.3 us: on_device(): lax.all_to_all(state.reshape(groups, HALF // groups, TB), ('x', 'zg'), 0,...]
    dot_general x60 -> x0, matrix products: 44.2 us -> none  [the longest x8 11.7 us: expand_features(): first = jnp.dot(inputs, pick_first, preferred_element_type=jnp.bfloat16)]
    all_to_all x0 -> x1, waiting for transfers between devices: none -> 23.4 us  [on_device(): lax.all_to_all(sums, ('x', 'zg'), 0, 0, tiled=True).reshape(HALF, TB)]
    unnamed x118 -> x14, local copies, waits for them, and re-layouts: 24.9 us -> 3.37 us
    pallas_call x0 -> x6, Pallas kernels: none -> 11 us  [call(): pl.pallas_call(body, out_shape=out_shape, in_specs=[VMEM] * len(args), ou...]
  transfers between devices with their start and end apart: 14 -> 2, of which waited for: 11 -> 2; matrix products, arithmetic and copies ran while one was open for 4% -> 0% of each run, Pallas kernels for 0% -> 2%
where the time goes in v1:
time: 164 us; the launch traced here: 163 us
  blocking collectives  112 us (68%)
  waiting for transfers between devices  25 us (15%)
  Pallas kernels  11 us (7%)
  starting transfers between devices  10.9 us (7%)
  local copies, waits for them, and re-layouts  3.37 us (2%)
    all_to_all x1, blocking collectives, on_device(): lax.all_to_all(state.reshape(groups, HALF // groups, TB), ('x', 'zg'), 0,...  47.3 us
    all_to_all x1, blocking collectives, on_device(): mine = lax.all_to_all(grads, ('zc', 'core'), 0, 0, tiled=True)  27.9 us
    all_to_all x1, waiting for transfers between devices, on_device(): lax.all_to_all(sums, ('x', 'zg'), 0, 0, tiled=True).reshape(HALF, TB)  23.4 us
    all_to_all x1, blocking collectives, on_device(): own = lax.all_to_all(packed, 'zc', 0, 0, tiled=True)  19.6 us
    all_to_all x1, blocking collectives, on_device(): pieces = lax.all_to_all(partial_sum, 'y', 0, 0, tiled=True)  17.7 us
    pallas_call x6, Pallas kernels, call(): pl.pallas_call(body, out_shape=out_shape, in_specs=[VMEM] * len(args), ou...  11 us
    all_to_all x1, starting transfers between devices, on_device(): lax.all_to_all(sums, ('x', 'zg'), 0, 0, tiled=True).reshape(HALF, TB)  6.89 us
    ppermute x1, starting transfers between devices, on_device(): other = lax.ppermute(own, 'core', [(0, 1), (1, 0)])  4 us
  transfers between devices with their start and end apart: 2, of which 2 were waited for; matrix products, arithmetic and copies ran while one was open for 0% of the time, Pallas kernels for 2%

profile of v1, /device:TPU:1, one launch (start us, length us, event | category | flops | bytes accessed | tf_op | source)
XLA Modules:
  0.0 163.5 jit_solution(4427190554184176709)
XLA Ops:
  0.0 0.0 copy-start.3
  0.0 0.8 copy-done.3
  0.8 0.0 copy-start.4
  0.8 0.8 copy-done.4
  1.7 0.0 copy-start.5
  1.7 0.8 copy-done.5
  2.5 0.0 copy-start.6
  2.5 0.8 copy-done.6
  3.4 0.1 pack.1
  3.5 19.6 %all_to_all.25.own_ref = f32[4,2,128,128]{3,2,1,0:T(8,128)S(1)} all-to-all(f32[4,2,128,128]{3,2,1,0:T(8,128)S(1)} %pack.1), channel_id=1, replica_groups=mesh['x'=4,'zg'=4,'zc'=4,'core'=2,'y'=4] {'zc'}, dimensions={0} | all-to-all | bytes 1048576 | tf_op jit(solution)/shard_map/all_to_all | solution.py:206
  23.1 4.0 %collective-permute-start = (f32[4,2,128,128]{3,2,1,0:T(8,128)S(1)}, f32[4,2,128,128]{3,2,1,0:T(8,128)S(1)}, u32[]{:S(2)}, u32[]{:S(2)}) collective-permute-start(f32[4,2,128,128]{3,2,1,0:T(8,128)S(1)} %all_to_all.25.own_ref), channel_id=1, source_target_pairs={{0,4},{4,0},{1,5},{5,1},{2,6},{6,2},{3,7},{7,3},{8,12},{12,8},{9,1... | collective-permute-start | bytes 1572872 | tf_op jit(solution)/shard_map/ppermute | solution.py:207
  27.1 1.5 collective-permute-done.other_ref
  28.6 2.3 %state.1 = (f32[1152,128]{1,0:T(8,128)S(1)}, bf16[8,128,128]{2,1,0:T(8,128)(2,1)S(1)}, bf16[8,128,128]{2,1,0:T(8,128)(2,1)S(1)}, bf16[8,128,128]{2,1,0:T(8,128)(2,1)S(1)}) custom-call(f32[4,2,128,128]{3,2,1,0:T(8,128)S(1)} %all_to_all.25.own_ref, f32[4,2,128,128]{3,2,1,0:T(8,128)S(1)} %collective-permute-done.other_ref), custom_call_target="tpu_custom_call" | custom-call | flops 4294967296 | bytes 3145728 | tf_op jit(solution)/shard_map/state/pallas_call | solution.py:27
  30.9 47.3 %all_to_all.26.parts_ref = f32[16,72,128]{2,1,0:T(8,128)S(1)} all-to-all(f32[16,72,128]{2,1,0:T(8,128)S(1)} %bitcast.3), channel_id=1, replica_groups=mesh['x'=4,'zg'=4,'zc'=4,'core'=2,'y'=4] {'x','zg'}, dimensions={0} | all-to-all | bytes 1179648 | tf_op jit(solution)/shard_map/all_to_all | solution.py:218
  78.2 0.9 scan.1
  79.1 6.9 %all-to-all-start.2 = ((f32[16,72,128]{2,1,0:T(8,128)}), f32[16,72,128]{2,1,0:T(8,128)S(1)}, u32[]{:S(2)}, u32[]{:S(2)}) async-start(f32[16,72,128]{2,1,0:T(8,128)} %scan.1), calls=%async_computation.2 | async-start | bytes 1179648 | tf_op jit(solution)/shard_map/all_to_all | solution.py:232
  86.0 3.6 %local.1.local_ref = f32[4,128,256]{2,1,0:T(8,128)S(1)} custom-call(bf16[8,128,128]{2,1,0:T(8,128)(2,1)S(1)} %get-tuple-element.11.tok_ref, bf16[8,128,128]{2,1,0:T(8,128)(2,1)S(1)} %get-tuple-element.12.src_ref, bf16[8,128,128]{2,1,0:T(8,128)(2,1)S(1)} %get-tuple-element.10.out_ref), custom_call_target="tpu_custom_call" | custom-call | flops 4294967296 | bytes 1048576 | tf_op jit(solution)/shard_map/local/pallas_call | solution.py:27
  89.6 23.4 %all-to-all-done.2 = f32[16,72,128]{2,1,0:T(8,128)S(1)} async-done(((f32[16,72,128]{2,1,0:T(8,128)}), f32[16,72,128]{2,1,0:T(8,128)S(1)}, u32[]{:S(2)}, u32[]{:S(2)}) %all-to-all-start.2) | async-done | bytes 589856 | tf_op jit(solution)/shard_map/all_to_all | solution.py:232
  113.1 0.0 copy-start.1
  113.1 0.0 copy-start.2
  113.1 3.4 %grads.1 = f32[8,128,128]{2,1,0:T(8,128)S(1)} custom-call(f32[1152,128]{1,0:T(8,128)S(1)} %bitcast.2, bf16[8,128,128]{2,1,0:T(8,128)(2,1)S(1)} %get-tuple-element.10.out_ref, f32[4,128,256]{2,1,0:T(8,128)S(1)} %local.1.local_ref), custom_call_target="tpu_custom_call" | custom-call | flops 4294967296 | bytes 3145728 | tf_op jit(solution)/shard_map/grads/pallas_call | solution.py:27
  116.5 0.0 copy-start
  116.5 27.9 %all_to_all.27.grads_ref = f32[8,128,128]{2,1,0:T(8,128)S(1)} all-to-all(f32[8,128,128]{2,1,0:T(8,128)S(1)} %grads.1), channel_id=1, replica_groups=mesh['x'=4,'zg'=4,'zc'=4,'core'=2,'y'=4] {'zc','core'}, dimensions={0} | all-to-all | bytes 1048576 | tf_op jit(solution)/shard_map/all_to_all | solution.py:247
  144.4 0.0 copy-done.1
  144.4 0.0 copy-done.2
  144.4 0.0 copy-done
  144.4 0.6 project.1
  145.0 17.7 %all_to_all.28 = f32[4,128,512]{2,1,0:T(8,128)S(1)} all-to-all(f32[4,128,512]{2,1,0:T(8,128)S(1)} %project.1), channel_id=1, replica_groups=mesh['x'=4,'zg'=4,'zc'=4,'core'=2,'y'=4] {'y'}, dimensions={0} | all-to-all | bytes 2097152 | tf_op jit(solution)/shard_map/all_to_all | solution.py:257
  162.7 0.8 reduce_sum.9
Async XLA Ops:
  0.0 0.8 copy-start.3
  0.8 0.8 copy-start.4
  1.7 0.8 copy-start.5
  2.5 0.8 copy-start.6
  23.1 5.5 %collective-permute-start = (f32[4,2,128,128]{3,2,1,0:T(8,128)S(1)}, f32[4,2,128,128]{3,2,1,0:T(8,128)S(1)}, u32[]{:S(2)}, u32[]{:S(2)}) collective-permute-start(f32[4,2,128,128]{3,2,1,0:T(8,128)S(1)} %all_to_all.25.own_ref), channel_id=1, source_target_pairs={{0,4},{4,0},{1,5},{5,1},{2,6},{6,2},{3,7},{7,3},{8,12},{12,8},{9,1... | collective-permute-start | bytes 1572872 | tf_op jit(solution)/shard_map/ppermute | solution.py:207
  79.1 34.0 %all-to-all-start.2 = ((f32[16,72,128]{2,1,0:T(8,128)}), f32[16,72,128]{2,1,0:T(8,128)S(1)}, u32[]{:S(2)}, u32[]{:S(2)}) async-start(f32[16,72,128]{2,1,0:T(8,128)} %scan.1), calls=%async_computation.2 | async-start | bytes 1179648 | tf_op jit(solution)/shard_map/all_to_all | solution.py:232
  113.1 31.3 %copy-start.1 = (bf16[256,2048]{1,0:T(8,128)(2,1)S(1)}, bf16[256,2048]{1,0:T(8,128)(2,1)}, u32[]{:S(2)}) copy-start(bf16[256,2048]{1,0:T(8,128)(2,1)} %wk_ref.1) | copy-start | bytes 3145732
  113.1 31.3 %copy-start.2 = (bf16[256,2048]{1,0:T(8,128)(2,1)S(1)}, bf16[256,2048]{1,0:T(8,128)(2,1)}, u32[]{:S(2)}) copy-start(bf16[256,2048]{1,0:T(8,128)(2,1)} %wv_ref.1) | copy-start | bytes 3145732
  116.5 27.9 %copy-start = (bf16[256,2048]{1,0:T(8,128)(2,1)S(1)}, bf16[256,2048]{1,0:T(8,128)(2,1)}, u32[]{:S(2)}) copy-start(bf16[256,2048]{1,0:T(8,128)(2,1)} %wq_ref.1) | copy-start | bytes 3145732

commit v2 on v1

--- a/solution.py
+++ b/solution.py
@@ -13,11 +13,24 @@
 CHIPS = 4
 BLOCKS = 8
 GRAIN = 8
-SIZES = [HD - GRAIN * (j // GRAIN) for j in range(HD)]
-STARTS = [sum(SIZES[:j]) for j in range(HD)]
-PAIRS = sum(SIZES)
-HALF = PAIRS // 2
-SPLIT_J = STARTS.index(HALF)
+GRAINS = HD // GRAIN
+HALF = 1056
+
+
+def row_tiles():
+    off = [
+        [("off", j, other) for j in range(GRAIN * block, GRAIN * (block + 1)) for other in range(block + 1, GRAINS)]
+        for block in range(GRAINS)
+    ]
+    ring = [[("ring", block, step) for step in range(GRAIN // 2)] for block in range(GRAINS)]
+    left = [("left", block, block + 1) for block in range(0, GRAINS, 2)]
+    empty = [("empty", 0, 0)] * 2
+    first = off[0] + off[1] + sum(ring[:6], []) + left[:2] + empty
+    return first + sum(off[2:], []) + sum(ring[6:], []) + left[2:] + empty
+
+
+TILES = row_tiles()
+assert len(TILES) * GRAIN == 2 * HALF
 VMEM = pl.BlockSpec(memory_space=pltpu.VMEM)
 F32 = jnp.float32
 BF16 = jnp.bfloat16
@@ -43,30 +56,70 @@
 def pack_body(q_ref, k_ref, v_ref, g_ref, out_ref):
     for head in range(CHIPS):
         cols = slice(head * HD, (head + 1) * HD)
-        out_ref[head, 0] = jnp.concatenate([q_ref[:, cols], g_ref[:, cols]], axis=1).astype(F32)
-        out_ref[head, 1] = jnp.concatenate([k_ref[:, cols], v_ref[:, cols]], axis=1).astype(F32)
+        out_ref[2 * head] = jnp.concatenate([k_ref[:, cols], v_ref[:, cols]], axis=1).astype(F32)
+        out_ref[2 * head + 1] = jnp.concatenate([q_ref[:, cols], g_ref[:, cols]], axis=1).astype(F32)
+
+
+def turned(grain, step):
+    return jnp.concatenate([grain[step:], grain[:step]], axis=0) if step else grain
 
 
 def write_features(xt, factor, feats_ref):
-    for block in range(HD // GRAIN):
-        low = GRAIN * block
-        base = xt[low:]
-        if factor != 1.0 and low + GRAIN < HD:
-            base = jnp.concatenate([xt[low : low + GRAIN], xt[low + GRAIN :] * factor], axis=0)
-        for j in range(low, low + GRAIN, 2):
-            pair = [base * xt[j : j + 1], base * xt[j + 1 : j + 2]]
-            start = STARTS[j]
-            feats_ref[start : start + 2 * SIZES[j], :] = jnp.concatenate(pair, axis=0).astype(BF16)
-
-
-def state_body(own_ref, other_ref, state_ref, tok_ref, src_ref, out_ref, feats_ref):
-    core = lax.axis_index("core")
-    for chip in range(CHIPS):
-        for ref, parity in ((own_ref, core), (other_ref, 1 - core)):
-            source = ref[chip, 1 - core]
-            tok_ref[2 * chip + parity] = source.astype(BF16)
-            src_ref[2 * chip + parity] = source.T.astype(BF16)
-            out_ref[2 * chip + parity] = ref[chip, core].T.astype(BF16)
+    grains = [xt[GRAIN * block : GRAIN * (block + 1)] for block in range(GRAINS)]
+    twice = [grain * factor for grain in grains] if factor != 1.0 else grains
+    half = GRAIN // 2
+    tiles = []
+    for kind, one, two in TILES:
+        if kind == "off":
+            tiles.append(xt[one : one + 1] * twice[two])
+        elif kind == "ring":
+            tiles.append(grains[one] * turned(twice[one] if two else grains[one], two))
+        elif kind == "empty":
+            tiles.append(jnp.zeros_like(grains[0]))
+        else:
+            pieces = [grains[block][:half] * twice[block][half:] for block in (one, two)]
+            tiles.append(jnp.concatenate(pieces, axis=0))
+    for place in range(0, len(tiles), 2):
+        rows = slice(GRAIN * place, GRAIN * (place + 2))
+        feats_ref[rows, :] = jnp.concatenate(tiles[place : place + 2], axis=0).astype(BF16)
+
+
+def chain_back(xt, wide_ref):
+    grains = [xt[GRAIN * block : GRAIN * (block + 1)] for block in range(GRAINS)]
+    sums = [jnp.zeros(grains[0].shape, F32) for unused in range(GRAINS)]
+    across = {}
+    half = GRAIN // 2
+    for place, (kind, one, two) in enumerate(TILES):
+        if kind == "empty":
+            continue
+        wide = wide_ref[GRAIN * place : GRAIN * (place + 1)]
+        if kind == "off":
+            sums[two] = sums[two] + xt[one : one + 1] * wide
+            term = grains[two] * wide
+            across[one] = across[one] + term if one in across else term
+        elif kind == "ring":
+            sums[one] = sums[one] + turned(grains[one], two) * wide
+            if two:
+                sums[one] = sums[one] + turned(grains[one] * wide, GRAIN - two)
+        else:
+            for number, block in enumerate((one, two)):
+                piece = wide[half * number : half * (number + 1)]
+                term = [grains[block][half:] * piece, grains[block][:half] * piece]
+                sums[block] = sums[block] + jnp.concatenate(term, axis=0)
+    for block in range(GRAINS - 1):
+        rows = [
+            jnp.sum(across[j], axis=0, keepdims=True)
+            for j in range(GRAIN * block, GRAIN * (block + 1))
+        ]
+        sums[block] = sums[block] + jnp.concatenate(rows, axis=0)
+    return jnp.concatenate(sums, axis=0)
+
+
+def state_body(source_ref, state_ref, tok_ref, src_ref, feats_ref):
+    for block in range(BLOCKS):
+        source = source_ref[block]
+        tok_ref[block] = source.astype(BF16)
+        src_ref[block] = source.T.astype(BF16)
     state_ref[...] = jnp.zeros_like(state_ref)
 
     def step(tile, carry):
@@ -83,11 +136,13 @@
     lax.fori_loop(0, BLOCKS // 2, step, 0)
 
 
-def local_body(tok_ref, src_ref, out_ref, local_ref):
+def local_body(tok_ref, src_ref, target_ref, local_ref, out_ref):
     core = lax.axis_index("core")
     tiles = BLOCKS // 2
     width = 2 * TB
     sign = 1 - 2 * core
+    for block in range(BLOCKS):
+        out_ref[block] = target_ref[block].T.astype(BF16)
     local_ref[...] = jnp.zeros_like(local_ref)
     ahead = lax.broadcasted_iota(jnp.int32, (width, width), 0) - lax.broadcasted_iota(
         jnp.int32, (width, width), 1
@@ -120,23 +175,43 @@
     lax.fori_loop(0, tiles, outer, 0)
 
 
-def scan_body(parts_ref, sums_ref):
+def total_body(parts_ref, total_ref):
+    total = parts_ref[0]
+    for place in range(1, parts_ref.shape[0]):
+        total = total + parts_ref[place]
+    for place in range(total_ref.shape[0]):
+        total_ref[place] = total
+
+
+def scan_body(parts_ref, totals_ref, sums_ref):
     core = lax.axis_index("core")
+    row = lax.axis_index("x")
+    rows = totals_ref.shape[0]
     count = parts_ref.shape[0]
+
+    def add(place, total):
+        return total + totals_ref[place]
+
+    first = jnp.where(core == 0, 0, row + 1)
+    last = jnp.where(core == 0, row, rows)
+    total = lax.fori_loop(first, last, add, jnp.zeros(parts_ref.shape[1:], F32))
 
     def step(number, total):
         place = number + core * (count - 1 - 2 * number)
         sums_ref[place] = total
         return total + parts_ref[place]
 
-    lax.fori_loop(0, count, step, jnp.zeros(parts_ref.shape[1:], F32))
+    lax.fori_loop(0, count, step, total)
 
 
 def grads_body(state_ref, out_ref, local_ref, grads_ref, rows_ref, cols_ref, wide_ref, feats_ref):
     rows_ref[...] = state_ref[...].astype(BF16)
-    for tile in range(HALF // TB):
-        part = slice(tile * TB, (tile + 1) * TB)
-        cols_ref[:, part] = state_ref[part, :].T.astype(BF16)
+    for start in range(0, HALF, TB):
+        stop = min(start + TB, HALF)
+        part = state_ref[start:stop, :]
+        if stop - start < TB:
+            part = jnp.concatenate([part, jnp.zeros((TB - stop + start, TB), F32)], axis=0)
+        cols_ref[:, start:stop] = part.T[:, : stop - start].astype(BF16)
 
     def step(tile, carry):
         target = jnp.concatenate([out_ref[2 * tile], out_ref[2 * tile + 1]], axis=1)
@@ -146,31 +221,8 @@
         wide_ref[HALF:] = dot(rows_ref[...], jnp.concatenate([zeros, target[HD:]], axis=0))
         write_features(xt, 2.0, feats_ref)
         values = dot(cols_ref[:HD, :], feats_ref[:HALF]) + dot(cols_ref[HD:, :], feats_ref[HALF:])
-        count = HD // GRAIN
-        grains = [xt[GRAIN * block : GRAIN * (block + 1)] for block in range(count)]
-        sums = [jnp.zeros((GRAIN, 2 * TB), F32) for unused in range(count)]
-        for block in range(count):
-            rows = []
-            for j in range(GRAIN * block, GRAIN * (block + 1)):
-                row = xt[j : j + 1]
-                across = None
-                for other in range(block, count):
-                    start = STARTS[j] + GRAIN * (other - block)
-                    wide = wide_ref[start : start + GRAIN]
-                    sums[other] = sums[other] + row * wide
-                    if other > block:
-                        term = grains[other] * wide
-                        across = term if across is None else across + term
-                if across is not None:
-                    rows.append(jnp.sum(across, axis=0, keepdims=True))
-            if rows:
-                sums[block] = sums[block] + jnp.concatenate(rows, axis=0)
         result = local_ref[tile] + jnp.concatenate(
-            [
-                jnp.concatenate(sums, axis=0) * (2.0 / (HD * HD)),
-                values * (1.0 / (HD * HD)),
-            ],
-            axis=0,
+            [chain_back(xt, wide_ref) * (2.0 / (HD * HD)), values * (1.0 / (HD * HD))], axis=0
         )
         grads_ref[2 * tile] = result[:, :TB].T
         grads_ref[2 * tile + 1] = result[:, TB:].T
@@ -194,42 +246,54 @@
 
 def on_device(queries, keys, values, out_grad, w_query, w_key, w_value):
     shape = jax.ShapeDtypeStruct
-    groups = lax.axis_size("x") * lax.axis_size("zg")
+    rows, cols = lax.axis_size("x"), lax.axis_size("zg")
     packed = call(
         pack_body,
-        shape((CHIPS, 2, TB, TB), F32),
+        shape((BLOCKS, TB, TB), F32),
         (queries, keys, values, out_grad),
         "pack",
         flops=1 << 20,
         nbytes=1 << 20,
     )
-    own = lax.all_to_all(packed, "zc", 0, 0, tiled=True)
-    other = lax.ppermute(own, "core", [(0, 1), (1, 0)])
+    source = lax.all_to_all(packed, ("zc", "core"), 0, 0, tiled=True)
+    target = lax.ppermute(source, "core", [(0, 1), (1, 0)])
     blocks = shape((BLOCKS, TB, TB), BF16)
-    state, tok, src, out = call(
+    state, tok, src = call(
         state_body,
-        (shape((HALF, TB), F32), blocks, blocks, blocks),
-        (own, other),
+        (shape((HALF, TB), F32), blocks, blocks),
+        (source,),
         "state",
-        scratch=[pltpu.VMEM((PAIRS, 2 * TB), BF16)],
+        scratch=[pltpu.VMEM((2 * HALF, 2 * TB), BF16)],
         flops=4 << 30,
         nbytes=3 << 20,
     )
-    shards = lax.all_to_all(
-        state.reshape(groups, HALF // groups, TB), ("x", "zg"), 0, 0, tiled=True
-    )
-    local = call(
+    parts = lax.all_to_all(state.reshape(cols, HALF // cols, TB), "zg", 0, 0, tiled=True)
+    total = call(
+        total_body,
+        shape((rows, HALF // cols, TB), F32),
+        (parts,),
+        "total",
+        flops=1 << 20,
+        nbytes=1 << 20,
+    )
+    totals = lax.all_to_all(total, "x", 0, 0, tiled=True)
+    sums = call(
+        scan_body,
+        shape(parts.shape, F32),
+        (parts, totals),
+        "scan",
+        flops=1 << 20,
+        nbytes=1 << 20,
+    )
+    before = lax.all_to_all(sums, "zg", 0, 0, tiled=True).reshape(HALF, TB)
+    local, out = call(
         local_body,
-        shape((BLOCKS // 2, TB, 2 * TB), F32),
-        (tok, src, out),
+        (shape((BLOCKS // 2, TB, 2 * TB), F32), blocks),
+        (tok, src, target),
         "local",
         flops=4 << 30,
         nbytes=1 << 20,
     )
-    sums = call(
-        scan_body, shape(shards.shape, F32), (shards,), "scan", flops=1 << 20, nbytes=1 << 20
-    )
-    before = lax.all_to_all(sums, ("x", "zg"), 0, 0, tiled=True).reshape(HALF, TB)
     grads = call(
         grads_body,
         shape((BLOCKS, TB, TB), F32),
@@ -238,8 +302,8 @@
         scratch=[
             pltpu.VMEM((HALF, TB), BF16),
             pltpu.VMEM((TB, HALF), BF16),
-            pltpu.VMEM((PAIRS, 2 * TB), F32),
-            pltpu.VMEM((PAIRS, 2 * TB), BF16),
+            pltpu.VMEM((2 * HALF, 2 * TB), F32),
+            pltpu.VMEM((2 * HALF, 2 * TB), BF16),
         ],
         flops=4 << 30,
         nbytes=3 << 20,

time: 164 us -> 156 us (0.951)
  waiting for transfers between devices: 25 us -> 19.9 us
  blocking collectives: 112 us -> 108 us
  starting transfers between devices: 10.9 us -> 12.9 us
    all_to_all x1, blocking collectives: 27.9 us -> 18.2 us  [on_device(): mine = lax.all_to_all(grads, ('zc', 'core'), 0, 0, tiled=True)]
    all_to_all x2 -> x3, blocking collectives: 66.8 us -> 72.1 us  [the longest x1 37.7 us: on_device(): lax.all_to_all(state.reshape(cols, HALF // cols, TB), 'zg', 0, 0, tiled=T...]
    all_to_all x1, waiting for transfers between devices: 23.4 us -> 18.4 us  [on_device(): before = lax.all_to_all(sums, 'zg', 0, 0, tiled=True).reshape(HALF, TB)]
    all_to_all x1, starting transfers between devices: 6.89 us -> 8.81 us  [on_device(): before = lax.all_to_all(sums, 'zg', 0, 0, tiled=True).reshape(HALF, TB)]
    pallas_call x6 -> x7, Pallas kernels: 11 us -> 10.9 us  [call(): pl.pallas_call(body, out_shape=out_shape, in_specs=[VMEM] * len(args), ou...]
where the time goes in v2:
time: 156 us
  blocking collectives  108 us (69%)
  waiting for transfers between devices  19.9 us (13%)
  starting transfers between devices  12.9 us (8%)
  Pallas kernels  10.9 us (7%)
  local copies, waits for them, and re-layouts  3.37 us (2%)
    all_to_all x1, blocking collectives, on_device(): lax.all_to_all(state.reshape(cols, HALF // cols, TB), 'zg', 0, 0, tiled=T...  37.7 us
    all_to_all x1, blocking collectives, on_device(): source = lax.all_to_all(packed, ('zc', 'core'), 0, 0, tiled=True)  23.5 us
    all_to_all x1, waiting for transfers between devices, on_device(): before = lax.all_to_all(sums, 'zg', 0, 0, tiled=True).reshape(HALF, TB)  18.4 us
    all_to_all x1, blocking collectives, on_device(): mine = lax.all_to_all(grads, ('zc', 'core'), 0, 0, tiled=True)  18.2 us
    all_to_all x1, blocking collectives, on_device(): pieces = lax.all_to_all(partial_sum, 'y', 0, 0, tiled=True)  17.6 us
    pallas_call x7, Pallas kernels, call(): pl.pallas_call(body, out_shape=out_shape, in_specs=[VMEM] * len(args), ou...  10.9 us
    all_to_all x1, blocking collectives, on_device(): totals = lax.all_to_all(total, 'x', 0, 0, tiled=True)  10.8 us
    all_to_all x1, starting transfers between devices, on_device(): before = lax.all_to_all(sums, 'zg', 0, 0, tiled=True).reshape(HALF, TB)  8.81 us
  transfers between devices with their start and end apart: 2, of which 2 were waited for; matrix products, arithmetic and copies ran while one was open for 0% of the time, Pallas kernels for 2%

profile of v2, /device:TPU:1, one launch (start us, length us, event | category | flops | bytes accessed | tf_op | source)
XLA Modules:
  0.0 155.7 jit_solution(6860755098155426166)
XLA Ops:
  0.0 0.0 copy-start.3
  0.0 0.8 copy-done.3
  0.8 0.0 copy-start.4
  0.8 0.8 copy-done.4
  1.7 0.0 copy-start.5
  1.7 0.8 copy-done.5
  2.5 0.0 copy-start.6
  2.5 0.8 copy-done.6
  3.4 0.1 pack.1
  3.5 23.5 %all_to_all.30.source_ref = f32[8,128,128]{2,1,0:T(8,128)S(1)} all-to-all(f32[8,128,128]{2,1,0:T(8,128)S(1)} %pack.1), channel_id=1, replica_groups=mesh['x'=4,'zg'=4,'zc'=4,'core'=2,'y'=4] {'zc','core'}, dimensions={0} | all-to-all | bytes 1048576 | tf_op jit(solution)/shard_map/all_to_all | solution.py:258
  27.0 2.1 %state.1 = (f32[1056,128]{1,0:T(8,128)S(1)}, bf16[8,128,128]{2,1,0:T(8,128)(2,1)S(1)}, bf16[8,128,128]{2,1,0:T(8,128)(2,1)S(1)}) custom-call(f32[8,128,128]{2,1,0:T(8,128)S(1)} %all_to_all.30.source_ref), custom_call_target="tpu_custom_call" | custom-call | flops 4294967296 | bytes 3145728 | tf_op jit(solution)/shard_map/state/pallas_call | solution.py:40
  29.2 37.7 %all_to_all.31.parts_ref = f32[4,264,128]{2,1,0:T(8,128)S(1)} all-to-all(f32[4,264,128]{2,1,0:T(8,128)S(1)} %bitcast.3), channel_id=1, replica_groups=mesh['x'=4,'zg'=4,'zc'=4,'core'=2,'y'=4] {'zg'}, dimensions={0} | all-to-all | bytes 1081344 | tf_op jit(solution)/shard_map/all_to_all | solution.py:270
  66.9 10.8 %all_to_all.32.totals_ref = f32[4,264,128]{2,1,0:T(8,128)S(1)} all-to-all(f32[4,264,128]{2,1,0:T(8,128)S(1)} %total.1), channel_id=1, replica_groups=mesh['x'=4,'zg'=4,'zc'=4,'core'=2,'y'=4] {'x'}, dimensions={0} | all-to-all | bytes 1081344 | tf_op jit(solution)/shard_map/all_to_all | solution.py:279
  77.8 0.9 scan.1
  78.7 8.8 %all-to-all-start.3 = ((f32[4,264,128]{2,1,0:T(8,128)}), f32[4,264,128]{2,1,0:T(8,128)S(1)}, u32[]{:S(2)}, u32[]{:S(2)}) async-start(f32[4,264,128]{2,1,0:T(8,128)} %scan.1), calls=%async_computation.3 | async-start | bytes 1081344 | tf_op jit(solution)/shard_map/all_to_all | solution.py:288
  87.5 4.1 %collective-permute-start = (f32[8,128,128]{2,1,0:T(8,128)S(1)}, f32[8,128,128]{2,1,0:T(8,128)S(1)}, u32[]{:S(2)}, u32[]{:S(2)}) collective-permute-start(f32[8,128,128]{2,1,0:T(8,128)S(1)} %all_to_all.30.source_ref), channel_id=1, source_target_pairs={{0,4},{4,0},{1,5},{5,1},{2,6},{6,2},{3,7},{7,3},{8,12},{12,8},{9,1... | collective-permute-start | bytes 1572872 | tf_op jit(solution)/shard_map/ppermute | solution.py:259
  91.5 1.5 collective-permute-done.target_ref
  93.1 3.7 %local.1 = (f32[4,128,256]{2,1,0:T(8,128)S(1)}, bf16[8,128,128]{2,1,0:T(8,128)(2,1)S(1)}) custom-call(bf16[8,128,128]{2,1,0:T(8,128)(2,1)S(1)} %get-tuple-element.11.tok_ref, bf16[8,128,128]{2,1,0:T(8,128)(2,1)S(1)} %get-tuple-element.12.src_ref, f32[8,128,128]{2,1,0:T(8,128)S(1)} %collective-permute-done.target_ref), custom_call_target="tpu_custom_call" | custom-call | flops 4294967296 | bytes 1048576 | tf_op jit(solution)/shard_map/local/pallas_call | solution.py:40
  96.7 18.4 %all-to-all-done.3 = f32[4,264,128]{2,1,0:T(8,128)S(1)} async-done(((f32[4,264,128]{2,1,0:T(8,128)}), f32[4,264,128]{2,1,0:T(8,128)S(1)}, u32[]{:S(2)}, u32[]{:S(2)}) %all-to-all-start.3) | async-done | bytes 540704 | tf_op jit(solution)/shard_map/all_to_all | solution.py:288
  115.1 0.0 copy-start.1
  115.1 0.0 copy-start.2
  115.1 3.3 %grads.1 = f32[8,128,128]{2,1,0:T(8,128)S(1)} custom-call(f32[1056,128]{1,0:T(8,128)S(1)} %bitcast.2, bf16[8,128,128]{2,1,0:T(8,128)(2,1)S(1)} %get-tuple-element.13.out_ref, f32[4,128,256]{2,1,0:T(8,128)S(1)} %get-tuple-element.14.local_ref), custom_call_target="tpu_custom_call" | custom-call | flops 4294967296 | bytes 3145728 | tf_op jit(solution)/shard_map/grads/pallas_call | solution.py:40
  118.5 0.0 copy-start
  118.5 18.2 %all_to_all.33.grads_ref = f32[8,128,128]{2,1,0:T(8,128)S(1)} all-to-all(f32[8,128,128]{2,1,0:T(8,128)S(1)} %grads.1), channel_id=1, replica_groups=mesh['x'=4,'zg'=4,'zc'=4,'core'=2,'y'=4] {'zc','core'}, dimensions={0} | all-to-all | bytes 1048576 | tf_op jit(solution)/shard_map/all_to_all | solution.py:311
  136.7 0.0 copy-done.1
  136.7 0.0 copy-done.2
  136.7 0.0 copy-done
  136.7 0.6 project.1
  137.4 17.6 %all_to_all.34 = f32[4,128,512]{2,1,0:T(8,128)S(1)} all-to-all(f32[4,128,512]{2,1,0:T(8,128)S(1)} %project.1), channel_id=1, replica_groups=mesh['x'=4,'zg'=4,'zc'=4,'core'=2,'y'=4] {'y'}, dimensions={0} | all-to-all | bytes 2097152 | tf_op jit(solution)/shard_map/all_to_all | solution.py:321
  154.9 0.8 reduce_sum.9
  (1 shorter events, 0.0 us)
Async XLA Ops:
  0.0 0.8 copy-start.3
  0.8 0.8 copy-start.4
  1.7 0.8 copy-start.5
  2.5 0.8 copy-start.6
  78.7 36.4 %all-to-all-start.3 = ((f32[4,264,128]{2,1,0:T(8,128)}), f32[4,264,128]{2,1,0:T(8,128)S(1)}, u32[]{:S(2)}, u32[]{:S(2)}) async-start(f32[4,264,128]{2,1,0:T(8,128)} %scan.1), calls=%async_computation.3 | async-start | bytes 1081344 | tf_op jit(solution)/shard_map/all_to_all | solution.py:288
  87.5 5.6 %collective-permute-start = (f32[8,128,128]{2,1,0:T(8,128)S(1)}, f32[8,128,128]{2,1,0:T(8,128)S(1)}, u32[]{:S(2)}, u32[]{:S(2)}) collective-permute-start(f32[8,128,128]{2,1,0:T(8,128)S(1)} %all_to_all.30.source_ref), channel_id=1, source_target_pairs={{0,4},{4,0},{1,5},{5,1},{2,6},{6,2},{3,7},{7,3},{8,12},{12,8},{9,1... | collective-permute-start | bytes 1572872 | tf_op jit(solution)/shard_map/ppermute | solution.py:259
  115.1 21.6 %copy-start.1 = (bf16[256,2048]{1,0:T(8,128)(2,1)S(1)}, bf16[256,2048]{1,0:T(8,128)(2,1)}, u32[]{:S(2)}) copy-start(bf16[256,2048]{1,0:T(8,128)(2,1)} %wk_ref.1) | copy-start | bytes 3145732
  115.1 21.6 %copy-start.2 = (bf16[256,2048]{1,0:T(8,128)(2,1)S(1)}, bf16[256,2048]{1,0:T(8,128)(2,1)}, u32[]{:S(2)}) copy-start(bf16[256,2048]{1,0:T(8,128)(2,1)} %wv_ref.1) | copy-start | bytes 3145732
  118.5 18.3 %copy-start = (bf16[256,2048]{1,0:T(8,128)(2,1)S(1)}, bf16[256,2048]{1,0:T(8,128)(2,1)}, u32[]{:S(2)}) copy-start(bf16[256,2048]{1,0:T(8,128)(2,1)} %wq_ref.1) | copy-start | bytes 3145732

commit v3 on v2

--- a/solution.py
+++ b/solution.py
@@ -14,7 +14,7 @@
 BLOCKS = 8
 GRAIN = 8
 GRAINS = HD // GRAIN
-HALF = 1056
+HALF = 1040
 
 
 def row_tiles():
@@ -24,9 +24,8 @@
     ]
     ring = [[("ring", block, step) for step in range(GRAIN // 2)] for block in range(GRAINS)]
     left = [("left", block, block + 1) for block in range(0, GRAINS, 2)]
-    empty = [("empty", 0, 0)] * 2
-    first = off[0] + off[1] + sum(ring[:6], []) + left[:2] + empty
-    return first + sum(off[2:], []) + sum(ring[6:], []) + left[2:] + empty
+    first = off[0] + off[1] + sum(ring[:6], []) + left[:2]
+    return first + sum(off[2:], []) + sum(ring[6:], []) + left[2:]
 
 
 TILES = row_tiles()
@@ -36,7 +35,7 @@
 BF16 = jnp.bfloat16
 
 
-def call(body, out_shape, args, name, scratch=(), flops=0, nbytes=0):
+def call(body, out_shape, args, name, scratch=(), flops=0, nbytes=0, limit=24 << 20):
     return pl.pallas_call(
         body,
         out_shape=out_shape,
@@ -44,7 +43,7 @@
         out_specs=jax.tree.map(lambda unused: VMEM, out_shape),
         scratch_shapes=list(scratch),
         name=name,
-        compiler_params=pltpu.CompilerParams(vmem_limit_bytes=24 << 20),
+        compiler_params=pltpu.CompilerParams(vmem_limit_bytes=limit),
         cost_estimate=pl.CostEstimate(flops=flops, bytes_accessed=nbytes, transcendentals=0),
     )(*args)
 
@@ -74,8 +73,6 @@
             tiles.append(xt[one : one + 1] * twice[two])
         elif kind == "ring":
             tiles.append(grains[one] * turned(twice[one] if two else grains[one], two))
-        elif kind == "empty":
-            tiles.append(jnp.zeros_like(grains[0]))
         else:
             pieces = [grains[block][:half] * twice[block][half:] for block in (one, two)]
             tiles.append(jnp.concatenate(pieces, axis=0))
@@ -90,8 +87,6 @@
     across = {}
     half = GRAIN // 2
     for place, (kind, one, two) in enumerate(TILES):
-        if kind == "empty":
-            continue
         wide = wide_ref[GRAIN * place : GRAIN * (place + 1)]
         if kind == "off":
             sums[two] = sums[two] + xt[one : one + 1] * wide
@@ -175,43 +170,30 @@
     lax.fori_loop(0, tiles, outer, 0)
 
 
-def total_body(parts_ref, total_ref):
-    total = parts_ref[0]
-    for place in range(1, parts_ref.shape[0]):
-        total = total + parts_ref[place]
-    for place in range(total_ref.shape[0]):
-        total_ref[place] = total
-
-
-def scan_body(parts_ref, totals_ref, sums_ref):
+def scan_body(parts_ref, sums_ref):
     core = lax.axis_index("core")
-    row = lax.axis_index("x")
-    rows = totals_ref.shape[0]
     count = parts_ref.shape[0]
-
-    def add(place, total):
-        return total + totals_ref[place]
-
-    first = jnp.where(core == 0, 0, row + 1)
-    last = jnp.where(core == 0, row, rows)
-    total = lax.fori_loop(first, last, add, jnp.zeros(parts_ref.shape[1:], F32))
 
     def step(number, total):
         place = number + core * (count - 1 - 2 * number)
         sums_ref[place] = total
         return total + parts_ref[place]
 
-    lax.fori_loop(0, count, step, total)
+    lax.fori_loop(0, count, step, jnp.zeros(parts_ref.shape[1:], F32))
 
 
 def grads_body(state_ref, out_ref, local_ref, grads_ref, rows_ref, cols_ref, wide_ref, feats_ref):
+    keyed = lax.axis_index("core") == 1
     rows_ref[...] = state_ref[...].astype(BF16)
-    for start in range(0, HALF, TB):
-        stop = min(start + TB, HALF)
-        part = state_ref[start:stop, :]
-        if stop - start < TB:
-            part = jnp.concatenate([part, jnp.zeros((TB - stop + start, TB), F32)], axis=0)
-        cols_ref[:, start:stop] = part.T[:, : stop - start].astype(BF16)
+
+    @pl.when(keyed)
+    def turn():
+        for start in range(0, HALF, TB):
+            stop = min(start + TB, HALF)
+            part = state_ref[start:stop, :]
+            if stop - start < TB:
+                part = jnp.concatenate([part, jnp.zeros((TB - stop + start, TB), F32)], axis=0)
+            cols_ref[:, start:stop] = part.T[:, : stop - start].astype(BF16)
 
     def step(tile, carry):
         target = jnp.concatenate([out_ref[2 * tile], out_ref[2 * tile + 1]], axis=1)
@@ -219,13 +201,25 @@
         zeros = jnp.zeros((HD, 2 * TB), BF16)
         wide_ref[:HALF] = dot(rows_ref[...], jnp.concatenate([target[HD:], zeros], axis=0))
         wide_ref[HALF:] = dot(rows_ref[...], jnp.concatenate([zeros, target[HD:]], axis=0))
-        write_features(xt, 2.0, feats_ref)
-        values = dot(cols_ref[:HD, :], feats_ref[:HALF]) + dot(cols_ref[HD:, :], feats_ref[HALF:])
-        result = local_ref[tile] + jnp.concatenate(
-            [chain_back(xt, wide_ref) * (2.0 / (HD * HD)), values * (1.0 / (HD * HD))], axis=0
-        )
-        grads_ref[2 * tile] = result[:, :TB].T
-        grads_ref[2 * tile + 1] = result[:, TB:].T
+        result = local_ref[tile, :HD] + chain_back(xt, wide_ref) * (2.0 / (HD * HD))
+        grads_ref[2 * tile, :, :HD] = result[:, :TB].T
+        grads_ref[2 * tile + 1, :, :HD] = result[:, TB:].T
+
+        @pl.when(keyed)
+        def value_part():
+            write_features(xt, 2.0, feats_ref)
+            values = dot(cols_ref[:HD, :], feats_ref[:HALF]) + dot(
+                cols_ref[HD:, :], feats_ref[HALF:]
+            )
+            total = local_ref[tile, HD:] + values * (1.0 / (HD * HD))
+            grads_ref[2 * tile, :, HD:] = total[:, :TB].T
+            grads_ref[2 * tile + 1, :, HD:] = total[:, TB:].T
+
+        @pl.when(jnp.logical_not(keyed))
+        def no_values():
+            grads_ref[2 * tile, :, HD:] = jnp.zeros((TB, HD), F32)
+            grads_ref[2 * tile + 1, :, HD:] = jnp.zeros((TB, HD), F32)
+
         return carry
 
     lax.fori_loop(0, BLOCKS // 2, step, 0)
@@ -246,12 +240,13 @@
 
 def on_device(queries, keys, values, out_grad, w_query, w_key, w_value):
     shape = jax.ShapeDtypeStruct
-    rows, cols = lax.axis_size("x"), lax.axis_size("zg")
+    groups = lax.axis_size("x") * lax.axis_size("zg")
     packed = call(
         pack_body,
         shape((BLOCKS, TB, TB), F32),
         (queries, keys, values, out_grad),
         "pack",
+        limit=None,
         flops=1 << 20,
         nbytes=1 << 20,
     )
@@ -267,25 +262,13 @@
         flops=4 << 30,
         nbytes=3 << 20,
     )
-    parts = lax.all_to_all(state.reshape(cols, HALF // cols, TB), "zg", 0, 0, tiled=True)
-    total = call(
-        total_body,
-        shape((rows, HALF // cols, TB), F32),
-        (parts,),
-        "total",
-        flops=1 << 20,
-        nbytes=1 << 20,
-    )
-    totals = lax.all_to_all(total, "x", 0, 0, tiled=True)
+    parts = lax.all_to_all(
+        state.reshape(groups, 1, HALF * TB // groups), ("x", "zg"), 0, 0, tiled=True
+    )
     sums = call(
-        scan_body,
-        shape(parts.shape, F32),
-        (parts, totals),
-        "scan",
-        flops=1 << 20,
-        nbytes=1 << 20,
-    )
-    before = lax.all_to_all(sums, "zg", 0, 0, tiled=True).reshape(HALF, TB)
+        scan_body, shape(parts.shape, F32), (parts,), "scan", flops=1 << 20, nbytes=1 << 20
+    )
+    before = lax.all_to_all(sums, ("x", "zg"), 0, 0, tiled=True).reshape(HALF, TB)
     local, out = call(
         local_body,
         (shape((BLOCKS // 2, TB, 2 * TB), F32), blocks),

time: 156 us -> 152 us (0.974)
  blocking collectives: 108 us -> 104 us
  local copies, waits for them, and re-layouts: 3.37 us -> 0.01 us
  Pallas kernels: 10.9 us -> 14.1 us
  waiting for transfers between devices: 19.9 us -> 22.9 us
  starting transfers between devices: 12.9 us -> 10.1 us
    all_to_all x2 -> x1, blocking collectives: 48.5 us -> 41.9 us  [on_device(): lax.all_to_all(state.reshape(groups, 1, HALF * TB // groups), ('x', 'zg')...]
    unnamed x14 -> x6, local copies, waits for them, and re-layouts: 3.37 us -> 0.01 us
    pallas_call x7 -> x6, Pallas kernels: 10.9 us -> 14.1 us  [call(): pl.pallas_call(body, out_shape=out_shape, in_specs=[VMEM] * len(args), ou...]
    all_to_all x1, waiting for transfers between devices: 18.4 us -> 21.4 us  [on_device(): lax.all_to_all(sums, ('x', 'zg'), 0, 0, tiled=True).reshape(HALF, TB)]
    all_to_all x1, starting transfers between devices: 8.81 us -> 7.11 us  [on_device(): lax.all_to_all(sums, ('x', 'zg'), 0, 0, tiled=True).reshape(HALF, TB)]
where the time goes in v3:
time: 152 us; the launch traced here: 151 us
  blocking collectives  104 us (68%)
  waiting for transfers between devices  22.9 us (15%)
  Pallas kernels  14.1 us (9%)
  starting transfers between devices  10.1 us (7%)
    all_to_all x1, blocking collectives, on_device(): lax.all_to_all(state.reshape(groups, 1, HALF * TB // groups), ('x', 'zg')...  41.9 us
    all_to_all x1, blocking collectives, on_device(): source = lax.all_to_all(packed, ('zc', 'core'), 0, 0, tiled=True)  24.5 us
    all_to_all x1, waiting for transfers between devices, on_device(): lax.all_to_all(sums, ('x', 'zg'), 0, 0, tiled=True).reshape(HALF, TB)  21.4 us
    all_to_all x1, blocking collectives, on_device(): mine = lax.all_to_all(grads, ('zc', 'core'), 0, 0, tiled=True)  19.6 us
    all_to_all x1, blocking collectives, on_device(): pieces = lax.all_to_all(partial_sum, 'y', 0, 0, tiled=True)  17.6 us
    pallas_call x6, Pallas kernels, call(): pl.pallas_call(body, out_shape=out_shape, in_specs=[VMEM] * len(args), ou...  14.1 us
    all_to_all x1, starting transfers between devices, on_device(): lax.all_to_all(sums, ('x', 'zg'), 0, 0, tiled=True).reshape(HALF, TB)  7.11 us
  transfers between devices with their start and end apart: 2, of which 2 were waited for; matrix products, arithmetic and copies ran while one was open for 0% of the time, Pallas kernels for 2%

profile of v3, /device:TPU:1, one launch (start us, length us, event | category | flops | bytes accessed | tf_op | source)
XLA Modules:
  0.0 151.5 jit_solution(1442956917993682762)
XLA Ops:
  0.0 1.9 %pack.1 = f32[8,128,128]{2,1,0:T(8,128)} custom-call(bf16[128,256]{1,0:T(8,128)(2,1)} %q_ref.1, bf16[128,256]{1,0:T(8,128)(2,1)} %k_ref.1, bf16[128,256]{1,0:T(8,128)(2,1)} %v_ref.1, bf16[128,256]{1,0:T(8,128)(2,1)} %g_ref.1), custom_call_target="tpu_custom_call" | custom-call | flops 1048576 | bytes 1048576 | tf_op jit(solution)/shard_map/pack/pallas_call | solution.py:39
  1.9 24.5 %all_to_all.25.source_ref = f32[8,128,128]{2,1,0:T(8,128)S(1)} all-to-all(f32[8,128,128]{2,1,0:T(8,128)} %pack.1), channel_id=1, replica_groups=mesh['x'=4,'zg'=4,'zc'=4,'core'=2,'y'=4] {'zc','core'}, dimensions={0} | all-to-all | bytes 1048576 | tf_op jit(solution)/shard_map/all_to_all | solution.py:253
  26.4 2.1 %state.1 = (f32[1040,128]{1,0:T(8,128)S(1)}, bf16[8,128,128]{2,1,0:T(8,128)(2,1)S(1)}, bf16[8,128,128]{2,1,0:T(8,128)(2,1)S(1)}) custom-call(f32[8,128,128]{2,1,0:T(8,128)S(1)} %all_to_all.25.source_ref), custom_call_target="tpu_custom_call" | custom-call | flops 4294967296 | bytes 3145728 | tf_op jit(solution)/shard_map/state/pallas_call | solution.py:39
  28.5 41.9 %all_to_all.26.parts_ref = f32[16,1,8320]{2,1,0:T(1,128)S(1)} all-to-all(f32[16,1,8320]{2,1,0:T(1,128)S(1)} %bitcast.3), channel_id=1, replica_groups=mesh['x'=4,'zg'=4,'zc'=4,'core'=2,'y'=4] {'x','zg'}, dimensions={0} | all-to-all | bytes 1064960 | tf_op jit(solution)/shard_map/all_to_all | solution.py:265
  70.4 0.9 scan.1
  71.3 7.1 %all-to-all-start.2 = ((f32[16,1,8320]{2,1,0:T(1,128)}), f32[16,1,8320]{2,1,0:T(1,128)S(1)}, u32[]{:S(2)}, u32[]{:S(2)}) async-start(f32[16,1,8320]{2,1,0:T(1,128)} %scan.1), calls=%async_computation.2 | async-start | bytes 1064960 | tf_op jit(solution)/shard_map/all_to_all | solution.py:271
  78.4 3.0 %collective-permute-start = (f32[8,128,128]{2,1,0:T(8,128)S(1)}, f32[8,128,128]{2,1,0:T(8,128)S(1)}, u32[]{:S(2)}, u32[]{:S(2)}) collective-permute-start(f32[8,128,128]{2,1,0:T(8,128)S(1)} %all_to_all.25.source_ref), channel_id=1, source_target_pairs={{0,4},{4,0},{1,5},{5,1},{2,6},{6,2},{3,7},{7,3},{8,12},{12,8},{9,1... | collective-permute-start | bytes 1572872 | tf_op jit(solution)/shard_map/ppermute | solution.py:254
  81.5 1.5 collective-permute-done.target_ref
  83.0 3.7 %local.1 = (f32[4,128,256]{2,1,0:T(8,128)S(1)}, bf16[8,128,128]{2,1,0:T(8,128)(2,1)S(1)}) custom-call(bf16[8,128,128]{2,1,0:T(8,128)(2,1)S(1)} %get-tuple-element.11.tok_ref, bf16[8,128,128]{2,1,0:T(8,128)(2,1)S(1)} %get-tuple-element.12.src_ref, f32[8,128,128]{2,1,0:T(8,128)S(1)} %collective-permute-done.target_ref), custom_call_target="tpu_custom_call" | custom-call | flops 4294967296 | bytes 1048576 | tf_op jit(solution)/shard_map/local/pallas_call | solution.py:39
  86.7 21.4 %all-to-all-done.2 = f32[16,1,8320]{2,1,0:T(1,128)S(1)} async-done(((f32[16,1,8320]{2,1,0:T(1,128)}), f32[16,1,8320]{2,1,0:T(1,128)S(1)}, u32[]{:S(2)}, u32[]{:S(2)}) %all-to-all-start.2) | async-done | bytes 532512 | tf_op jit(solution)/shard_map/all_to_all | solution.py:271
  108.0 0.0 copy-start.1
  108.0 0.0 copy-start.2
  108.0 4.9 %grads.1 = f32[8,128,128]{2,1,0:T(8,128)S(1)} custom-call(f32[1040,128]{1,0:T(8,128)S(1)} %bitcast.2, bf16[8,128,128]{2,1,0:T(8,128)(2,1)S(1)} %get-tuple-element.13.out_ref, f32[4,128,256]{2,1,0:T(8,128)S(1)} %get-tuple-element.14.local_ref), custom_call_target="tpu_custom_call" | custom-call | flops 4294967296 | bytes 3145728 | tf_op jit(solution)/shard_map/grads/pallas_call | solution.py:39
  112.9 0.0 copy-start
  112.9 19.6 %all_to_all.27.grads_ref = f32[8,128,128]{2,1,0:T(8,128)S(1)} all-to-all(f32[8,128,128]{2,1,0:T(8,128)S(1)} %grads.1), channel_id=1, replica_groups=mesh['x'=4,'zg'=4,'zc'=4,'core'=2,'y'=4] {'zc','core'}, dimensions={0} | all-to-all | bytes 1048576 | tf_op jit(solution)/shard_map/all_to_all | solution.py:294
  132.5 0.0 copy-done.1
  132.5 0.0 copy-done.2
  132.5 0.0 copy-done
  132.5 0.6 project.1
  133.1 17.6 %all_to_all.28 = f32[4,128,512]{2,1,0:T(8,128)S(1)} all-to-all(f32[4,128,512]{2,1,0:T(8,128)S(1)} %project.1), channel_id=1, replica_groups=mesh['x'=4,'zg'=4,'zc'=4,'core'=2,'y'=4] {'y'}, dimensions={0} | all-to-all | bytes 2097152 | tf_op jit(solution)/shard_map/all_to_all | solution.py:304
  150.7 0.8 reduce_sum.9
Async XLA Ops:
  71.3 36.7 %all-to-all-start.2 = ((f32[16,1,8320]{2,1,0:T(1,128)}), f32[16,1,8320]{2,1,0:T(1,128)S(1)}, u32[]{:S(2)}, u32[]{:S(2)}) async-start(f32[16,1,8320]{2,1,0:T(1,128)} %scan.1), calls=%async_computation.2 | async-start | bytes 1064960 | tf_op jit(solution)/shard_map/all_to_all | solution.py:271
  78.4 4.5 %collective-permute-start = (f32[8,128,128]{2,1,0:T(8,128)S(1)}, f32[8,128,128]{2,1,0:T(8,128)S(1)}, u32[]{:S(2)}, u32[]{:S(2)}) collective-permute-start(f32[8,128,128]{2,1,0:T(8,128)S(1)} %all_to_all.25.source_ref), channel_id=1, source_target_pairs={{0,4},{4,0},{1,5},{5,1},{2,6},{6,2},{3,7},{7,3},{8,12},{12,8},{9,1... | collective-permute-start | bytes 1572872 | tf_op jit(solution)/shard_map/ppermute | solution.py:254
  108.0 24.5 %copy-start.1 = (bf16[256,2048]{1,0:T(8,128)(2,1)S(1)}, bf16[256,2048]{1,0:T(8,128)(2,1)}, u32[]{:S(2)}) copy-start(bf16[256,2048]{1,0:T(8,128)(2,1)} %wk_ref.1) | copy-start | bytes 3145732
  108.0 24.5 %copy-start.2 = (bf16[256,2048]{1,0:T(8,128)(2,1)S(1)}, bf16[256,2048]{1,0:T(8,128)(2,1)}, u32[]{:S(2)}) copy-start(bf16[256,2048]{1,0:T(8,128)(2,1)} %wv_ref.1) | copy-start | bytes 3145732
  112.9 19.6 %copy-start = (bf16[256,2048]{1,0:T(8,128)(2,1)S(1)}, bf16[256,2048]{1,0:T(8,128)(2,1)}, u32[]{:S(2)}) copy-start(bf16[256,2048]{1,0:T(8,128)(2,1)} %wq_ref.1) | copy-start | bytes 3145732

commit v4 on v3

--- a/solution.py
+++ b/solution.py
@@ -110,7 +110,7 @@
     return jnp.concatenate(sums, axis=0)
 
 
-def state_body(source_ref, state_ref, tok_ref, src_ref, feats_ref):
+def state_body(source_ref, unused_ref, state_ref, tok_ref, src_ref, feats_ref):
     for block in range(BLOCKS):
         source = source_ref[block]
         tok_ref[block] = source.astype(BF16)
@@ -131,19 +131,26 @@
     lax.fori_loop(0, BLOCKS // 2, step, 0)
 
 
-def local_body(tok_ref, src_ref, target_ref, local_ref, out_ref):
+def tick_body(unused_ref, tick_ref):
+    tick_ref[...] = jnp.zeros_like(tick_ref)
+
+
+def local_body(tiles, first_tile, tok_ref, src_ref, target_ref, local_ref, *out_refs):
     core = lax.axis_index("core")
-    tiles = BLOCKS // 2
     width = 2 * TB
     sign = 1 - 2 * core
-    for block in range(BLOCKS):
-        out_ref[block] = target_ref[block].T.astype(BF16)
+    out_ref = target_ref
+    if out_refs:
+        out_ref = out_refs[0]
+        for block in range(BLOCKS):
+            out_ref[block] = target_ref[block].T.astype(BF16)
     local_ref[...] = jnp.zeros_like(local_ref)
     ahead = lax.broadcasted_iota(jnp.int32, (width, width), 0) - lax.broadcasted_iota(
         jnp.int32, (width, width), 1
     )
 
-    def outer(tile, carry):
+    def outer(number, carry):
+        tile = first_tile + number
         target = jnp.concatenate([out_ref[2 * tile], out_ref[2 * tile + 1]], axis=1)
         zeros = jnp.zeros((HD, width), BF16)
         score_rhs = jnp.concatenate([target[:HD], zeros], axis=0)
@@ -158,19 +165,19 @@
             attn = (scaled * scaled).astype(BF16)
             pgrad = (scaled * products * (2.0 / HD)).astype(BF16)
             left = jnp.concatenate([src_ref[2 * source], src_ref[2 * source + 1]], axis=1)
-            local_ref[tile, :HD] += dot(left[:HD], pgrad)
-            local_ref[tile, HD:] += dot(left[HD:], attn)
+            local_ref[number, :HD] += dot(left[:HD], pgrad)
+            local_ref[number, HD:] += dot(left[HD:], attn)
             return carry
 
         first = jnp.where(core == 0, 0, tile)
-        last = jnp.where(core == 0, tile + 1, tiles)
+        last = jnp.where(core == 0, tile + 1, BLOCKS // 2)
         lax.fori_loop(first, last, inner, 0)
         return carry
 
     lax.fori_loop(0, tiles, outer, 0)
 
 
-def scan_body(parts_ref, sums_ref):
+def scan_body(parts_ref, unused_ref, sums_ref):
     core = lax.axis_index("core")
     count = parts_ref.shape[0]
 
@@ -182,18 +189,14 @@
     lax.fori_loop(0, count, step, jnp.zeros(parts_ref.shape[1:], F32))
 
 
-def grads_body(state_ref, out_ref, local_ref, grads_ref, rows_ref, cols_ref, wide_ref, feats_ref):
-    keyed = lax.axis_index("core") == 1
+def grads_body(state_ref, out_ref, early_ref, late_ref, grads_ref, rows_ref, cols_ref, wide_ref, feats_ref):
     rows_ref[...] = state_ref[...].astype(BF16)
-
-    @pl.when(keyed)
-    def turn():
-        for start in range(0, HALF, TB):
-            stop = min(start + TB, HALF)
-            part = state_ref[start:stop, :]
-            if stop - start < TB:
-                part = jnp.concatenate([part, jnp.zeros((TB - stop + start, TB), F32)], axis=0)
-            cols_ref[:, start:stop] = part.T[:, : stop - start].astype(BF16)
+    for start in range(0, HALF, TB):
+        stop = min(start + TB, HALF)
+        part = state_ref[start:stop, :]
+        if stop - start < TB:
+            part = jnp.concatenate([part, jnp.zeros((TB - stop + start, TB), F32)], axis=0)
+        cols_ref[:, start:stop] = part.T[:, : stop - start].astype(BF16)
 
     def step(tile, carry):
         target = jnp.concatenate([out_ref[2 * tile], out_ref[2 * tile + 1]], axis=1)
@@ -201,31 +204,20 @@
         zeros = jnp.zeros((HD, 2 * TB), BF16)
         wide_ref[:HALF] = dot(rows_ref[...], jnp.concatenate([target[HD:], zeros], axis=0))
         wide_ref[HALF:] = dot(rows_ref[...], jnp.concatenate([zeros, target[HD:]], axis=0))
-        result = local_ref[tile, :HD] + chain_back(xt, wide_ref) * (2.0 / (HD * HD))
-        grads_ref[2 * tile, :, :HD] = result[:, :TB].T
-        grads_ref[2 * tile + 1, :, :HD] = result[:, TB:].T
-
-        @pl.when(keyed)
-        def value_part():
-            write_features(xt, 2.0, feats_ref)
-            values = dot(cols_ref[:HD, :], feats_ref[:HALF]) + dot(
-                cols_ref[HD:, :], feats_ref[HALF:]
-            )
-            total = local_ref[tile, HD:] + values * (1.0 / (HD * HD))
-            grads_ref[2 * tile, :, HD:] = total[:, :TB].T
-            grads_ref[2 * tile + 1, :, HD:] = total[:, TB:].T
-
-        @pl.when(jnp.logical_not(keyed))
-        def no_values():
-            grads_ref[2 * tile, :, HD:] = jnp.zeros((TB, HD), F32)
-            grads_ref[2 * tile + 1, :, HD:] = jnp.zeros((TB, HD), F32)
-
+        write_features(xt, 2.0, feats_ref)
+        values = dot(cols_ref[:HD, :], feats_ref[:HALF]) + dot(cols_ref[HD:, :], feats_ref[HALF:])
+        local = jnp.where(tile < 2, early_ref[tile % 2], late_ref[tile % 2])
+        result = local + jnp.concatenate(
+            [chain_back(xt, wide_ref) * (2.0 / (HD * HD)), values * (1.0 / (HD * HD))], axis=0
+        )
+        grads_ref[2 * tile] = result[:, :TB].T
+        grads_ref[2 * tile + 1] = result[:, TB:].T
         return carry
 
     lax.fori_loop(0, BLOCKS // 2, step, 0)
 
 
-def project_body(grads_ref, wq_ref, wk_ref, wv_ref, out_ref):
+def project_body(grads_ref, unused_ref, wq_ref, wk_ref, wv_ref, out_ref):
     query = jnp.concatenate([grads_ref[2 * h][:, :HD] for h in range(CHIPS)], axis=1)
     key = jnp.concatenate([grads_ref[2 * h + 1][:, :HD] for h in range(CHIPS)], axis=1)
     value = jnp.concatenate([grads_ref[2 * h + 1][:, HD:] for h in range(CHIPS)], axis=1)
@@ -236,6 +228,13 @@
         out_ref[place] = (
             dot(query, wq_ref[:, cols]) + dot(key, wk_ref[:, cols]) + dot(value, wv_ref[:, cols])
         )
+
+
+def finish_body(pieces_ref, unused_ref, out_ref):
+    total = pieces_ref[0]
+    for place in range(1, pieces_ref.shape[0]):
+        total = total + pieces_ref[place]
+    out_ref[...] = total.astype(BF16)
 
 
 def on_device(queries, keys, values, out_grad, w_query, w_key, w_value):
@@ -250,13 +249,16 @@
         flops=1 << 20,
         nbytes=1 << 20,
     )
+    def tick(value, name):
+        return call(tick_body, shape((8, TB), F32), (value,), name, flops=1 << 20, nbytes=1 << 12)
+
     source = lax.all_to_all(packed, ("zc", "core"), 0, 0, tiled=True)
     target = lax.ppermute(source, "core", [(0, 1), (1, 0)])
     blocks = shape((BLOCKS, TB, TB), BF16)
     state, tok, src = call(
         state_body,
         (shape((HALF, TB), F32), blocks, blocks),
-        (source,),
+        (source, tick(packed, "tick_in")),
         "state",
         scratch=[pltpu.VMEM((2 * HALF, 2 * TB), BF16)],
         flops=4 << 30,
@@ -265,22 +267,32 @@
     parts = lax.all_to_all(
         state.reshape(groups, 1, HALF * TB // groups), ("x", "zg"), 0, 0, tiled=True
     )
+    tiles = BLOCKS // 4
+    halves = shape((tiles, TB, 2 * TB), F32)
+    early, out = call(
+        functools.partial(local_body, tiles, 0),
+        (halves, blocks),
+        (tok, src, target),
+        "early",
+        flops=2 << 30,
+        nbytes=1 << 20,
+    )
     sums = call(
-        scan_body, shape(parts.shape, F32), (parts,), "scan", flops=1 << 20, nbytes=1 << 20
+        scan_body, shape(parts.shape, F32), (parts, early), "scan", flops=1 << 20, nbytes=1 << 20
     )
     before = lax.all_to_all(sums, ("x", "zg"), 0, 0, tiled=True).reshape(HALF, TB)
-    local, out = call(
-        local_body,
-        (shape((BLOCKS // 2, TB, 2 * TB), F32), blocks),
-        (tok, src, target),
-        "local",
-        flops=4 << 30,
+    (late,) = call(
+        functools.partial(local_body, tiles, tiles),
+        (halves,),
+        (tok, src, out),
+        "late",
+        flops=2 << 30,
         nbytes=1 << 20,
     )
     grads = call(
         grads_body,
         shape((BLOCKS, TB, TB), F32),
-        (before, out, local),
+        (before, out, early, late),
         "grads",
         scratch=[
             pltpu.VMEM((HALF, TB), BF16),
@@ -296,13 +308,20 @@
     partial_sum = call(
         project_body,
         shape((heads, TB, w_query.shape[1] // heads), F32),
-        (mine, w_query, w_key, w_value),
+        (mine, tick(grads, "tick_grads"), w_query, w_key, w_value),
         "project",
         flops=1 << 29,
         nbytes=4 << 20,
     )
     pieces = lax.all_to_all(partial_sum, "y", 0, 0, tiled=True)
-    return jnp.sum(pieces, axis=0).astype(BF16)
+    return call(
+        finish_body,
+        shape(pieces.shape[1:], BF16),
+        (pieces, tick(partial_sum, "tick_out")),
+        "finish",
+        flops=1 << 20,
+        nbytes=1 << 20,
+    )
 
 
 def solution(mesh):

time: 152 us -> 157 us (1.033)
  blocking collectives: 104 us -> 0 us
  waiting for transfers between devices: 22.9 us -> 91.2 us
  starting transfers between devices: 10.1 us -> 44.2 us
  Pallas kernels: 14.1 us -> 18.2 us
    all_to_all x4 -> x0, blocking collectives: 104 us -> none  [the longest x1 41.9 us: on_device(): lax.all_to_all(state.reshape(groups, 1, HALF * TB // groups), ('x', 'zg')...]
    all_to_all x0 -> x4, waiting for transfers between devices: none -> 62.1 us  [the longest x1 21.8 us: on_device(): lax.all_to_all(state.reshape(groups, 1, HALF * TB // groups), ('x', 'zg')...]
    all_to_all x0 -> x4, starting transfers between devices: none -> 33.7 us  [the longest x1 12 us: on_device(): lax.all_to_all(state.reshape(groups, 1, HALF * TB // groups), ('x', 'zg')...]
    all_to_all x1, waiting for transfers between devices: 21.4 us -> 27.6 us  [on_device(): lax.all_to_all(sums, ('x', 'zg'), 0, 0, tiled=True).reshape(HALF, TB)]
    pallas_call x6 -> x11, Pallas kernels: 14.1 us -> 18.2 us  [call(): pl.pallas_call(body, out_shape=out_shape, in_specs=[VMEM] * len(args), ou...]
  transfers between devices with their start and end apart: 2 -> 6, of which waited for: 2 -> 6; matrix products, arithmetic and copies ran while one was open for 0% -> 0% of each run, Pallas kernels for 2% -> 4%
where the time goes in v4:
time: 157 us; the launch traced here: 155 us
  waiting for transfers between devices  91.2 us (58%)
  starting transfers between devices  44.2 us (28%)
  Pallas kernels  18.2 us (12%)
    all_to_all x1, waiting for transfers between devices, on_device(): lax.all_to_all(sums, ('x', 'zg'), 0, 0, tiled=True).reshape(HALF, TB)  27.6 us
    all_to_all x1, waiting for transfers between devices, on_device(): lax.all_to_all(state.reshape(groups, 1, HALF * TB // groups), ('x', 'zg')...  21.8 us
    pallas_call x11, Pallas kernels, call(): pl.pallas_call(body, out_shape=out_shape, in_specs=[VMEM] * len(args), ou...  18.2 us
    all_to_all x1, waiting for transfers between devices, on_device(): source = lax.all_to_all(packed, ('zc', 'core'), 0, 0, tiled=True)  14.4 us
    all_to_all x1, waiting for transfers between devices, on_device(): mine = lax.all_to_all(grads, ('zc', 'core'), 0, 0, tiled=True)  13.3 us
    all_to_all x1, waiting for transfers between devices, on_device(): pieces = lax.all_to_all(partial_sum, 'y', 0, 0, tiled=True)  12.7 us
    all_to_all x1, starting transfers between devices, on_device(): lax.all_to_all(state.reshape(groups, 1, HALF * TB // groups), ('x', 'zg')...  12 us
    all_to_all x1, starting transfers between devices, on_device(): source = lax.all_to_all(packed, ('zc', 'core'), 0, 0, tiled=True)  10.4 us
  transfers between devices with their start and end apart: 6, of which 6 were waited for; matrix products, arithmetic and copies ran while one was open for 0% of the time, Pallas kernels for 4%

profile of v4, /device:TPU:1, one launch (start us, length us, event | category | flops | bytes accessed | tf_op | source)
XLA Modules:
  0.0 155.0 jit_solution(11093013740797916731)
XLA Ops:
  0.0 1.9 %pack.1.unused_ref = f32[8,128,128]{2,1,0:T(8,128)} custom-call(bf16[128,256]{1,0:T(8,128)(2,1)} %q_ref.1, bf16[128,256]{1,0:T(8,128)(2,1)} %k_ref.1, bf16[128,256]{1,0:T(8,128)(2,1)} %v_ref.1, bf16[128,256]{1,0:T(8,128)(2,1)} %g_ref.1), custom_call_target="tpu_custom_call" | custom-call | flops 1048576 | bytes 1048576 | tf_op jit(solution)/shard_map/pack/pallas_call | solution.py:39
  1.9 0.0 copy-start
  1.9 10.4 %all-to-all-start = ((f32[8,128,128]{2,1,0:T(8,128)}), f32[8,128,128]{2,1,0:T(8,128)S(1)}, u32[]{:S(2)}, u32[]{:S(2)}) async-start(f32[8,128,128]{2,1,0:T(8,128)} %pack.1.unused_ref), calls=%async_computation | async-start | bytes 1048576 | tf_op jit(solution)/shard_map/all_to_all | solution.py:255
  12.2 0.0 copy-done
  12.2 14.4 %all-to-all-done.source_ref = f32[8,128,128]{2,1,0:T(8,128)S(1)} async-done(((f32[8,128,128]{2,1,0:T(8,128)}), f32[8,128,128]{2,1,0:T(8,128)S(1)}, u32[]{:S(2)}, u32[]{:S(2)}) %all-to-all-start) | async-done | bytes 524320 | tf_op jit(solution)/shard_map/all_to_all | solution.py:255
  26.6 2.9 %state.1 = (f32[1040,128]{1,0:T(8,128)}, bf16[8,128,128]{2,1,0:T(8,128)(2,1)S(1)}, bf16[8,128,128]{2,1,0:T(8,128)(2,1)S(1)}) custom-call(f32[8,128,128]{2,1,0:T(8,128)S(1)} %all-to-all-done.source_ref, f32[8,128]{1,0:T(8,128)S(1)} %tick_in.1.unused_ref), custom_call_target="tpu_custom_call" | custom-call | flops 4294967296 | bytes 3145728 | tf_op jit(solution)/shard_map/state/pallas_call | solution.py:39
  29.6 12.0 %all-to-all-start.1 = ((f32[16,1,8320]{2,1,0:T(1,128)}), f32[16,1,8320]{2,1,0:T(1,128)S(1)}, u32[]{:S(2)}, u32[]{:S(2)}) async-start(f32[16,1,8320]{2,1,0:T(1,128)} %bitcast), calls=%async_computation.1 | async-start | bytes 1064960 | tf_op jit(solution)/shard_map/all_to_all | solution.py:267
  41.6 3.2 %collective-permute-start = (f32[8,128,128]{2,1,0:T(8,128)S(1)}, f32[8,128,128]{2,1,0:T(8,128)S(1)}, u32[]{:S(2)}, u32[]{:S(2)}) collective-permute-start(f32[8,128,128]{2,1,0:T(8,128)S(1)} %all-to-all-done.source_ref), channel_id=1, source_target_pairs={{0,4},{4,0},{1,5},{5,1},{2,6},{6,2},{3,7},{7,3},{8,12},{12,8},{9,1... | collective-permute-start | bytes 1572872 | tf_op jit(solution)/shard_map/ppermute | solution.py:256
  44.8 1.5 collective-permute-done.target_ref
  46.3 2.6 %early.1 = (f32[2,128,256]{2,1,0:T(8,128)S(1)}, bf16[8,128,128]{2,1,0:T(8,128)(2,1)S(1)}) custom-call(bf16[8,128,128]{2,1,0:T(8,128)(2,1)S(1)} %get-tuple-element.11.tok_ref, bf16[8,128,128]{2,1,0:T(8,128)(2,1)S(1)} %get-tuple-element.12.src_ref, f32[8,128,128]{2,1,0:T(8,128)S(1)} %collective-permute-done.target_ref), custom_call_target="tpu_custom_call" | custom-call | flops 2147483648 | bytes 1048576 | tf_op jit(solution)/shard_map/early/pallas_call | solution.py:39
  48.9 21.8 %all-to-all-done.1.parts_ref = f32[16,1,8320]{2,1,0:T(1,128)S(1)} async-done(((f32[16,1,8320]{2,1,0:T(1,128)}), f32[16,1,8320]{2,1,0:T(1,128)S(1)}, u32[]{:S(2)}, u32[]{:S(2)}) %all-to-all-start.1) | async-done | bytes 532512 | tf_op jit(solution)/shard_map/all_to_all | solution.py:267
  70.6 0.9 scan.1
  71.6 7.3 %all-to-all-start.2 = ((f32[16,1,8320]{2,1,0:T(1,128)}), f32[16,1,8320]{2,1,0:T(1,128)S(1)}, u32[]{:S(2)}, u32[]{:S(2)}) async-start(f32[16,1,8320]{2,1,0:T(1,128)} %scan.1), calls=%async_computation.2 | async-start | bytes 1064960 | tf_op jit(solution)/shard_map/all_to_all | solution.py:283
  78.9 1.1 late.1.late_ref
  80.0 27.6 %all-to-all-done.2 = f32[16,1,8320]{2,1,0:T(1,128)S(1)} async-done(((f32[16,1,8320]{2,1,0:T(1,128)}), f32[16,1,8320]{2,1,0:T(1,128)S(1)}, u32[]{:S(2)}, u32[]{:S(2)}) %all-to-all-start.2) | async-done | bytes 532512 | tf_op jit(solution)/shard_map/all_to_all | solution.py:283
  107.6 0.0 copy-start.2
  107.6 4.2 %grads.1.unused_ref = f32[8,128,128]{2,1,0:T(8,128)} custom-call(f32[1040,128]{1,0:T(8,128)S(1)} %bitcast.2, bf16[8,128,128]{2,1,0:T(8,128)(2,1)S(1)} %get-tuple-element.14.target_ref.out_ref, f32[2,128,256]{2,1,0:T(8,128)S(1)} %get-tuple-element.13.unused_ref.early_ref, f32[2,128,256]{2,1,0:T(8,128)S(1)} %late.1.late_ref), custom_call_target="tpu_custom_call" | custom-call | flops 4294967296 | bytes 3145728 | tf_op jit(solution)/shard_map/grads/pallas_call | solution.py:39
  111.8 0.0 copy-start.1
  111.8 7.2 %all-to-all-start.3 = ((f32[8,128,128]{2,1,0:T(8,128)}), f32[8,128,128]{2,1,0:T(8,128)S(1)}, u32[]{:S(2)}, u32[]{:S(2)}) async-start(f32[8,128,128]{2,1,0:T(8,128)} %grads.1.unused_ref), calls=%async_computation.3 | async-start | bytes 1048576 | tf_op jit(solution)/shard_map/all_to_all | solution.py:306
  119.0 1.1 tick_grads.1.unused_ref
  120.1 13.3 %all-to-all-done.3.grads_ref = f32[8,128,128]{2,1,0:T(8,128)S(1)} async-done(((f32[8,128,128]{2,1,0:T(8,128)}), f32[8,128,128]{2,1,0:T(8,128)S(1)}, u32[]{:S(2)}, u32[]{:S(2)}) %all-to-all-start.3) | async-done | bytes 524320 | tf_op jit(solution)/shard_map/all_to_all | solution.py:306
  133.3 0.0 copy-done.2
  133.3 0.0 copy-done.1
  133.3 0.0 copy-start.3
  133.3 1.2 copy-done.3
  134.6 1.6 %project.1.unused_ref = f32[4,128,512]{2,1,0:T(8,128)} custom-call(f32[8,128,128]{2,1,0:T(8,128)S(1)} %all-to-all-done.3.grads_ref, f32[8,128]{1,0:T(8,128)S(1)} %tick_grads.1.unused_ref, bf16[256,2048]{1,0:T(8,128)(2,1)S(1)} %copy-done.1, bf16[256,2048]{1,0:T(8,128)(2,1)S(1)} %copy-done.2, bf16[256,2048]{1,0:T(8,128)(2,1)S(1)} %copy-done.3), custom_call_target="tpu_custom_call" | custom-call | flops 536870912 | bytes 4194304 | tf_op jit(solution)/shard_map/project/pallas_call | solution.py:39
  136.2 4.2 %all-to-all-start.4 = ((f32[4,128,512]{2,1,0:T(8,128)}), f32[4,128,512]{2,1,0:T(8,128)S(1)}, u32[]{:S(2)}, u32[]{:S(2)}) async-start(f32[4,128,512]{2,1,0:T(8,128)} %project.1.unused_ref), calls=%async_computation.4 | async-start | bytes 2097152 | tf_op jit(solution)/shard_map/all_to_all | solution.py:316
  140.3 1.3 tick_out.1.unused_ref
  141.6 12.7 %all-to-all-done.4.pieces_ref = f32[4,128,512]{2,1,0:T(8,128)S(1)} async-done(((f32[4,128,512]{2,1,0:T(8,128)}), f32[4,128,512]{2,1,0:T(8,128)S(1)}, u32[]{:S(2)}, u32[]{:S(2)}) %all-to-all-start.4) | async-done | bytes 1048608 | tf_op jit(solution)/shard_map/all_to_all | solution.py:316
  154.3 0.7 finish.1
  (1 shorter events, 0.0 us)
Async XLA Ops:
  1.9 10.4 %copy-start = (f32[8,128,128]{2,1,0:T(8,128)S(1)}, f32[8,128,128]{2,1,0:T(8,128)}, u32[]{:S(2)}) copy-start(f32[8,128,128]{2,1,0:T(8,128)} %pack.1.unused_ref) | copy-start | bytes 1572868
  1.9 24.8 %all-to-all-start = ((f32[8,128,128]{2,1,0:T(8,128)}), f32[8,128,128]{2,1,0:T(8,128)S(1)}, u32[]{:S(2)}, u32[]{:S(2)}) async-start(f32[8,128,128]{2,1,0:T(8,128)} %pack.1.unused_ref), calls=%async_computation | async-start | bytes 1048576 | tf_op jit(solution)/shard_map/all_to_all | solution.py:255
  29.6 41.1 %all-to-all-start.1 = ((f32[16,1,8320]{2,1,0:T(1,128)}), f32[16,1,8320]{2,1,0:T(1,128)S(1)}, u32[]{:S(2)}, u32[]{:S(2)}) async-start(f32[16,1,8320]{2,1,0:T(1,128)} %bitcast), calls=%async_computation.1 | async-start | bytes 1064960 | tf_op jit(solution)/shard_map/all_to_all | solution.py:267
  41.6 4.7 %collective-permute-start = (f32[8,128,128]{2,1,0:T(8,128)S(1)}, f32[8,128,128]{2,1,0:T(8,128)S(1)}, u32[]{:S(2)}, u32[]{:S(2)}) collective-permute-start(f32[8,128,128]{2,1,0:T(8,128)S(1)} %all-to-all-done.source_ref), channel_id=1, source_target_pairs={{0,4},{4,0},{1,5},{5,1},{2,6},{6,2},{3,7},{7,3},{8,12},{12,8},{9,1... | collective-permute-start | bytes 1572872 | tf_op jit(solution)/shard_map/ppermute | solution.py:256
  71.6 36.1 %all-to-all-start.2 = ((f32[16,1,8320]{2,1,0:T(1,128)}), f32[16,1,8320]{2,1,0:T(1,128)S(1)}, u32[]{:S(2)}, u32[]{:S(2)}) async-start(f32[16,1,8320]{2,1,0:T(1,128)} %scan.1), calls=%async_computation.2 | async-start | bytes 1064960 | tf_op jit(solution)/shard_map/all_to_all | solution.py:283
  107.6 25.7 %copy-start.2 = (bf16[256,2048]{1,0:T(8,128)(2,1)S(1)}, bf16[256,2048]{1,0:T(8,128)(2,1)}, u32[]{:S(2)}) copy-start(bf16[256,2048]{1,0:T(8,128)(2,1)} %wk_ref.1) | copy-start | bytes 3145732
  111.8 21.5 %copy-start.1 = (bf16[256,2048]{1,0:T(8,128)(2,1)S(1)}, bf16[256,2048]{1,0:T(8,128)(2,1)}, u32[]{:S(2)}) copy-start(bf16[256,2048]{1,0:T(8,128)(2,1)} %wq_ref.1) | copy-start | bytes 3145732
  111.8 21.5 %all-to-all-start.3 = ((f32[8,128,128]{2,1,0:T(8,128)}), f32[8,128,128]{2,1,0:T(8,128)S(1)}, u32[]{:S(2)}, u32[]{:S(2)}) async-start(f32[8,128,128]{2,1,0:T(8,128)} %grads.1.unused_ref), calls=%async_computation.3 | async-start | bytes 1048576 | tf_op jit(solution)/shard_map/all_to_all | solution.py:306
  133.3 1.2 copy-start.3
  136.2 18.1 %all-to-all-start.4 = ((f32[4,128,512]{2,1,0:T(8,128)}), f32[4,128,512]{2,1,0:T(8,128)S(1)}, u32[]{:S(2)}, u32[]{:S(2)}) async-start(f32[4,128,512]{2,1,0:T(8,128)} %project.1.unused_ref), calls=%async_computation.4 | async-start | bytes 2097152 | tf_op jit(solution)/shard_map/all_to_all | solution.py:316

commit v5 on v4

--- a/solution.py
+++ b/solution.py
@@ -110,7 +110,7 @@
     return jnp.concatenate(sums, axis=0)
 
 
-def state_body(source_ref, unused_ref, state_ref, tok_ref, src_ref, feats_ref):
+def state_body(source_ref, state_ref, tok_ref, src_ref, feats_ref):
     for block in range(BLOCKS):
         source = source_ref[block]
         tok_ref[block] = source.astype(BF16)
@@ -129,10 +129,6 @@
         return carry
 
     lax.fori_loop(0, BLOCKS // 2, step, 0)
-
-
-def tick_body(unused_ref, tick_ref):
-    tick_ref[...] = jnp.zeros_like(tick_ref)
 
 
 def local_body(tiles, first_tile, tok_ref, src_ref, target_ref, local_ref, *out_refs):
@@ -217,7 +213,7 @@
     lax.fori_loop(0, BLOCKS // 2, step, 0)
 
 
-def project_body(grads_ref, unused_ref, wq_ref, wk_ref, wv_ref, out_ref):
+def project_body(grads_ref, wq_ref, wk_ref, wv_ref, out_ref):
     query = jnp.concatenate([grads_ref[2 * h][:, :HD] for h in range(CHIPS)], axis=1)
     key = jnp.concatenate([grads_ref[2 * h + 1][:, :HD] for h in range(CHIPS)], axis=1)
     value = jnp.concatenate([grads_ref[2 * h + 1][:, HD:] for h in range(CHIPS)], axis=1)
@@ -228,13 +224,6 @@
         out_ref[place] = (
             dot(query, wq_ref[:, cols]) + dot(key, wk_ref[:, cols]) + dot(value, wv_ref[:, cols])
         )
-
-
-def finish_body(pieces_ref, unused_ref, out_ref):
-    total = pieces_ref[0]
-    for place in range(1, pieces_ref.shape[0]):
-        total = total + pieces_ref[place]
-    out_ref[...] = total.astype(BF16)
 
 
 def on_device(queries, keys, values, out_grad, w_query, w_key, w_value):
@@ -249,16 +238,13 @@
         flops=1 << 20,
         nbytes=1 << 20,
     )
-    def tick(value, name):
-        return call(tick_body, shape((8, TB), F32), (value,), name, flops=1 << 20, nbytes=1 << 12)
-
     source = lax.all_to_all(packed, ("zc", "core"), 0, 0, tiled=True)
     target = lax.ppermute(source, "core", [(0, 1), (1, 0)])
     blocks = shape((BLOCKS, TB, TB), BF16)
     state, tok, src = call(
         state_body,
         (shape((HALF, TB), F32), blocks, blocks),
-        (source, tick(packed, "tick_in")),
+        (source,),
         "state",
         scratch=[pltpu.VMEM((2 * HALF, 2 * TB), BF16)],
         flops=4 << 30,
@@ -308,20 +294,13 @@
     partial_sum = call(
         project_body,
         shape((heads, TB, w_query.shape[1] // heads), F32),
-        (mine, tick(grads, "tick_grads"), w_query, w_key, w_value),
+        (mine, w_query, w_key, w_value),
         "project",
         flops=1 << 29,
         nbytes=4 << 20,
     )
     pieces = lax.all_to_all(partial_sum, "y", 0, 0, tiled=True)
-    return call(
-        finish_body,
-        shape(pieces.shape[1:], BF16),
-        (pieces, tick(partial_sum, "tick_out")),
-        "finish",
-        flops=1 << 20,
-        nbytes=1 << 20,
-    )
+    return jnp.sum(pieces, axis=0).astype(BF16)
 
 
 def solution(mesh):

time: 157 us -> 154 us (0.981)
  blocking collectives: 0 us -> 62.7 us
  waiting for transfers between devices: 91.2 us -> 51.6 us
  starting transfers between devices: 44.2 us -> 23.3 us
  Pallas kernels: 18.2 us -> 13.4 us
    all_to_all x0 -> x3, blocking collectives: none -> 62.7 us  [the longest x1 24.5 us: on_device(): source = lax.all_to_all(packed, ('zc', 'core'), 0, 0, tiled=True)]
    all_to_all x3 -> x0, waiting for transfers between devices: 40.4 us -> none  [the longest x1 14.4 us: on_device(): source = lax.all_to_all(packed, ('zc', 'core'), 0, 0, tiled=True)]
    all_to_all x3 -> x0, starting transfers between devices: 21.7 us -> none  [the longest x1 10.4 us: on_device(): source = lax.all_to_all(packed, ('zc', 'core'), 0, 0, tiled=True)]
    pallas_call x11 -> x7, Pallas kernels: 18.2 us -> 13.4 us  [call(): pl.pallas_call(body, out_shape=out_shape, in_specs=[VMEM] * len(args), ou...]
  transfers between devices with their start and end apart: 6 -> 3, of which waited for: 6 -> 3; matrix products, arithmetic and copies ran while one was open for 0% -> 0% of each run, Pallas kernels for 4% -> 2%
where the time goes in v5:
time: 154 us; the launch traced here: 152 us
  blocking collectives  62.7 us (41%)
  waiting for transfers between devices  51.6 us (34%)
  starting transfers between devices  23.3 us (15%)
  Pallas kernels  13.4 us (9%)
    all_to_all x1, waiting for transfers between devices, on_device(): lax.all_to_all(sums, ('x', 'zg'), 0, 0, tiled=True).reshape(HALF, TB)  28.6 us
    all_to_all x1, blocking collectives, on_device(): source = lax.all_to_all(packed, ('zc', 'core'), 0, 0, tiled=True)  24.5 us
    all_to_all x1, waiting for transfers between devices, on_device(): lax.all_to_all(state.reshape(groups, 1, HALF * TB // groups), ('x', 'zg')...  21.5 us
    all_to_all x1, blocking collectives, on_device(): mine = lax.all_to_all(grads, ('zc', 'core'), 0, 0, tiled=True)  20.4 us
    all_to_all x1, blocking collectives, on_device(): pieces = lax.all_to_all(partial_sum, 'y', 0, 0, tiled=True)  17.8 us
    pallas_call x7, Pallas kernels, call(): pl.pallas_call(body, out_shape=out_shape, in_specs=[VMEM] * len(args), ou...  13.4 us
    all_to_all x1, starting transfers between devices, on_device(): lax.all_to_all(state.reshape(groups, 1, HALF * TB // groups), ('x', 'zg')...  12 us
    all_to_all x1, starting transfers between devices, on_device(): lax.all_to_all(sums, ('x', 'zg'), 0, 0, tiled=True).reshape(HALF, TB)  8 us
  transfers between devices with their start and end apart: 3, of which 3 were waited for; matrix products, arithmetic and copies ran while one was open for 0% of the time, Pallas kernels for 2%

profile of v5, /device:TPU:1, one launch (start us, length us, event | category | flops | bytes accessed | tf_op | source)
XLA Modules:
  0.0 151.7 jit_solution(2013823278827210753)
XLA Ops:
  0.0 1.9 %pack.1 = f32[8,128,128]{2,1,0:T(8,128)} custom-call(bf16[128,256]{1,0:T(8,128)(2,1)} %q_ref.1, bf16[128,256]{1,0:T(8,128)(2,1)} %k_ref.1, bf16[128,256]{1,0:T(8,128)(2,1)} %v_ref.1, bf16[128,256]{1,0:T(8,128)(2,1)} %g_ref.1), custom_call_target="tpu_custom_call" | custom-call | flops 1048576 | bytes 1048576 | tf_op jit(solution)/shard_map/pack/pallas_call | solution.py:39
  1.9 24.5 %all_to_all.25.source_ref = f32[8,128,128]{2,1,0:T(8,128)S(1)} all-to-all(f32[8,128,128]{2,1,0:T(8,128)} %pack.1), channel_id=1, replica_groups=mesh['x'=4,'zg'=4,'zc'=4,'core'=2,'y'=4] {'zc','core'}, dimensions={0} | all-to-all | bytes 1048576 | tf_op jit(solution)/shard_map/all_to_all | solution.py:241
  26.4 2.9 %state.1 = (f32[1040,128]{1,0:T(8,128)}, bf16[8,128,128]{2,1,0:T(8,128)(2,1)S(1)}, bf16[8,128,128]{2,1,0:T(8,128)(2,1)S(1)}) custom-call(f32[8,128,128]{2,1,0:T(8,128)S(1)} %all_to_all.25.source_ref), custom_call_target="tpu_custom_call" | custom-call | flops 4294967296 | bytes 3145728 | tf_op jit(solution)/shard_map/state/pallas_call | solution.py:39
  29.3 12.0 %all-to-all-start.1 = ((f32[16,1,8320]{2,1,0:T(1,128)}), f32[16,1,8320]{2,1,0:T(1,128)S(1)}, u32[]{:S(2)}, u32[]{:S(2)}) async-start(f32[16,1,8320]{2,1,0:T(1,128)} %bitcast), calls=%async_computation.1 | async-start | bytes 1064960 | tf_op jit(solution)/shard_map/all_to_all | solution.py:253
  41.3 3.2 %collective-permute-start = (f32[8,128,128]{2,1,0:T(8,128)S(1)}, f32[8,128,128]{2,1,0:T(8,128)S(1)}, u32[]{:S(2)}, u32[]{:S(2)}) collective-permute-start(f32[8,128,128]{2,1,0:T(8,128)S(1)} %all_to_all.25.source_ref), channel_id=1, source_target_pairs={{0,4},{4,0},{1,5},{5,1},{2,6},{6,2},{3,7},{7,3},{8,12},{12,8},{9,1... | collective-permute-start | bytes 1572872 | tf_op jit(solution)/shard_map/ppermute | solution.py:242
  44.6 1.5 collective-permute-done.target_ref
  46.1 2.6 %early.1 = (f32[2,128,256]{2,1,0:T(8,128)S(1)}, bf16[8,128,128]{2,1,0:T(8,128)(2,1)S(1)}) custom-call(bf16[8,128,128]{2,1,0:T(8,128)(2,1)S(1)} %get-tuple-element.11.tok_ref, bf16[8,128,128]{2,1,0:T(8,128)(2,1)S(1)} %get-tuple-element.12.src_ref, f32[8,128,128]{2,1,0:T(8,128)S(1)} %collective-permute-done.target_ref), custom_call_target="tpu_custom_call" | custom-call | flops 2147483648 | bytes 1048576 | tf_op jit(solution)/shard_map/early/pallas_call | solution.py:39
  48.7 21.5 %all-to-all-done.1.parts_ref = f32[16,1,8320]{2,1,0:T(1,128)S(1)} async-done(((f32[16,1,8320]{2,1,0:T(1,128)}), f32[16,1,8320]{2,1,0:T(1,128)S(1)}, u32[]{:S(2)}, u32[]{:S(2)}) %all-to-all-start.1) | async-done | bytes 532512 | tf_op jit(solution)/shard_map/all_to_all | solution.py:253
  70.2 0.9 scan.1
  71.1 8.0 %all-to-all-start.2 = ((f32[16,1,8320]{2,1,0:T(1,128)}), f32[16,1,8320]{2,1,0:T(1,128)S(1)}, u32[]{:S(2)}, u32[]{:S(2)}) async-start(f32[16,1,8320]{2,1,0:T(1,128)} %scan.1), calls=%async_computation.2 | async-start | bytes 1064960 | tf_op jit(solution)/shard_map/all_to_all | solution.py:269
  79.1 1.1 late.1.late_ref
  80.2 28.6 %all-to-all-done.2 = f32[16,1,8320]{2,1,0:T(1,128)S(1)} async-done(((f32[16,1,8320]{2,1,0:T(1,128)}), f32[16,1,8320]{2,1,0:T(1,128)S(1)}, u32[]{:S(2)}, u32[]{:S(2)}) %all-to-all-start.2) | async-done | bytes 532512 | tf_op jit(solution)/shard_map/all_to_all | solution.py:269
  108.8 0.0 copy-start.1
  108.8 0.0 copy-start.2
  108.8 3.4 %grads.1 = f32[8,128,128]{2,1,0:T(8,128)S(1)} custom-call(f32[1040,128]{1,0:T(8,128)S(1)} %bitcast.2, bf16[8,128,128]{2,1,0:T(8,128)(2,1)S(1)} %get-tuple-element.14.target_ref.out_ref, f32[2,128,256]{2,1,0:T(8,128)S(1)} %get-tuple-element.13.unused_ref.early_ref, f32[2,128,256]{2,1,0:T(8,128)S(1)} %late.1.late_ref), custom_call_target="tpu_custom_call" | custom-call | flops 4294967296 | bytes 3145728 | tf_op jit(solution)/shard_map/grads/pallas_call | solution.py:39
  112.2 0.0 copy-start
  112.2 20.4 %all_to_all.26.grads_ref = f32[8,128,128]{2,1,0:T(8,128)S(1)} all-to-all(f32[8,128,128]{2,1,0:T(8,128)S(1)} %grads.1), channel_id=1, replica_groups=mesh['x'=4,'zg'=4,'zc'=4,'core'=2,'y'=4] {'zc','core'}, dimensions={0} | all-to-all | bytes 1048576 | tf_op jit(solution)/shard_map/all_to_all | solution.py:292
  132.6 0.0 copy-done.1
  132.6 0.0 copy-done.2
  132.6 0.0 copy-done
  132.6 0.6 project.1
  133.2 17.8 %all_to_all.27 = f32[4,128,512]{2,1,0:T(8,128)S(1)} all-to-all(f32[4,128,512]{2,1,0:T(8,128)S(1)} %project.1), channel_id=1, replica_groups=mesh['x'=4,'zg'=4,'zc'=4,'core'=2,'y'=4] {'y'}, dimensions={0} | all-to-all | bytes 2097152 | tf_op jit(solution)/shard_map/all_to_all | solution.py:302
  151.0 0.8 reduce_sum.9
Async XLA Ops:
  29.3 40.9 %all-to-all-start.1 = ((f32[16,1,8320]{2,1,0:T(1,128)}), f32[16,1,8320]{2,1,0:T(1,128)S(1)}, u32[]{:S(2)}, u32[]{:S(2)}) async-start(f32[16,1,8320]{2,1,0:T(1,128)} %bitcast), calls=%async_computation.1 | async-start | bytes 1064960 | tf_op jit(solution)/shard_map/all_to_all | solution.py:253
  41.3 4.7 %collective-permute-start = (f32[8,128,128]{2,1,0:T(8,128)S(1)}, f32[8,128,128]{2,1,0:T(8,128)S(1)}, u32[]{:S(2)}, u32[]{:S(2)}) collective-permute-start(f32[8,128,128]{2,1,0:T(8,128)S(1)} %all_to_all.25.source_ref), channel_id=1, source_target_pairs={{0,4},{4,0},{1,5},{5,1},{2,6},{6,2},{3,7},{7,3},{8,12},{12,8},{9,1... | collective-permute-start | bytes 1572872 | tf_op jit(solution)/shard_map/ppermute | solution.py:242
  71.1 37.7 %all-to-all-start.2 = ((f32[16,1,8320]{2,1,0:T(1,128)}), f32[16,1,8320]{2,1,0:T(1,128)S(1)}, u32[]{:S(2)}, u32[]{:S(2)}) async-start(f32[16,1,8320]{2,1,0:T(1,128)} %scan.1), calls=%async_computation.2 | async-start | bytes 1064960 | tf_op jit(solution)/shard_map/all_to_all | solution.py:269
  108.8 23.8 %copy-start.1 = (bf16[256,2048]{1,0:T(8,128)(2,1)S(1)}, bf16[256,2048]{1,0:T(8,128)(2,1)}, u32[]{:S(2)}) copy-start(bf16[256,2048]{1,0:T(8,128)(2,1)} %wk_ref.1) | copy-start | bytes 3145732
  108.8 23.8 %copy-start.2 = (bf16[256,2048]{1,0:T(8,128)(2,1)S(1)}, bf16[256,2048]{1,0:T(8,128)(2,1)}, u32[]{:S(2)}) copy-start(bf16[256,2048]{1,0:T(8,128)(2,1)} %wv_ref.1) | copy-start | bytes 3145732
  112.2 20.4 %copy-start = (bf16[256,2048]{1,0:T(8,128)(2,1)S(1)}, bf16[256,2048]{1,0:T(8,128)(2,1)}, u32[]{:S(2)}) copy-start(bf16[256,2048]{1,0:T(8,128)(2,1)} %wq_ref.1) | copy-start | bytes 3145732

commit v6 on v3

--- a/solution.py
+++ b/solution.py
@@ -110,25 +110,22 @@
     return jnp.concatenate(sums, axis=0)
 
 
-def state_body(source_ref, state_ref, tok_ref, src_ref, feats_ref):
-    for block in range(BLOCKS):
-        source = source_ref[block]
-        tok_ref[block] = source.astype(BF16)
-        src_ref[block] = source.T.astype(BF16)
-    state_ref[...] = jnp.zeros_like(state_ref)
-
-    def step(tile, carry):
+def state_body(source_ref, state_ref, tok_ref, src_ref, *feats_refs):
+    for tile in range(BLOCKS // 2):
+        feats_ref = feats_refs[tile % len(feats_refs)]
+        for block in (2 * tile, 2 * tile + 1):
+            source = source_ref[block]
+            tok_ref[block] = source.astype(BF16)
+            src_ref[block] = source.T.astype(BF16)
         xt = jnp.concatenate([src_ref[2 * tile, :HD], src_ref[2 * tile + 1, :HD]], axis=1)
         write_features(xt.astype(F32), 1.0, feats_ref)
         tok = jnp.concatenate([tok_ref[2 * tile], tok_ref[2 * tile + 1]], axis=0)
         values = tok[:, HD:]
         zeros = jnp.zeros_like(values)
-        state_ref[...] += dot(
-            feats_ref[:HALF, :], jnp.concatenate([values, zeros], axis=1)
-        ) + dot(feats_ref[HALF:, :], jnp.concatenate([zeros, values], axis=1))
-        return carry
-
-    lax.fori_loop(0, BLOCKS // 2, step, 0)
+        part = dot(feats_ref[:HALF, :], jnp.concatenate([values, zeros], axis=1)) + dot(
+            feats_ref[HALF:, :], jnp.concatenate([zeros, values], axis=1)
+        )
+        state_ref[...] = part if tile == 0 else state_ref[...] + part
 
 
 def local_body(tok_ref, src_ref, target_ref, local_ref, out_ref):
@@ -182,47 +179,29 @@
     lax.fori_loop(0, count, step, jnp.zeros(parts_ref.shape[1:], F32))
 
 
-def grads_body(state_ref, out_ref, local_ref, grads_ref, rows_ref, cols_ref, wide_ref, feats_ref):
-    keyed = lax.axis_index("core") == 1
+def grads_body(state_ref, out_ref, local_ref, grads_ref, rows_ref, cols_ref, *tile_refs):
     rows_ref[...] = state_ref[...].astype(BF16)
-
-    @pl.when(keyed)
-    def turn():
-        for start in range(0, HALF, TB):
-            stop = min(start + TB, HALF)
-            part = state_ref[start:stop, :]
-            if stop - start < TB:
-                part = jnp.concatenate([part, jnp.zeros((TB - stop + start, TB), F32)], axis=0)
-            cols_ref[:, start:stop] = part.T[:, : stop - start].astype(BF16)
-
-    def step(tile, carry):
+    for start in range(0, HALF, TB):
+        stop = min(start + TB, HALF)
+        part = state_ref[start:stop, :]
+        if stop - start < TB:
+            part = jnp.concatenate([part, jnp.zeros((TB - stop + start, TB), F32)], axis=0)
+        cols_ref[:, start:stop] = part.T[:, : stop - start].astype(BF16)
+    zeros = jnp.zeros((HD, 2 * TB), BF16)
+    for tile in range(BLOCKS // 2):
+        wide_ref, feats_ref = tile_refs[tile % 2], tile_refs[2 + tile % 2]
         target = jnp.concatenate([out_ref[2 * tile], out_ref[2 * tile + 1]], axis=1)
-        xt = target[:HD].astype(F32)
-        zeros = jnp.zeros((HD, 2 * TB), BF16)
         wide_ref[:HALF] = dot(rows_ref[...], jnp.concatenate([target[HD:], zeros], axis=0))
         wide_ref[HALF:] = dot(rows_ref[...], jnp.concatenate([zeros, target[HD:]], axis=0))
-        result = local_ref[tile, :HD] + chain_back(xt, wide_ref) * (2.0 / (HD * HD))
-        grads_ref[2 * tile, :, :HD] = result[:, :TB].T
-        grads_ref[2 * tile + 1, :, :HD] = result[:, TB:].T
-
-        @pl.when(keyed)
-        def value_part():
-            write_features(xt, 2.0, feats_ref)
-            values = dot(cols_ref[:HD, :], feats_ref[:HALF]) + dot(
-                cols_ref[HD:, :], feats_ref[HALF:]
-            )
-            total = local_ref[tile, HD:] + values * (1.0 / (HD * HD))
-            grads_ref[2 * tile, :, HD:] = total[:, :TB].T
-            grads_ref[2 * tile + 1, :, HD:] = total[:, TB:].T
-
-        @pl.when(jnp.logical_not(keyed))
-        def no_values():
-            grads_ref[2 * tile, :, HD:] = jnp.zeros((TB, HD), F32)
-            grads_ref[2 * tile + 1, :, HD:] = jnp.zeros((TB, HD), F32)
-
-        return carry
-
-    lax.fori_loop(0, BLOCKS // 2, step, 0)
+        xt = target[:HD].astype(F32)
+        write_features(xt, 2.0, feats_ref)
+        values = dot(cols_ref[:HD, :], feats_ref[:HALF]) + dot(cols_ref[HD:, :], feats_ref[HALF:])
+        back = chain_back(xt, wide_ref)
+        result = local_ref[tile] + jnp.concatenate(
+            [back * (2.0 / (HD * HD)), values * (1.0 / (HD * HD))], axis=0
+        )
+        grads_ref[2 * tile] = result[:, :TB].T
+        grads_ref[2 * tile + 1] = result[:, TB:].T
 
 
 def project_body(grads_ref, wq_ref, wk_ref, wv_ref, out_ref):
@@ -258,7 +237,7 @@
         (shape((HALF, TB), F32), blocks, blocks),
         (source,),
         "state",
-        scratch=[pltpu.VMEM((2 * HALF, 2 * TB), BF16)],
+        scratch=[pltpu.VMEM((2 * HALF, 2 * TB), BF16)] * 2,
         flops=4 << 30,
         nbytes=3 << 20,
     )
@@ -286,6 +265,8 @@
             pltpu.VMEM((HALF, TB), BF16),
             pltpu.VMEM((TB, HALF), BF16),
             pltpu.VMEM((2 * HALF, 2 * TB), F32),
+            pltpu.VMEM((2 * HALF, 2 * TB), F32),
+            pltpu.VMEM((2 * HALF, 2 * TB), BF16),
             pltpu.VMEM((2 * HALF, 2 * TB), BF16),
         ],
         flops=4 << 30,

time: 152 us -> 152 us (level); the launches traced: 151 us -> 150 us
  Pallas kernels: 14.1 us -> 11.3 us
    pallas_call x6, Pallas kernels: 14.1 us -> 11.3 us  [call(): pl.pallas_call(body, out_shape=out_shape, in_specs=[VMEM] * len(args), ou...]
where the time goes in v6:
time: 152 us; the launch traced here: 150 us
  blocking collectives  104 us (68%)
  waiting for transfers between devices  22.9 us (15%)
  Pallas kernels  11.3 us (7%)
  starting transfers between devices  10.1 us (7%)
    all_to_all x1, blocking collectives, on_device(): lax.all_to_all(state.reshape(groups, 1, HALF * TB // groups), ('x', 'zg')...  41.9 us
    all_to_all x1, blocking collectives, on_device(): source = lax.all_to_all(packed, ('zc', 'core'), 0, 0, tiled=True)  24.5 us
    all_to_all x1, waiting for transfers between devices, on_device(): lax.all_to_all(sums, ('x', 'zg'), 0, 0, tiled=True).reshape(HALF, TB)  21.4 us
    all_to_all x1, blocking collectives, on_device(): mine = lax.all_to_all(grads, ('zc', 'core'), 0, 0, tiled=True)  20.4 us
    all_to_all x1, blocking collectives, on_device(): pieces = lax.all_to_all(partial_sum, 'y', 0, 0, tiled=True)  17.7 us
    pallas_call x6, Pallas kernels, call(): pl.pallas_call(body, out_shape=out_shape, in_specs=[VMEM] * len(args), ou...  11.3 us
    all_to_all x1, starting transfers between devices, on_device(): lax.all_to_all(sums, ('x', 'zg'), 0, 0, tiled=True).reshape(HALF, TB)  7.11 us
  transfers between devices with their start and end apart: 2, of which 2 were waited for; matrix products, arithmetic and copies ran while one was open for 0% of the time, Pallas kernels for 2%

profile of v6, /device:TPU:1, one launch (start us, length us, event | category | flops | bytes accessed | tf_op | source)
XLA Modules:
  0.0 149.6 jit_solution(15171779704538800857)
XLA Ops:
  0.0 1.9 %pack.1 = f32[8,128,128]{2,1,0:T(8,128)} custom-call(bf16[128,256]{1,0:T(8,128)(2,1)} %q_ref.1, bf16[128,256]{1,0:T(8,128)(2,1)} %k_ref.1, bf16[128,256]{1,0:T(8,128)(2,1)} %v_ref.1, bf16[128,256]{1,0:T(8,128)(2,1)} %g_ref.1), custom_call_target="tpu_custom_call" | custom-call | flops 1048576 | bytes 1048576 | tf_op jit(solution)/shard_map/pack/pallas_call | solution.py:39
  1.9 24.5 %all_to_all.25.source_ref = f32[8,128,128]{2,1,0:T(8,128)S(1)} all-to-all(f32[8,128,128]{2,1,0:T(8,128)} %pack.1), channel_id=1, replica_groups=mesh['x'=4,'zg'=4,'zc'=4,'core'=2,'y'=4] {'zc','core'}, dimensions={0} | all-to-all | bytes 1048576 | tf_op jit(solution)/shard_map/all_to_all | solution.py:232
  26.4 1.4 state.1
  27.7 41.9 %all_to_all.26.parts_ref = f32[16,1,8320]{2,1,0:T(1,128)S(1)} all-to-all(f32[16,1,8320]{2,1,0:T(1,128)S(1)} %bitcast.3), channel_id=1, replica_groups=mesh['x'=4,'zg'=4,'zc'=4,'core'=2,'y'=4] {'x','zg'}, dimensions={0} | all-to-all | bytes 1064960 | tf_op jit(solution)/shard_map/all_to_all | solution.py:244
  69.6 0.9 scan.1
  70.6 7.1 %all-to-all-start.2 = ((f32[16,1,8320]{2,1,0:T(1,128)}), f32[16,1,8320]{2,1,0:T(1,128)S(1)}, u32[]{:S(2)}, u32[]{:S(2)}) async-start(f32[16,1,8320]{2,1,0:T(1,128)} %scan.1), calls=%async_computation.2 | async-start | bytes 1064960 | tf_op jit(solution)/shard_map/all_to_all | solution.py:250
  77.7 3.0 %collective-permute-start = (f32[8,128,128]{2,1,0:T(8,128)S(1)}, f32[8,128,128]{2,1,0:T(8,128)S(1)}, u32[]{:S(2)}, u32[]{:S(2)}) collective-permute-start(f32[8,128,128]{2,1,0:T(8,128)S(1)} %all_to_all.25.source_ref), channel_id=1, source_target_pairs={{0,4},{4,0},{1,5},{5,1},{2,6},{6,2},{3,7},{7,3},{8,12},{12,8},{9,1... | collective-permute-start | bytes 1572872 | tf_op jit(solution)/shard_map/ppermute | solution.py:233
  80.7 1.5 %collective-permute-done.target_ref = f32[8,128,128]{2,1,0:T(8,128)S(1)} collective-permute-done((f32[8,128,128]{2,1,0:T(8,128)S(1)}, f32[8,128,128]{2,1,0:T(8,128)S(1)}, u32[]{:S(2)}, u32[]{:S(2)}) %collective-permute-start) | collective-permute-done | bytes 524320 | tf_op jit(solution)/shard_map/ppermute | solution.py:233
  82.2 3.7 %local.1 = (f32[4,128,256]{2,1,0:T(8,128)S(1)}, bf16[8,128,128]{2,1,0:T(8,128)(2,1)S(1)}) custom-call(bf16[8,128,128]{2,1,0:T(8,128)(2,1)S(1)} %get-tuple-element.11.tok_ref, bf16[8,128,128]{2,1,0:T(8,128)(2,1)S(1)} %get-tuple-element.12.src_ref, f32[8,128,128]{2,1,0:T(8,128)S(1)} %collective-permute-done.target_ref), custom_call_target="tpu_custom_call" | custom-call | flops 4294967296 | bytes 1048576 | tf_op jit(solution)/shard_map/local/pallas_call | solution.py:39
  85.9 21.4 %all-to-all-done.2 = f32[16,1,8320]{2,1,0:T(1,128)S(1)} async-done(((f32[16,1,8320]{2,1,0:T(1,128)}), f32[16,1,8320]{2,1,0:T(1,128)S(1)}, u32[]{:S(2)}, u32[]{:S(2)}) %all-to-all-start.2) | async-done | bytes 532512 | tf_op jit(solution)/shard_map/all_to_all | solution.py:250
  107.3 0.0 copy-start.1
  107.3 0.0 copy-start.2
  107.3 2.8 %grads.1 = f32[8,128,128]{2,1,0:T(8,128)S(1)} custom-call(f32[1040,128]{1,0:T(8,128)S(1)} %bitcast.2, bf16[8,128,128]{2,1,0:T(8,128)(2,1)S(1)} %get-tuple-element.13.out_ref, f32[4,128,256]{2,1,0:T(8,128)S(1)} %get-tuple-element.14.local_ref), custom_call_target="tpu_custom_call" | custom-call | flops 4294967296 | bytes 3145728 | tf_op jit(solution)/shard_map/grads/pallas_call | solution.py:39
  110.1 0.0 copy-start
  110.1 20.4 %all_to_all.27.grads_ref = f32[8,128,128]{2,1,0:T(8,128)S(1)} all-to-all(f32[8,128,128]{2,1,0:T(8,128)S(1)} %grads.1), channel_id=1, replica_groups=mesh['x'=4,'zg'=4,'zc'=4,'core'=2,'y'=4] {'zc','core'}, dimensions={0} | all-to-all | bytes 1048576 | tf_op jit(solution)/shard_map/all_to_all | solution.py:275
  130.5 0.0 copy-done.1
  130.5 0.0 copy-done.2
  130.5 0.0 copy-done
  130.5 0.6 project.1
  131.2 17.7 %all_to_all.28 = f32[4,128,512]{2,1,0:T(8,128)S(1)} all-to-all(f32[4,128,512]{2,1,0:T(8,128)S(1)} %project.1), channel_id=1, replica_groups=mesh['x'=4,'zg'=4,'zc'=4,'core'=2,'y'=4] {'y'}, dimensions={0} | all-to-all | bytes 2097152 | tf_op jit(solution)/shard_map/all_to_all | solution.py:285
  148.9 0.8 reduce_sum.9
Async XLA Ops:
  70.6 36.7 %all-to-all-start.2 = ((f32[16,1,8320]{2,1,0:T(1,128)}), f32[16,1,8320]{2,1,0:T(1,128)S(1)}, u32[]{:S(2)}, u32[]{:S(2)}) async-start(f32[16,1,8320]{2,1,0:T(1,128)} %scan.1), calls=%async_computation.2 | async-start | bytes 1064960 | tf_op jit(solution)/shard_map/all_to_all | solution.py:250
  77.7 4.5 %collective-permute-start = (f32[8,128,128]{2,1,0:T(8,128)S(1)}, f32[8,128,128]{2,1,0:T(8,128)S(1)}, u32[]{:S(2)}, u32[]{:S(2)}) collective-permute-start(f32[8,128,128]{2,1,0:T(8,128)S(1)} %all_to_all.25.source_ref), channel_id=1, source_target_pairs={{0,4},{4,0},{1,5},{5,1},{2,6},{6,2},{3,7},{7,3},{8,12},{12,8},{9,1... | collective-permute-start | bytes 1572872 | tf_op jit(solution)/shard_map/ppermute | solution.py:233
  107.3 23.2 %copy-start.1 = (bf16[256,2048]{1,0:T(8,128)(2,1)S(1)}, bf16[256,2048]{1,0:T(8,128)(2,1)}, u32[]{:S(2)}) copy-start(bf16[256,2048]{1,0:T(8,128)(2,1)} %wk_ref.1) | copy-start | bytes 3145732
  107.3 23.2 %copy-start.2 = (bf16[256,2048]{1,0:T(8,128)(2,1)S(1)}, bf16[256,2048]{1,0:T(8,128)(2,1)}, u32[]{:S(2)}) copy-start(bf16[256,2048]{1,0:T(8,128)(2,1)} %wv_ref.1) | copy-start | bytes 3145732
  110.1 20.4 %copy-start = (bf16[256,2048]{1,0:T(8,128)(2,1)S(1)}, bf16[256,2048]{1,0:T(8,128)(2,1)}, u32[]{:S(2)}) copy-start(bf16[256,2048]{1,0:T(8,128)(2,1)} %wq_ref.1) | copy-start | bytes 3145732

commit v7 on v6

--- a/solution.py
+++ b/solution.py
@@ -170,9 +170,11 @@
 def scan_body(parts_ref, sums_ref):
     core = lax.axis_index("core")
     count = parts_ref.shape[0]
+    cols, rows = lax.axis_size("zg"), lax.axis_size("x")
 
     def step(number, total):
-        place = number + core * (count - 1 - 2 * number)
+        segment = number + core * (count - 1 - 2 * number)
+        place = lax.rem(segment, cols) * rows + lax.div(segment, cols)
         sums_ref[place] = total
         return total + parts_ref[place]
 
@@ -242,12 +244,12 @@
         nbytes=3 << 20,
     )
     parts = lax.all_to_all(
-        state.reshape(groups, 1, HALF * TB // groups), ("x", "zg"), 0, 0, tiled=True
+        state.reshape(groups, 1, HALF * TB // groups), ("zg", "x"), 0, 0, tiled=True
     )
     sums = call(
         scan_body, shape(parts.shape, F32), (parts,), "scan", flops=1 << 20, nbytes=1 << 20
     )
-    before = lax.all_to_all(sums, ("x", "zg"), 0, 0, tiled=True).reshape(HALF, TB)
+    before = lax.all_to_all(sums, ("zg", "x"), 0, 0, tiled=True).reshape(HALF, TB)
     local, out = call(
         local_body,
         (shape((BLOCKS // 2, TB, 2 * TB), F32), blocks),

time: 152 us -> 150 us (0.987); the launches traced: 150 us -> 149 us
    all_to_all x1, blocking collectives: 20.4 us -> 18.6 us  [on_device(): mine = lax.all_to_all(grads, ('zc', 'core'), 0, 0, tiled=True)]
where the time goes in v7:
time: 150 us; the launch traced here: 149 us
  blocking collectives  103 us (69%)
  waiting for transfers between devices  23.8 us (16%)
  Pallas kernels  11.3 us (8%)
  starting transfers between devices  10.4 us (7%)
    all_to_all x1, blocking collectives, on_device(): lax.all_to_all(state.reshape(groups, 1, HALF * TB // groups), ('zg', 'x')...  42.3 us
    all_to_all x1, blocking collectives, on_device(): source = lax.all_to_all(packed, ('zc', 'core'), 0, 0, tiled=True)  24.5 us
    all_to_all x1, waiting for transfers between devices, on_device(): lax.all_to_all(sums, ('zg', 'x'), 0, 0, tiled=True).reshape(HALF, TB)  22.3 us
    all_to_all x1, blocking collectives, on_device(): mine = lax.all_to_all(grads, ('zc', 'core'), 0, 0, tiled=True)  18.6 us
    all_to_all x1, blocking collectives, on_device(): pieces = lax.all_to_all(partial_sum, 'y', 0, 0, tiled=True)  17.5 us
    pallas_call x6, Pallas kernels, call(): pl.pallas_call(body, out_shape=out_shape, in_specs=[VMEM] * len(args), ou...  11.3 us
    all_to_all x1, starting transfers between devices, on_device(): lax.all_to_all(sums, ('zg', 'x'), 0, 0, tiled=True).reshape(HALF, TB)  7.65 us
  transfers between devices with their start and end apart: 2, of which 2 were waited for; matrix products, arithmetic and copies ran while one was open for 0% of the time, Pallas kernels for 2%

profile of v7, /device:TPU:1, one launch (start us, length us, event | category | flops | bytes accessed | tf_op | source)
XLA Modules:
  0.0 149.3 jit_solution(13418534166915874618)
XLA Ops:
  0.0 1.9 %pack.1 = f32[8,128,128]{2,1,0:T(8,128)} custom-call(bf16[128,256]{1,0:T(8,128)(2,1)} %q_ref.1, bf16[128,256]{1,0:T(8,128)(2,1)} %k_ref.1, bf16[128,256]{1,0:T(8,128)(2,1)} %v_ref.1, bf16[128,256]{1,0:T(8,128)(2,1)} %g_ref.1), custom_call_target="tpu_custom_call" | custom-call | flops 1048576 | bytes 1048576 | tf_op jit(solution)/shard_map/pack/pallas_call | solution.py:39
  1.9 24.5 %all_to_all.25.source_ref = f32[8,128,128]{2,1,0:T(8,128)S(1)} all-to-all(f32[8,128,128]{2,1,0:T(8,128)} %pack.1), channel_id=1, replica_groups=mesh['x'=4,'zg'=4,'zc'=4,'core'=2,'y'=4] {'zc','core'}, dimensions={0} | all-to-all | bytes 1048576 | tf_op jit(solution)/shard_map/all_to_all | solution.py:234
  26.4 1.4 state.1
  27.7 42.3 %all_to_all.26.parts_ref = f32[16,1,8320]{2,1,0:T(1,128)S(1)} all-to-all(f32[16,1,8320]{2,1,0:T(1,128)S(1)} %bitcast.3), channel_id=1, replica_groups=mesh['x'=4,'zg'=4,'zc'=4,'core'=2,'y'=4] {'zg','x'}, dimensions={0} | all-to-all | bytes 1064960 | tf_op jit(solution)/shard_map/all_to_all | solution.py:246
  70.1 1.0 scan.1
  71.0 7.7 %all-to-all-start.2 = ((f32[16,1,8320]{2,1,0:T(1,128)}), f32[16,1,8320]{2,1,0:T(1,128)S(1)}, u32[]{:S(2)}, u32[]{:S(2)}) async-start(f32[16,1,8320]{2,1,0:T(1,128)} %scan.1), calls=%async_computation.2 | async-start | bytes 1064960 | tf_op jit(solution)/shard_map/all_to_all | solution.py:252
  78.7 2.8 %collective-permute-start = (f32[8,128,128]{2,1,0:T(8,128)S(1)}, f32[8,128,128]{2,1,0:T(8,128)S(1)}, u32[]{:S(2)}, u32[]{:S(2)}) collective-permute-start(f32[8,128,128]{2,1,0:T(8,128)S(1)} %all_to_all.25.source_ref), channel_id=1, source_target_pairs={{0,4},{4,0},{1,5},{5,1},{2,6},{6,2},{3,7},{7,3},{8,12},{12,8},{9,1... | collective-permute-start | bytes 1572872 | tf_op jit(solution)/shard_map/ppermute | solution.py:235
  81.5 1.5 %collective-permute-done.target_ref = f32[8,128,128]{2,1,0:T(8,128)S(1)} collective-permute-done((f32[8,128,128]{2,1,0:T(8,128)S(1)}, f32[8,128,128]{2,1,0:T(8,128)S(1)}, u32[]{:S(2)}, u32[]{:S(2)}) %collective-permute-start) | collective-permute-done | bytes 524320 | tf_op jit(solution)/shard_map/ppermute | solution.py:235
  83.0 3.7 %local.1 = (f32[4,128,256]{2,1,0:T(8,128)S(1)}, bf16[8,128,128]{2,1,0:T(8,128)(2,1)S(1)}) custom-call(bf16[8,128,128]{2,1,0:T(8,128)(2,1)S(1)} %get-tuple-element.11.tok_ref, bf16[8,128,128]{2,1,0:T(8,128)(2,1)S(1)} %get-tuple-element.12.src_ref, f32[8,128,128]{2,1,0:T(8,128)S(1)} %collective-permute-done.target_ref), custom_call_target="tpu_custom_call" | custom-call | flops 4294967296 | bytes 1048576 | tf_op jit(solution)/shard_map/local/pallas_call | solution.py:39
  86.7 22.3 %all-to-all-done.2 = f32[16,1,8320]{2,1,0:T(1,128)S(1)} async-done(((f32[16,1,8320]{2,1,0:T(1,128)}), f32[16,1,8320]{2,1,0:T(1,128)S(1)}, u32[]{:S(2)}, u32[]{:S(2)}) %all-to-all-start.2) | async-done | bytes 532512 | tf_op jit(solution)/shard_map/all_to_all | solution.py:252
  109.0 0.0 copy-start.1
  109.0 0.0 copy-start.2
  109.0 2.8 %grads.1 = f32[8,128,128]{2,1,0:T(8,128)S(1)} custom-call(f32[1040,128]{1,0:T(8,128)S(1)} %bitcast.2, bf16[8,128,128]{2,1,0:T(8,128)(2,1)S(1)} %get-tuple-element.13.out_ref, f32[4,128,256]{2,1,0:T(8,128)S(1)} %get-tuple-element.14.local_ref), custom_call_target="tpu_custom_call" | custom-call | flops 4294967296 | bytes 3145728 | tf_op jit(solution)/shard_map/grads/pallas_call | solution.py:39
  111.8 0.0 copy-start
  111.8 18.6 %all_to_all.27.grads_ref = f32[8,128,128]{2,1,0:T(8,128)S(1)} all-to-all(f32[8,128,128]{2,1,0:T(8,128)S(1)} %grads.1), channel_id=1, replica_groups=mesh['x'=4,'zg'=4,'zc'=4,'core'=2,'y'=4] {'zc','core'}, dimensions={0} | all-to-all | bytes 1048576 | tf_op jit(solution)/shard_map/all_to_all | solution.py:277
  130.5 0.0 copy-done.1
  130.5 0.0 copy-done.2
  130.5 0.0 copy-done
  130.5 0.6 project.1
  131.1 17.5 %all_to_all.28 = f32[4,128,512]{2,1,0:T(8,128)S(1)} all-to-all(f32[4,128,512]{2,1,0:T(8,128)S(1)} %project.1), channel_id=1, replica_groups=mesh['x'=4,'zg'=4,'zc'=4,'core'=2,'y'=4] {'y'}, dimensions={0} | all-to-all | bytes 2097152 | tf_op jit(solution)/shard_map/all_to_all | solution.py:287
  148.6 0.8 reduce_sum.9
Async XLA Ops:
  71.0 37.9 %all-to-all-start.2 = ((f32[16,1,8320]{2,1,0:T(1,128)}), f32[16,1,8320]{2,1,0:T(1,128)S(1)}, u32[]{:S(2)}, u32[]{:S(2)}) async-start(f32[16,1,8320]{2,1,0:T(1,128)} %scan.1), calls=%async_computation.2 | async-start | bytes 1064960 | tf_op jit(solution)/shard_map/all_to_all | solution.py:252
  78.7 4.3 %collective-permute-start = (f32[8,128,128]{2,1,0:T(8,128)S(1)}, f32[8,128,128]{2,1,0:T(8,128)S(1)}, u32[]{:S(2)}, u32[]{:S(2)}) collective-permute-start(f32[8,128,128]{2,1,0:T(8,128)S(1)} %all_to_all.25.source_ref), channel_id=1, source_target_pairs={{0,4},{4,0},{1,5},{5,1},{2,6},{6,2},{3,7},{7,3},{8,12},{12,8},{9,1... | collective-permute-start | bytes 1572872 | tf_op jit(solution)/shard_map/ppermute | solution.py:235
  109.0 21.5 %copy-start.1 = (bf16[256,2048]{1,0:T(8,128)(2,1)S(1)}, bf16[256,2048]{1,0:T(8,128)(2,1)}, u32[]{:S(2)}) copy-start(bf16[256,2048]{1,0:T(8,128)(2,1)} %wk_ref.1) | copy-start | bytes 3145732
  109.0 21.5 %copy-start.2 = (bf16[256,2048]{1,0:T(8,128)(2,1)S(1)}, bf16[256,2048]{1,0:T(8,128)(2,1)}, u32[]{:S(2)}) copy-start(bf16[256,2048]{1,0:T(8,128)(2,1)} %wv_ref.1) | copy-start | bytes 3145732
  111.8 18.6 %copy-start = (bf16[256,2048]{1,0:T(8,128)(2,1)S(1)}, bf16[256,2048]{1,0:T(8,128)(2,1)}, u32[]{:S(2)}) copy-start(bf16[256,2048]{1,0:T(8,128)(2,1)} %wq_ref.1) | copy-start | bytes 3145732

commit v8 on v7

--- a/solution.py
+++ b/solution.py
@@ -5,7 +5,6 @@
 from jax import lax
 from jax.experimental import pallas as pl
 from jax.experimental.pallas import tpu as pltpu
-from jax.sharding import Mesh
 from jax.sharding import PartitionSpec as P
 
 HD = 64
@@ -129,7 +128,7 @@
 
 
 def local_body(tok_ref, src_ref, target_ref, local_ref, out_ref):
-    core = lax.axis_index("core")
+    core = lax.rem(lax.axis_index("seq"), 2)
     tiles = BLOCKS // 2
     width = 2 * TB
     sign = 1 - 2 * core
@@ -167,14 +166,16 @@
     lax.fori_loop(0, tiles, outer, 0)
 
 
-def scan_body(parts_ref, sums_ref):
-    core = lax.axis_index("core")
+def scan_body(cols, parts_ref, sums_ref):
+    core = lax.rem(lax.axis_index("seq"), 2)
     count = parts_ref.shape[0]
-    cols, rows = lax.axis_size("zg"), lax.axis_size("x")
+    rows = count // cols
 
     def step(number, total):
         segment = number + core * (count - 1 - 2 * number)
-        place = lax.rem(segment, cols) * rows + lax.div(segment, cols)
+        column = lax.rem(segment, cols)
+        column = jnp.where(core == 0, column, lax.rem(cols - column, cols))
+        place = column * rows + lax.div(segment, cols)
         sums_ref[place] = total
         return total + parts_ref[place]
 
@@ -219,9 +220,23 @@
         )
 
 
+def segment_groups(rows, cols):
+    groups = []
+    for place in range(BLOCKS):
+        order = [(column if place % 2 == 0 else -column) % cols for column in range(cols)]
+        groups.append(
+            [(row * cols + column) * BLOCKS + place for column in order for row in range(rows)]
+        )
+    return groups
+
+
 def on_device(queries, keys, values, out_grad, w_query, w_key, w_value):
     shape = jax.ShapeDtypeStruct
-    groups = lax.axis_size("x") * lax.axis_size("zg")
+    devices = lax.axis_size("seq")
+    groups = devices // BLOCKS
+    cols = 4 if groups >= 16 else 2
+    near = [list(range(first, first + BLOCKS)) for first in range(0, devices, BLOCKS)]
+    far = segment_groups(groups // cols, cols)
     packed = call(
         pack_body,
         shape((BLOCKS, TB, TB), F32),
@@ -231,8 +246,8 @@
         flops=1 << 20,
         nbytes=1 << 20,
     )
-    source = lax.all_to_all(packed, ("zc", "core"), 0, 0, tiled=True)
-    target = lax.ppermute(source, "core", [(0, 1), (1, 0)])
+    source = lax.all_to_all(packed, "seq", 0, 0, axis_index_groups=near, tiled=True)
+    target = lax.ppermute(source, "seq", [(place, place ^ 1) for place in range(devices)])
     blocks = shape((BLOCKS, TB, TB), BF16)
     state, tok, src = call(
         state_body,
@@ -244,12 +259,18 @@
         nbytes=3 << 20,
     )
     parts = lax.all_to_all(
-        state.reshape(groups, 1, HALF * TB // groups), ("zg", "x"), 0, 0, tiled=True
+        state.reshape(groups, 1, HALF * TB // groups),
+        "seq",
+        0,
+        0,
+        axis_index_groups=far,
+        tiled=True,
     )
     sums = call(
-        scan_body, shape(parts.shape, F32), (parts,), "scan", flops=1 << 20, nbytes=1 << 20
-    )
-    before = lax.all_to_all(sums, ("zg", "x"), 0, 0, tiled=True).reshape(HALF, TB)
+        functools.partial(scan_body, cols), shape(parts.shape, F32), (parts,), "scan", flops=1 << 20, nbytes=1 << 20
+    )
+    before = lax.all_to_all(sums, "seq", 0, 0, axis_index_groups=far, tiled=True)
+    before = before.reshape(HALF, TB)
     local, out = call(
         local_body,
         (shape((BLOCKS // 2, TB, 2 * TB), F32), blocks),
@@ -274,8 +295,8 @@
         flops=4 << 30,
         nbytes=3 << 20,
     )
-    mine = lax.all_to_all(grads, ("zc", "core"), 0, 0, tiled=True)
-    heads = lax.axis_size("y")
+    mine = lax.all_to_all(grads, "seq", 0, 0, axis_index_groups=near, tiled=True)
+    heads = lax.axis_size("head")
     partial_sum = call(
         project_body,
         shape((heads, TB, w_query.shape[1] // heads), F32),
@@ -284,19 +305,12 @@
         flops=1 << 29,
         nbytes=4 << 20,
     )
-    pieces = lax.all_to_all(partial_sum, "y", 0, 0, tiled=True)
+    pieces = lax.all_to_all(partial_sum, "head", 0, 0, tiled=True)
     return jnp.sum(pieces, axis=0).astype(BF16)
 
 
 def solution(mesh):
-    seq, head = mesh.devices.shape
-    cols = 4 if seq >= 128 else 2
-    grid = Mesh(
-        mesh.devices.reshape(seq // (cols * 8), cols, CHIPS, 2, head),
-        ("x", "zg", "zc", "core", "y"),
-    )
-    tokens = ("x", "zg", "zc", "core")
-    placed = (P(tokens, "y"),) * 4 + (P("y", None),) * 3
+    placed = (P("seq", "head"),) * 4 + (P("head", None),) * 3
     return jax.shard_map(
-        on_device, mesh=grid, in_specs=placed, out_specs=P(tokens, "y"), check_vma=False
-    )
+        on_device, mesh=mesh, in_specs=placed, out_specs=P("seq", "head"), check_vma=False
+    )

time: 150 us -> 151 us (level)
  no operation moved by 1% of the time
where the time goes in v8:
time: 151 us; the launch traced here: 150 us
  blocking collectives  104 us (69%)
  waiting for transfers between devices  24 us (16%)
  Pallas kernels  11.3 us (7%)
  starting transfers between devices  10.2 us (7%)
    all_to_all x1, blocking collectives, on_device(): lax.all_to_all(state.reshape(groups, 1, HALF * TB // groups), 'seq', 0, 0...  42.6 us
    all_to_all x1, blocking collectives, on_device(): lax.all_to_all(packed, 'seq', 0, 0, axis_index_groups=near, tiled=True)  24.5 us
    all_to_all x1, waiting for transfers between devices, on_device(): lax.all_to_all(sums, 'seq', 0, 0, axis_index_groups=far, tiled=True)  22.5 us
    all_to_all x1, blocking collectives, on_device(): lax.all_to_all(grads, 'seq', 0, 0, axis_index_groups=near, tiled=True)  18.7 us
    all_to_all x1, blocking collectives, on_device(): pieces = lax.all_to_all(partial_sum, 'head', 0, 0, tiled=True)  18 us
    pallas_call x6, Pallas kernels, call(): pl.pallas_call(body, out_shape=out_shape, in_specs=[VMEM] * len(args), ou...  11.3 us
    all_to_all x1, starting transfers between devices, on_device(): lax.all_to_all(sums, 'seq', 0, 0, axis_index_groups=far, tiled=True)  7.37 us
  transfers between devices with their start and end apart: 2, of which 2 were waited for; matrix products, arithmetic and copies ran while one was open for 0% of the time, Pallas kernels for 2%

profile of v8, /device:TPU:1, one launch (start us, length us, event | category | flops | bytes accessed | tf_op | source)
XLA Modules:
  0.0 150.2 jit_solution(2584980999070786851)
XLA Ops:
  0.0 1.9 %pack.1 = f32[8,128,128]{2,1,0:T(8,128)} custom-call(bf16[128,256]{1,0:T(8,128)(2,1)} %q_ref.1, bf16[128,256]{1,0:T(8,128)(2,1)} %k_ref.1, bf16[128,256]{1,0:T(8,128)(2,1)} %v_ref.1, bf16[128,256]{1,0:T(8,128)(2,1)} %g_ref.1), custom_call_target="tpu_custom_call" | custom-call | flops 1048576 | bytes 1048576 | tf_op jit(solution)/shard_map/pack/pallas_call | solution.py:38
  1.9 24.5 %all_to_all.25.source_ref = f32[8,128,128]{2,1,0:T(8,128)S(1)} all-to-all(f32[8,128,128]{2,1,0:T(8,128)} %pack.1), channel_id=1, replica_groups={{0,4,8,12,16,20,24,28},{32,36,40,44,48,52,56,60},{64,68,72,76,80,84,88,..., dimensions={0} | all-to-all | bytes 1048576 | tf_op jit(solution)/shard_map/all_to_all | solution.py:249
  26.4 1.4 state.1
  27.7 42.6 %all_to_all.26.parts_ref = f32[16,1,8320]{2,1,0:T(1,128)S(1)} all-to-all(f32[16,1,8320]{2,1,0:T(1,128)S(1)} %bitcast.3), channel_id=1, replica_groups={{0,128,256,384,32,160,288,416,64,192,320,448,96,224,352,480},{4,132,260..., dimensions={0} | all-to-all | bytes 1064960 | tf_op jit(solution)/shard_map/all_to_all | solution.py:261
  70.3 1.0 scan.1
  71.3 7.4 %all-to-all-start.2 = ((f32[16,1,8320]{2,1,0:T(1,128)}), f32[16,1,8320]{2,1,0:T(1,128)S(1)}, u32[]{:S(2)}, u32[]{:S(2)}) async-start(f32[16,1,8320]{2,1,0:T(1,128)} %scan.1), calls=%async_computation.2 | async-start | bytes 1064960 | tf_op jit(solution)/shard_map/all_to_all | solution.py:272
  78.7 2.8 %collective-permute-start = (f32[8,128,128]{2,1,0:T(8,128)S(1)}, f32[8,128,128]{2,1,0:T(8,128)S(1)}, u32[]{:S(2)}, u32[]{:S(2)}) collective-permute-start(f32[8,128,128]{2,1,0:T(8,128)S(1)} %all_to_all.25.source_ref), channel_id=1, source_target_pairs={{0,4},{4,0},{8,12},{12,8},{16,20},{20,16},{24,28},{28,24},{32,36},... | collective-permute-start | bytes 1572872 | tf_op jit(solution)/shard_map/ppermute | solution.py:250
  81.5 1.5 %collective-permute-done.target_ref = f32[8,128,128]{2,1,0:T(8,128)S(1)} collective-permute-done((f32[8,128,128]{2,1,0:T(8,128)S(1)}, f32[8,128,128]{2,1,0:T(8,128)S(1)}, u32[]{:S(2)}, u32[]{:S(2)}) %collective-permute-start) | collective-permute-done | bytes 524320 | tf_op jit(solution)/shard_map/ppermute | solution.py:250
  83.0 3.7 %local.1 = (f32[4,128,256]{2,1,0:T(8,128)S(1)}, bf16[8,128,128]{2,1,0:T(8,128)(2,1)S(1)}) custom-call(bf16[8,128,128]{2,1,0:T(8,128)(2,1)S(1)} %get-tuple-element.11.tok_ref, bf16[8,128,128]{2,1,0:T(8,128)(2,1)S(1)} %get-tuple-element.12.src_ref, f32[8,128,128]{2,1,0:T(8,128)S(1)} %collective-permute-done.target_ref), custom_call_target="tpu_custom_call" | custom-call | flops 4294967296 | bytes 1048576 | tf_op jit(solution)/shard_map/local/pallas_call | solution.py:38
  86.7 22.5 %all-to-all-done.2 = f32[16,1,8320]{2,1,0:T(1,128)S(1)} async-done(((f32[16,1,8320]{2,1,0:T(1,128)}), f32[16,1,8320]{2,1,0:T(1,128)S(1)}, u32[]{:S(2)}, u32[]{:S(2)}) %all-to-all-start.2) | async-done | bytes 532512 | tf_op jit(solution)/shard_map/all_to_all | solution.py:272
  109.1 0.0 copy-start.1
  109.1 0.0 copy-start.2
  109.1 2.8 %grads.1 = f32[8,128,128]{2,1,0:T(8,128)S(1)} custom-call(f32[1040,128]{1,0:T(8,128)S(1)} %bitcast.2, bf16[8,128,128]{2,1,0:T(8,128)(2,1)S(1)} %get-tuple-element.13.out_ref, f32[4,128,256]{2,1,0:T(8,128)S(1)} %get-tuple-element.14.local_ref), custom_call_target="tpu_custom_call" | custom-call | flops 4294967296 | bytes 3145728 | tf_op jit(solution)/shard_map/grads/pallas_call | solution.py:38
  112.0 0.0 copy-start
  112.0 18.7 %all_to_all.27.grads_ref = f32[8,128,128]{2,1,0:T(8,128)S(1)} all-to-all(f32[8,128,128]{2,1,0:T(8,128)S(1)} %grads.1), channel_id=1, replica_groups={{0,4,8,12,16,20,24,28},{32,36,40,44,48,52,56,60},{64,68,72,76,80,84,88,..., dimensions={0} | all-to-all | bytes 1048576 | tf_op jit(solution)/shard_map/all_to_all | solution.py:298
  130.7 0.0 copy-done.1
  130.7 0.0 copy-done.2
  130.7 0.0 copy-done
  130.7 0.6 project.1
  131.4 18.0 %all_to_all.28 = f32[4,128,512]{2,1,0:T(8,128)S(1)} all-to-all(f32[4,128,512]{2,1,0:T(8,128)S(1)} %project.1), channel_id=1, replica_groups=mesh['seq'=128,'head'=4] {'head'}, dimensions={0} | all-to-all | bytes 2097152 | tf_op jit(solution)/shard_map/all_to_all | solution.py:308
  149.4 0.8 reduce_sum.9
Async XLA Ops:
  71.3 37.8 %all-to-all-start.2 = ((f32[16,1,8320]{2,1,0:T(1,128)}), f32[16,1,8320]{2,1,0:T(1,128)S(1)}, u32[]{:S(2)}, u32[]{:S(2)}) async-start(f32[16,1,8320]{2,1,0:T(1,128)} %scan.1), calls=%async_computation.2 | async-start | bytes 1064960 | tf_op jit(solution)/shard_map/all_to_all | solution.py:272
  78.7 4.3 %collective-permute-start = (f32[8,128,128]{2,1,0:T(8,128)S(1)}, f32[8,128,128]{2,1,0:T(8,128)S(1)}, u32[]{:S(2)}, u32[]{:S(2)}) collective-permute-start(f32[8,128,128]{2,1,0:T(8,128)S(1)} %all_to_all.25.source_ref), channel_id=1, source_target_pairs={{0,4},{4,0},{8,12},{12,8},{16,20},{20,16},{24,28},{28,24},{32,36},... | collective-permute-start | bytes 1572872 | tf_op jit(solution)/shard_map/ppermute | solution.py:250
  109.1 21.6 %copy-start.1 = (bf16[256,2048]{1,0:T(8,128)(2,1)S(1)}, bf16[256,2048]{1,0:T(8,128)(2,1)}, u32[]{:S(2)}) copy-start(bf16[256,2048]{1,0:T(8,128)(2,1)} %wk_ref.1) | copy-start | bytes 3145732
  109.1 21.6 %copy-start.2 = (bf16[256,2048]{1,0:T(8,128)(2,1)S(1)}, bf16[256,2048]{1,0:T(8,128)(2,1)}, u32[]{:S(2)}) copy-start(bf16[256,2048]{1,0:T(8,128)(2,1)} %wv_ref.1) | copy-start | bytes 3145732
  112.0 18.8 %copy-start = (bf16[256,2048]{1,0:T(8,128)(2,1)S(1)}, bf16[256,2048]{1,0:T(8,128)(2,1)}, u32[]{:S(2)}) copy-start(bf16[256,2048]{1,0:T(8,128)(2,1)} %wq_ref.1) | copy-start | bytes 3145732

commit v9 on v5

--- a/solution.py
+++ b/solution.py
@@ -110,25 +110,22 @@
     return jnp.concatenate(sums, axis=0)
 
 
-def state_body(source_ref, state_ref, tok_ref, src_ref, feats_ref):
-    for block in range(BLOCKS):
-        source = source_ref[block]
-        tok_ref[block] = source.astype(BF16)
-        src_ref[block] = source.T.astype(BF16)
-    state_ref[...] = jnp.zeros_like(state_ref)
-
-    def step(tile, carry):
+def state_body(source_ref, state_ref, tok_ref, src_ref, *feats_refs):
+    for tile in range(BLOCKS // 2):
+        feats_ref = feats_refs[tile % len(feats_refs)]
+        for block in (2 * tile, 2 * tile + 1):
+            source = source_ref[block]
+            tok_ref[block] = source.astype(BF16)
+            src_ref[block] = source.T.astype(BF16)
         xt = jnp.concatenate([src_ref[2 * tile, :HD], src_ref[2 * tile + 1, :HD]], axis=1)
         write_features(xt.astype(F32), 1.0, feats_ref)
         tok = jnp.concatenate([tok_ref[2 * tile], tok_ref[2 * tile + 1]], axis=0)
         values = tok[:, HD:]
         zeros = jnp.zeros_like(values)
-        state_ref[...] += dot(
-            feats_ref[:HALF, :], jnp.concatenate([values, zeros], axis=1)
-        ) + dot(feats_ref[HALF:, :], jnp.concatenate([zeros, values], axis=1))
-        return carry
-
-    lax.fori_loop(0, BLOCKS // 2, step, 0)
+        part = dot(feats_ref[:HALF, :], jnp.concatenate([values, zeros], axis=1)) + dot(
+            feats_ref[HALF:, :], jnp.concatenate([zeros, values], axis=1)
+        )
+        state_ref[...] = part if tile == 0 else state_ref[...] + part
 
 
 def local_body(tiles, first_tile, tok_ref, src_ref, target_ref, local_ref, *out_refs):
@@ -176,16 +173,18 @@
 def scan_body(parts_ref, unused_ref, sums_ref):
     core = lax.axis_index("core")
     count = parts_ref.shape[0]
+    cols, rows = lax.axis_size("zg"), lax.axis_size("x")
 
     def step(number, total):
-        place = number + core * (count - 1 - 2 * number)
+        segment = number + core * (count - 1 - 2 * number)
+        place = lax.rem(segment, cols) * rows + lax.div(segment, cols)
         sums_ref[place] = total
         return total + parts_ref[place]
 
     lax.fori_loop(0, count, step, jnp.zeros(parts_ref.shape[1:], F32))
 
 
-def grads_body(state_ref, out_ref, early_ref, late_ref, grads_ref, rows_ref, cols_ref, wide_ref, feats_ref):
+def grads_body(state_ref, out_ref, early_ref, late_ref, grads_ref, rows_ref, cols_ref, *tile_refs):
     rows_ref[...] = state_ref[...].astype(BF16)
     for start in range(0, HALF, TB):
         stop = min(start + TB, HALF)
@@ -193,24 +192,22 @@
         if stop - start < TB:
             part = jnp.concatenate([part, jnp.zeros((TB - stop + start, TB), F32)], axis=0)
         cols_ref[:, start:stop] = part.T[:, : stop - start].astype(BF16)
-
-    def step(tile, carry):
+    zeros = jnp.zeros((HD, 2 * TB), BF16)
+    for tile in range(BLOCKS // 2):
+        wide_ref, feats_ref = tile_refs[tile % 2], tile_refs[2 + tile % 2]
         target = jnp.concatenate([out_ref[2 * tile], out_ref[2 * tile + 1]], axis=1)
-        xt = target[:HD].astype(F32)
-        zeros = jnp.zeros((HD, 2 * TB), BF16)
         wide_ref[:HALF] = dot(rows_ref[...], jnp.concatenate([target[HD:], zeros], axis=0))
         wide_ref[HALF:] = dot(rows_ref[...], jnp.concatenate([zeros, target[HD:]], axis=0))
+        xt = target[:HD].astype(F32)
         write_features(xt, 2.0, feats_ref)
         values = dot(cols_ref[:HD, :], feats_ref[:HALF]) + dot(cols_ref[HD:, :], feats_ref[HALF:])
-        local = jnp.where(tile < 2, early_ref[tile % 2], late_ref[tile % 2])
+        back = chain_back(xt, wide_ref)
+        local = early_ref[tile] if tile < 2 else late_ref[tile - 2]
         result = local + jnp.concatenate(
-            [chain_back(xt, wide_ref) * (2.0 / (HD * HD)), values * (1.0 / (HD * HD))], axis=0
+            [back * (2.0 / (HD * HD)), values * (1.0 / (HD * HD))], axis=0
         )
         grads_ref[2 * tile] = result[:, :TB].T
         grads_ref[2 * tile + 1] = result[:, TB:].T
-        return carry
-
-    lax.fori_loop(0, BLOCKS // 2, step, 0)
 
 
 def project_body(grads_ref, wq_ref, wk_ref, wv_ref, out_ref):
@@ -246,12 +243,12 @@
         (shape((HALF, TB), F32), blocks, blocks),
         (source,),
         "state",
-        scratch=[pltpu.VMEM((2 * HALF, 2 * TB), BF16)],
+        scratch=[pltpu.VMEM((2 * HALF, 2 * TB), BF16)] * 2,
         flops=4 << 30,
         nbytes=3 << 20,
     )
     parts = lax.all_to_all(
-        state.reshape(groups, 1, HALF * TB // groups), ("x", "zg"), 0, 0, tiled=True
+        state.reshape(groups, 1, HALF * TB // groups), ("zg", "x"), 0, 0, tiled=True
     )
     tiles = BLOCKS // 4
     halves = shape((tiles, TB, 2 * TB), F32)
@@ -266,7 +263,7 @@
     sums = call(
         scan_body, shape(parts.shape, F32), (parts, early), "scan", flops=1 << 20, nbytes=1 << 20
     )
-    before = lax.all_to_all(sums, ("x", "zg"), 0, 0, tiled=True).reshape(HALF, TB)
+    before = lax.all_to_all(sums, ("zg", "x"), 0, 0, tiled=True).reshape(HALF, TB)
     (late,) = call(
         functools.partial(local_body, tiles, tiles),
         (halves,),
@@ -284,6 +281,8 @@
             pltpu.VMEM((HALF, TB), BF16),
             pltpu.VMEM((TB, HALF), BF16),
             pltpu.VMEM((2 * HALF, 2 * TB), F32),
+            pltpu.VMEM((2 * HALF, 2 * TB), F32),
+            pltpu.VMEM((2 * HALF, 2 * TB), BF16),
             pltpu.VMEM((2 * HALF, 2 * TB), BF16),
         ],
         flops=4 << 30,

time: 154 us -> 151 us (0.981)
  blocking collectives: 62.7 us -> 59.4 us
  waiting for transfers between devices: 51.6 us -> 54.4 us
    all_to_all x1, blocking collectives: 20.4 us -> 17.3 us  [on_device(): mine = lax.all_to_all(grads, ('zc', 'core'), 0, 0, tiled=True)]
    all_to_all x2, waiting for transfers between devices: 50.1 us -> 52.9 us  [the longest x1 30.4 us: on_device(): lax.all_to_all(sums, ('zg', 'x'), 0, 0, tiled=True).reshape(HALF, TB)]
where the time goes in v9:
time: 151 us; the launch traced here: 150 us
  blocking collectives  59.4 us (39%)
  waiting for transfers between devices  54.4 us (36%)
  starting transfers between devices  23.4 us (15%)
  Pallas kernels  12.1 us (8%)
    all_to_all x1, waiting for transfers between devices, on_device(): lax.all_to_all(sums, ('zg', 'x'), 0, 0, tiled=True).reshape(HALF, TB)  30.4 us
    all_to_all x1, blocking collectives, on_device(): source = lax.all_to_all(packed, ('zc', 'core'), 0, 0, tiled=True)  24.5 us
    all_to_all x1, waiting for transfers between devices, on_device(): lax.all_to_all(state.reshape(groups, 1, HALF * TB // groups), ('zg', 'x')...  22.5 us
    all_to_all x1, blocking collectives, on_device(): pieces = lax.all_to_all(partial_sum, 'y', 0, 0, tiled=True)  17.5 us
    all_to_all x1, blocking collectives, on_device(): mine = lax.all_to_all(grads, ('zc', 'core'), 0, 0, tiled=True)  17.3 us
    pallas_call x7, Pallas kernels, call(): pl.pallas_call(body, out_shape=out_shape, in_specs=[VMEM] * len(args), ou...  12.1 us
    all_to_all x1, starting transfers between devices, on_device(): lax.all_to_all(state.reshape(groups, 1, HALF * TB // groups), ('zg', 'x')...  12 us
    all_to_all x1, starting transfers between devices, on_device(): lax.all_to_all(sums, ('zg', 'x'), 0, 0, tiled=True).reshape(HALF, TB)  8.18 us
  transfers between devices with their start and end apart: 3, of which 3 were waited for; matrix products, arithmetic and copies ran while one was open for 0% of the time, Pallas kernels for 2%

profile of v9, /device:TPU:1, one launch (start us, length us, event | category | flops | bytes accessed | tf_op | source)
XLA Modules:
  0.0 150.2 jit_solution(1626053501153976735)
XLA Ops:
  0.0 1.9 %pack.1 = f32[8,128,128]{2,1,0:T(8,128)} custom-call(bf16[128,256]{1,0:T(8,128)(2,1)} %q_ref.1, bf16[128,256]{1,0:T(8,128)(2,1)} %k_ref.1, bf16[128,256]{1,0:T(8,128)(2,1)} %v_ref.1, bf16[128,256]{1,0:T(8,128)(2,1)} %g_ref.1), custom_call_target="tpu_custom_call" | custom-call | flops 1048576 | bytes 1048576 | tf_op jit(solution)/shard_map/pack/pallas_call | solution.py:39
  1.9 24.5 %all_to_all.25.source_ref = f32[8,128,128]{2,1,0:T(8,128)S(1)} all-to-all(f32[8,128,128]{2,1,0:T(8,128)} %pack.1), channel_id=1, replica_groups=mesh['x'=4,'zg'=4,'zc'=4,'core'=2,'y'=4] {'zc','core'}, dimensions={0} | all-to-all | bytes 1048576 | tf_op jit(solution)/shard_map/all_to_all | solution.py:238
  26.4 2.1 %state.1 = (f32[1040,128]{1,0:T(8,128)}, bf16[8,128,128]{2,1,0:T(8,128)(2,1)S(1)}, bf16[8,128,128]{2,1,0:T(8,128)(2,1)S(1)}) custom-call(f32[8,128,128]{2,1,0:T(8,128)S(1)} %all_to_all.25.source_ref), custom_call_target="tpu_custom_call" | custom-call | flops 4294967296 | bytes 3145728 | tf_op jit(solution)/shard_map/state/pallas_call | solution.py:39
  28.5 12.0 %all-to-all-start.1 = ((f32[16,1,8320]{2,1,0:T(1,128)}), f32[16,1,8320]{2,1,0:T(1,128)S(1)}, u32[]{:S(2)}, u32[]{:S(2)}) async-start(f32[16,1,8320]{2,1,0:T(1,128)} %bitcast), calls=%async_computation.1 | async-start | bytes 1064960 | tf_op jit(solution)/shard_map/all_to_all | solution.py:250
  40.6 3.2 %collective-permute-start = (f32[8,128,128]{2,1,0:T(8,128)S(1)}, f32[8,128,128]{2,1,0:T(8,128)S(1)}, u32[]{:S(2)}, u32[]{:S(2)}) collective-permute-start(f32[8,128,128]{2,1,0:T(8,128)S(1)} %all_to_all.25.source_ref), channel_id=1, source_target_pairs={{0,4},{4,0},{1,5},{5,1},{2,6},{6,2},{3,7},{7,3},{8,12},{12,8},{9,1... | collective-permute-start | bytes 1572872 | tf_op jit(solution)/shard_map/ppermute | solution.py:239
  43.8 1.5 %collective-permute-done.target_ref = f32[8,128,128]{2,1,0:T(8,128)S(1)} collective-permute-done((f32[8,128,128]{2,1,0:T(8,128)S(1)}, f32[8,128,128]{2,1,0:T(8,128)S(1)}, u32[]{:S(2)}, u32[]{:S(2)}) %collective-permute-start) | collective-permute-done | bytes 524320 | tf_op jit(solution)/shard_map/ppermute | solution.py:239
  45.3 2.6 %early.1 = (f32[2,128,256]{2,1,0:T(8,128)S(1)}, bf16[8,128,128]{2,1,0:T(8,128)(2,1)S(1)}) custom-call(bf16[8,128,128]{2,1,0:T(8,128)(2,1)S(1)} %get-tuple-element.11.tok_ref, bf16[8,128,128]{2,1,0:T(8,128)(2,1)S(1)} %get-tuple-element.12.src_ref, f32[8,128,128]{2,1,0:T(8,128)S(1)} %collective-permute-done.target_ref), custom_call_target="tpu_custom_call" | custom-call | flops 2147483648 | bytes 1048576 | tf_op jit(solution)/shard_map/early/pallas_call | solution.py:39
  47.9 22.5 %all-to-all-done.1.parts_ref = f32[16,1,8320]{2,1,0:T(1,128)S(1)} async-done(((f32[16,1,8320]{2,1,0:T(1,128)}), f32[16,1,8320]{2,1,0:T(1,128)S(1)}, u32[]{:S(2)}, u32[]{:S(2)}) %all-to-all-start.1) | async-done | bytes 532512 | tf_op jit(solution)/shard_map/all_to_all | solution.py:250
  70.5 1.0 scan.1
  71.4 8.2 %all-to-all-start.2 = ((f32[16,1,8320]{2,1,0:T(1,128)}), f32[16,1,8320]{2,1,0:T(1,128)S(1)}, u32[]{:S(2)}, u32[]{:S(2)}) async-start(f32[16,1,8320]{2,1,0:T(1,128)} %scan.1), calls=%async_computation.2 | async-start | bytes 1064960 | tf_op jit(solution)/shard_map/all_to_all | solution.py:266
  79.6 1.1 late.1.late_ref
  80.7 30.4 %all-to-all-done.2 = f32[16,1,8320]{2,1,0:T(1,128)S(1)} async-done(((f32[16,1,8320]{2,1,0:T(1,128)}), f32[16,1,8320]{2,1,0:T(1,128)S(1)}, u32[]{:S(2)}, u32[]{:S(2)}) %all-to-all-start.2) | async-done | bytes 532512 | tf_op jit(solution)/shard_map/all_to_all | solution.py:266
  111.1 0.0 copy-start.1
  111.1 0.0 copy-start.2
  111.1 2.8 %grads.1 = f32[8,128,128]{2,1,0:T(8,128)S(1)} custom-call(f32[1040,128]{1,0:T(8,128)S(1)} %bitcast.2, bf16[8,128,128]{2,1,0:T(8,128)(2,1)S(1)} %get-tuple-element.14.target_ref.out_ref, f32[2,128,256]{2,1,0:T(8,128)S(1)} %get-tuple-element.13.unused_ref.early_ref, f32[2,128,256]{2,1,0:T(8,128)S(1)} %late.1.late_ref), custom_call_target="tpu_custom_call" | custom-call | flops 4294967296 | bytes 3145728 | tf_op jit(solution)/shard_map/grads/pallas_call | solution.py:39
  113.9 0.0 copy-start
  113.9 17.3 %all_to_all.26.grads_ref = f32[8,128,128]{2,1,0:T(8,128)S(1)} all-to-all(f32[8,128,128]{2,1,0:T(8,128)S(1)} %grads.1), channel_id=1, replica_groups=mesh['x'=4,'zg'=4,'zc'=4,'core'=2,'y'=4] {'zc','core'}, dimensions={0} | all-to-all | bytes 1048576 | tf_op jit(solution)/shard_map/all_to_all | solution.py:291
  131.3 0.0 copy-done.1
  131.3 0.0 copy-done.2
  131.3 0.0 copy-done
  131.3 0.6 project.1
  131.9 17.5 %all_to_all.27 = f32[4,128,512]{2,1,0:T(8,128)S(1)} all-to-all(f32[4,128,512]{2,1,0:T(8,128)S(1)} %project.1), channel_id=1, replica_groups=mesh['x'=4,'zg'=4,'zc'=4,'core'=2,'y'=4] {'y'}, dimensions={0} | all-to-all | bytes 2097152 | tf_op jit(solution)/shard_map/all_to_all | solution.py:301
  149.4 0.8 reduce_sum.9
Async XLA Ops:
  28.5 41.9 %all-to-all-start.1 = ((f32[16,1,8320]{2,1,0:T(1,128)}), f32[16,1,8320]{2,1,0:T(1,128)S(1)}, u32[]{:S(2)}, u32[]{:S(2)}) async-start(f32[16,1,8320]{2,1,0:T(1,128)} %bitcast), calls=%async_computation.1 | async-start | bytes 1064960 | tf_op jit(solution)/shard_map/all_to_all | solution.py:250
  40.6 4.8 %collective-permute-start = (f32[8,128,128]{2,1,0:T(8,128)S(1)}, f32[8,128,128]{2,1,0:T(8,128)S(1)}, u32[]{:S(2)}, u32[]{:S(2)}) collective-permute-start(f32[8,128,128]{2,1,0:T(8,128)S(1)} %all_to_all.25.source_ref), channel_id=1, source_target_pairs={{0,4},{4,0},{1,5},{5,1},{2,6},{6,2},{3,7},{7,3},{8,12},{12,8},{9,1... | collective-permute-start | bytes 1572872 | tf_op jit(solution)/shard_map/ppermute | solution.py:239
  71.4 39.7 %all-to-all-start.2 = ((f32[16,1,8320]{2,1,0:T(1,128)}), f32[16,1,8320]{2,1,0:T(1,128)S(1)}, u32[]{:S(2)}, u32[]{:S(2)}) async-start(f32[16,1,8320]{2,1,0:T(1,128)} %scan.1), calls=%async_computation.2 | async-start | bytes 1064960 | tf_op jit(solution)/shard_map/all_to_all | solution.py:266
  111.1 20.2 %copy-start.1 = (bf16[256,2048]{1,0:T(8,128)(2,1)S(1)}, bf16[256,2048]{1,0:T(8,128)(2,1)}, u32[]{:S(2)}) copy-start(bf16[256,2048]{1,0:T(8,128)(2,1)} %wk_ref.1) | copy-start | bytes 3145732
  111.1 20.2 %copy-start.2 = (bf16[256,2048]{1,0:T(8,128)(2,1)S(1)}, bf16[256,2048]{1,0:T(8,128)(2,1)}, u32[]{:S(2)}) copy-start(bf16[256,2048]{1,0:T(8,128)(2,1)} %wv_ref.1) | copy-start | bytes 3145732
  113.9 17.3 %copy-start = (bf16[256,2048]{1,0:T(8,128)(2,1)S(1)}, bf16[256,2048]{1,0:T(8,128)(2,1)}, u32[]{:S(2)}) copy-start(bf16[256,2048]{1,0:T(8,128)(2,1)} %wq_ref.1) | copy-start | bytes 3145732

commit v10 on v7

--- a/solution.py
+++ b/solution.py
@@ -178,7 +178,7 @@
         sums_ref[place] = total
         return total + parts_ref[place]
 
-    lax.fori_loop(0, count, step, jnp.zeros(parts_ref.shape[1:], F32))
+    lax.fori_loop(0, count, step, jnp.zeros(parts_ref.shape[1:], F32), unroll=True)
 
 
 def grads_body(state_ref, out_ref, local_ref, grads_ref, rows_ref, cols_ref, *tile_refs):

time: 150 us -> 150 us (level)
  no operation moved by 1% of the time
where the time goes in v10:
time: 150 us; the launch traced here: 149 us
  blocking collectives  103 us (69%)
  waiting for transfers between devices  23.8 us (16%)
  Pallas kernels  11.2 us (7%)
  starting transfers between devices  10.4 us (7%)
    all_to_all x1, blocking collectives, on_device(): lax.all_to_all(state.reshape(groups, 1, HALF * TB // groups), ('zg', 'x')...  42.3 us
    all_to_all x1, blocking collectives, on_device(): source = lax.all_to_all(packed, ('zc', 'core'), 0, 0, tiled=True)  24.5 us
    all_to_all x1, waiting for transfers between devices, on_device(): lax.all_to_all(sums, ('zg', 'x'), 0, 0, tiled=True).reshape(HALF, TB)  22.3 us
    all_to_all x1, blocking collectives, on_device(): mine = lax.all_to_all(grads, ('zc', 'core'), 0, 0, tiled=True)  18.6 us
    all_to_all x1, blocking collectives, on_device(): pieces = lax.all_to_all(partial_sum, 'y', 0, 0, tiled=True)  17.5 us
    pallas_call x6, Pallas kernels, call(): pl.pallas_call(body, out_shape=out_shape, in_specs=[VMEM] * len(args), ou...  11.2 us
    all_to_all x1, starting transfers between devices, on_device(): lax.all_to_all(sums, ('zg', 'x'), 0, 0, tiled=True).reshape(HALF, TB)  7.65 us
  transfers between devices with their start and end apart: 2, of which 2 were waited for; matrix products, arithmetic and copies ran while one was open for 0% of the time, Pallas kernels for 2%

profile of v10, /device:TPU:1, one launch (start us, length us, event | category | flops | bytes accessed | tf_op | source)
XLA Modules:
  0.0 149.2 jit_solution(2544307196365388892)
XLA Ops:
  0.0 1.9 %pack.1 = f32[8,128,128]{2,1,0:T(8,128)} custom-call(bf16[128,256]{1,0:T(8,128)(2,1)} %q_ref.1, bf16[128,256]{1,0:T(8,128)(2,1)} %k_ref.1, bf16[128,256]{1,0:T(8,128)(2,1)} %v_ref.1, bf16[128,256]{1,0:T(8,128)(2,1)} %g_ref.1), custom_call_target="tpu_custom_call" | custom-call | flops 1048576 | bytes 1048576 | tf_op jit(solution)/shard_map/pack/pallas_call | solution.py:39
  1.9 24.5 %all_to_all.25.source_ref = f32[8,128,128]{2,1,0:T(8,128)S(1)} all-to-all(f32[8,128,128]{2,1,0:T(8,128)} %pack.1), channel_id=1, replica_groups=mesh['x'=4,'zg'=4,'zc'=4,'core'=2,'y'=4] {'zc','core'}, dimensions={0} | all-to-all | bytes 1048576 | tf_op jit(solution)/shard_map/all_to_all | solution.py:234
  26.4 1.4 state.1
  27.7 42.3 %all_to_all.26.parts_ref = f32[16,1,8320]{2,1,0:T(1,128)S(1)} all-to-all(f32[16,1,8320]{2,1,0:T(1,128)S(1)} %bitcast.3), channel_id=1, replica_groups=mesh['x'=4,'zg'=4,'zc'=4,'core'=2,'y'=4] {'zg','x'}, dimensions={0} | all-to-all | bytes 1064960 | tf_op jit(solution)/shard_map/all_to_all | solution.py:246
  70.1 0.8 scan.1
  70.9 7.7 %all-to-all-start.2 = ((f32[16,1,8320]{2,1,0:T(1,128)}), f32[16,1,8320]{2,1,0:T(1,128)S(1)}, u32[]{:S(2)}, u32[]{:S(2)}) async-start(f32[16,1,8320]{2,1,0:T(1,128)} %scan.1), calls=%async_computation.2 | async-start | bytes 1064960 | tf_op jit(solution)/shard_map/all_to_all | solution.py:252
  78.6 2.8 %collective-permute-start = (f32[8,128,128]{2,1,0:T(8,128)S(1)}, f32[8,128,128]{2,1,0:T(8,128)S(1)}, u32[]{:S(2)}, u32[]{:S(2)}) collective-permute-start(f32[8,128,128]{2,1,0:T(8,128)S(1)} %all_to_all.25.source_ref), channel_id=1, source_target_pairs={{0,4},{4,0},{1,5},{5,1},{2,6},{6,2},{3,7},{7,3},{8,12},{12,8},{9,1... | collective-permute-start | bytes 1572872 | tf_op jit(solution)/shard_map/ppermute | solution.py:235
  81.3 1.5 %collective-permute-done.target_ref = f32[8,128,128]{2,1,0:T(8,128)S(1)} collective-permute-done((f32[8,128,128]{2,1,0:T(8,128)S(1)}, f32[8,128,128]{2,1,0:T(8,128)S(1)}, u32[]{:S(2)}, u32[]{:S(2)}) %collective-permute-start) | collective-permute-done | bytes 524320 | tf_op jit(solution)/shard_map/ppermute | solution.py:235
  82.9 3.7 %local.1 = (f32[4,128,256]{2,1,0:T(8,128)S(1)}, bf16[8,128,128]{2,1,0:T(8,128)(2,1)S(1)}) custom-call(bf16[8,128,128]{2,1,0:T(8,128)(2,1)S(1)} %get-tuple-element.11.tok_ref, bf16[8,128,128]{2,1,0:T(8,128)(2,1)S(1)} %get-tuple-element.12.src_ref, f32[8,128,128]{2,1,0:T(8,128)S(1)} %collective-permute-done.target_ref), custom_call_target="tpu_custom_call" | custom-call | flops 4294967296 | bytes 1048576 | tf_op jit(solution)/shard_map/local/pallas_call | solution.py:39
  86.5 22.3 %all-to-all-done.2 = f32[16,1,8320]{2,1,0:T(1,128)S(1)} async-done(((f32[16,1,8320]{2,1,0:T(1,128)}), f32[16,1,8320]{2,1,0:T(1,128)S(1)}, u32[]{:S(2)}, u32[]{:S(2)}) %all-to-all-start.2) | async-done | bytes 532512 | tf_op jit(solution)/shard_map/all_to_all | solution.py:252
  108.9 0.0 copy-start.1
  108.9 0.0 copy-start.2
  108.9 2.8 %grads.1 = f32[8,128,128]{2,1,0:T(8,128)S(1)} custom-call(f32[1040,128]{1,0:T(8,128)S(1)} %bitcast.2, bf16[8,128,128]{2,1,0:T(8,128)(2,1)S(1)} %get-tuple-element.13.out_ref, f32[4,128,256]{2,1,0:T(8,128)S(1)} %get-tuple-element.14.local_ref), custom_call_target="tpu_custom_call" | custom-call | flops 4294967296 | bytes 3145728 | tf_op jit(solution)/shard_map/grads/pallas_call | solution.py:39
  111.7 0.0 copy-start
  111.7 18.6 %all_to_all.27.grads_ref = f32[8,128,128]{2,1,0:T(8,128)S(1)} all-to-all(f32[8,128,128]{2,1,0:T(8,128)S(1)} %grads.1), channel_id=1, replica_groups=mesh['x'=4,'zg'=4,'zc'=4,'core'=2,'y'=4] {'zc','core'}, dimensions={0} | all-to-all | bytes 1048576 | tf_op jit(solution)/shard_map/all_to_all | solution.py:277
  130.3 0.0 copy-done.1
  130.3 0.0 copy-done.2
  130.3 0.0 copy-done
  130.4 0.6 project.1
  131.0 17.5 %all_to_all.28 = f32[4,128,512]{2,1,0:T(8,128)S(1)} all-to-all(f32[4,128,512]{2,1,0:T(8,128)S(1)} %project.1), channel_id=1, replica_groups=mesh['x'=4,'zg'=4,'zc'=4,'core'=2,'y'=4] {'y'}, dimensions={0} | all-to-all | bytes 2097152 | tf_op jit(solution)/shard_map/all_to_all | solution.py:287
  148.5 0.8 reduce_sum.9
Async XLA Ops:
  70.9 37.9 %all-to-all-start.2 = ((f32[16,1,8320]{2,1,0:T(1,128)}), f32[16,1,8320]{2,1,0:T(1,128)S(1)}, u32[]{:S(2)}, u32[]{:S(2)}) async-start(f32[16,1,8320]{2,1,0:T(1,128)} %scan.1), calls=%async_computation.2 | async-start | bytes 1064960 | tf_op jit(solution)/shard_map/all_to_all | solution.py:252
  78.6 4.3 %collective-permute-start = (f32[8,128,128]{2,1,0:T(8,128)S(1)}, f32[8,128,128]{2,1,0:T(8,128)S(1)}, u32[]{:S(2)}, u32[]{:S(2)}) collective-permute-start(f32[8,128,128]{2,1,0:T(8,128)S(1)} %all_to_all.25.source_ref), channel_id=1, source_target_pairs={{0,4},{4,0},{1,5},{5,1},{2,6},{6,2},{3,7},{7,3},{8,12},{12,8},{9,1... | collective-permute-start | bytes 1572872 | tf_op jit(solution)/shard_map/ppermute | solution.py:235
  108.9 21.5 %copy-start.1 = (bf16[256,2048]{1,0:T(8,128)(2,1)S(1)}, bf16[256,2048]{1,0:T(8,128)(2,1)}, u32[]{:S(2)}) copy-start(bf16[256,2048]{1,0:T(8,128)(2,1)} %wk_ref.1) | copy-start | bytes 3145732
  108.9 21.5 %copy-start.2 = (bf16[256,2048]{1,0:T(8,128)(2,1)S(1)}, bf16[256,2048]{1,0:T(8,128)(2,1)}, u32[]{:S(2)}) copy-start(bf16[256,2048]{1,0:T(8,128)(2,1)} %wv_ref.1) | copy-start | bytes 3145732
  111.7 18.7 %copy-start = (bf16[256,2048]{1,0:T(8,128)(2,1)S(1)}, bf16[256,2048]{1,0:T(8,128)(2,1)}, u32[]{:S(2)}) copy-start(bf16[256,2048]{1,0:T(8,128)(2,1)} %wq_ref.1) | copy-start | bytes 3145732
